TPU v7x, 32 devices: a whole 2x2x4 slice. The times are simulated.
32 devices in a mesh: rep: 4 (over z), fsdp: 8 (over y, x, core).
Axes of the slice: x: 2, y: 2, z: 4, core: 2. Of those that a mesh axis runs over, the one named last changes fastest.
Arguments:
- tokens: bfloat16 [7680, 2048], P(('rep', 'fsdp')), may hold values from -6 to 6
- cotangent: bfloat16 [7680, 2048], P(('rep', 'fsdp')), may hold values from -6 to 6
- counts: int32 [4, 8, 8], P('rep'), may hold values from 24 to 36, as said below
- deal_order: int32 [4, 8], P('rep'), may hold values from 0 to 7, as said below
- seq_lengths: int32 [4, 8], P('rep', 'fsdp'), may hold values from 192 to 288, as said below
- input_gain: bfloat16 [2048], P('fsdp'), may hold values from 0.5 to 1.5
- w_query: bfloat16 [2048, 2048], P('fsdp'), may hold values from -0.125 to 0.125
- key_projection: bfloat16 [2048, 1024], P('fsdp'), may hold values from -0.125 to 0.125
- value_projection: bfloat16 [2048, 1024], P('fsdp'), may hold values from -0.125 to 0.125
- query_gain: bfloat16 [128], P('fsdp'), may hold values from 0.5 to 1.5
- key_gain: bfloat16 [128], P('fsdp'), may hold values from 0.5 to 1.5
- w_out: bfloat16 [2048, 2048], P('fsdp'), may hold values from -1 to 1
- mlp_gain: bfloat16 [2048], P('fsdp'), may hold values from 0.5 to 1.5
- w_gate: bfloat16 [2048, 6144], P('fsdp'), may hold values from -0.125 to 0.125
- w_up: bfloat16 [2048, 6144], P('fsdp'), may hold values from -0.125 to 0.125
- w_down: bfloat16 [6144, 2048], P('fsdp'), may hold values from -0.078125 to 0.078125
Outputs:
- output: bfloat16 [7680, 2048], P(('rep', 'fsdp'))
- input_grad: bfloat16 [7680, 2048], P(('rep', 'fsdp'))
- input_gain_grad: float32 [2048], P('fsdp')
- w_query_grad: float32 [2048, 2048], P('fsdp')
- w_key_grad: float32 [2048, 1024], P('fsdp')
- w_value_grad: float32 [2048, 1024], P('fsdp')
- query_gain_grad: float32 [128], P('fsdp')
- key_gain_grad: float32 [128], P('fsdp')
- w_out_grad: float32 [2048, 2048], P('fsdp')
- mlp_gain_grad: float32 [2048], P('fsdp')
- w_gate_grad: float32 [2048, 6144], P('fsdp')
- w_up_grad: float32 [2048, 6144], P('fsdp')
- w_down_grad: float32 [6144, 2048], P('fsdp')
Inputs may be any that keep to these rules, and one draw needn't show every extreme that they name: Each device's counts over its runs sum to 240; every entry is 36 or 24; in each replica some run has 36 rows on every device. `deal_order`: each replica's row is a permutation of the devices. seq_lengths[r, deal_order[r, k]] equals the sum over f of counts[r, f, k], so no length is under 8 * 24; each replica has a sequence of 288 rows.
All inputs are finite; a program needn't handle non-finite values.
Results may differ from a plain program's by a relative error of at most 0.02.
Values may be sent and summed in bfloat16 or wider, within the bound.
A program may use at most 448 MiB of HBM per device.

v0:
```python
import jax
import jax.numpy as jnp
from jax import lax
from jax.sharding import PartitionSpec as P

QUERY_HEADS = 16
KEY_VALUE_HEADS = 8
HEAD_SIZE = 128
SLOT_LENGTH = 288


EPSILON = 1e-06
ROPE_BASE = 1000000.0
NEG_LARGE = -1e30


def rms_scale(values):
    return lax.rsqrt(jnp.mean(values * values, axis=-1, keepdims=True) + EPSILON)


def rope_tables(sequence_length, head_width):
    positions = jnp.arange(sequence_length, dtype=jnp.float32)
    inverse = ROPE_BASE ** (-jnp.arange(0, head_width, 2, dtype=jnp.float32) / head_width)
    angles = positions[:, None] * inverse[None, :]
    angles = jnp.concatenate([angles, angles], axis=-1)
    return (jnp.cos(angles)[:, None, :], jnp.sin(angles)[:, None, :])


def rotate_half(values):
    halfway = values.shape[-1] // 2
    return jnp.concatenate([-values[..., halfway:], values[..., :halfway]], axis=-1)


def rotate_back(values):
    halfway = values.shape[-1] // 2
    return jnp.concatenate([values[..., halfway:], -values[..., :halfway]], axis=-1)


def norm_back(grad_normed, unit_rows, scale_rows, gain_rows):
    scaled = grad_normed * gain_rows
    lead_axes = tuple(range(grad_normed.ndim - 1))
    grad_gain = jnp.sum(grad_normed * unit_rows, axis=lead_axes)
    grad_raw = scale_rows * (
        scaled - unit_rows * jnp.mean(scaled * unit_rows, axis=-1, keepdims=True)
    )
    return (grad_raw, grad_gain)


def pad_rows(values):
    return jnp.concatenate([values, jnp.zeros((1, values.shape[1]), values.dtype)], axis=0)


def on_device(
    tokens,
    cotangent,
    counts,
    deal_order,
    seq_lengths,
    input_gain,
    w_query,
    key_projection,
    value_projection,
    query_gain,
    key_gain,
    w_out,
    mlp_gain,
    w_gate,
    w_up,
    w_down,
):
    groups = lax.axis_size("fsdp")
    device = lax.axis_index("fsdp")
    in_rows, model_width = tokens.shape
    capacity = SLOT_LENGTH // groups
    rank_ids = jnp.arange(groups, dtype=jnp.int32)
    slot_ids = jnp.arange(capacity, dtype=jnp.int32)
    positions = jnp.arange(SLOT_LENGTH, dtype=jnp.int32)
    count_table = counts[0]
    run_owner = deal_order[0]
    seq_length = seq_lengths[0, 0]
    owner_hot = (run_owner[None, :] == rank_ids[:, None]).astype(jnp.int32)
    run_of_dev = jnp.sum(owner_hot * rank_ids[None, :], axis=1)
    my_counts = jnp.sum(count_table * (rank_ids == device).astype(jnp.int32)[:, None], axis=0)
    my_starts = jnp.cumsum(my_counts) - my_counts
    my_run = jnp.sum(rank_ids * (run_owner == device).astype(jnp.int32))
    column = jnp.sum(count_table * (rank_ids == my_run).astype(jnp.int32)[None, :], axis=1)
    column_start = jnp.cumsum(column) - column
    filled = jnp.minimum(jnp.sum(column), seq_length)
    run_hot = (run_of_dev[:, None] == rank_ids[None, :]).astype(jnp.int32)
    send_start = jnp.sum(run_hot * my_starts[None, :], axis=1)
    send_count = jnp.sum(run_hot * my_counts[None, :], axis=1)
    send_index = jnp.where(
        slot_ids[None, :] < send_count[:, None], send_start[:, None] + slot_ids[None, :], in_rows
    ).reshape(-1)
    sent_rows = jnp.take(pad_rows(tokens), send_index, axis=0).reshape(
        groups, capacity, model_width
    )
    sent_grads = jnp.take(pad_rows(cotangent), send_index, axis=0).reshape(
        groups, capacity, model_width
    )
    got_rows, got_grads = (
        lax.all_to_all(sent_rows, "fsdp", split_axis=0, concat_axis=0, tiled=True),
        lax.all_to_all(sent_grads, "fsdp", split_axis=0, concat_axis=0, tiled=True),
    )
    column_end = column_start + column
    source = jnp.minimum(
        jnp.sum((column_end[None, :] <= positions[:, None]).astype(jnp.int32), axis=1), groups - 1
    )
    source_hot = (source[:, None] == rank_ids[None, :]).astype(jnp.int32)
    offset_in = positions - jnp.sum(source_hot * column_start[None, :], axis=1)
    slot_index = jnp.where(positions < filled, source * capacity + offset_in, groups * capacity)
    slot_rows = jnp.take(
        pad_rows(got_rows.reshape(groups * capacity, model_width)), slot_index, axis=0
    )
    slot_grads = jnp.take(
        pad_rows(got_grads.reshape(groups * capacity, model_width)), slot_index, axis=0
    )
    full_query, gathered_keys, full_value, full_out, gain_one, gain_query, gain_key = (
        lax.all_gather(w_query, "fsdp", axis=0, tiled=True),
        lax.all_gather(key_projection, "fsdp", axis=0, tiled=True),
        lax.all_gather(value_projection, "fsdp", axis=0, tiled=True),
        lax.all_gather(w_out, "fsdp", axis=0, tiled=True),
        lax.all_gather(input_gain, "fsdp", axis=0, tiled=True),
        lax.all_gather(query_gain, "fsdp", axis=0, tiled=True),
        lax.all_gather(key_gain, "fsdp", axis=0, tiled=True),
    )
    gain_one = gain_one.astype(jnp.float32)
    gain_query = gain_query.astype(jnp.float32)
    gain_key = gain_key.astype(jnp.float32)
    group_factor = QUERY_HEADS // KEY_VALUE_HEADS
    softmax_scale = HEAD_SIZE ** (-0.5)
    resid = slot_rows.astype(jnp.float32)
    scale_one = rms_scale(resid)
    normed_one = resid * scale_one
    attention_input = (normed_one * gain_one).astype(jnp.bfloat16)
    query_raw = jnp.dot(attention_input, full_query, preferred_element_type=jnp.float32).reshape(
        SLOT_LENGTH, QUERY_HEADS, HEAD_SIZE
    )
    key_unrotated = jnp.dot(
        attention_input, gathered_keys, preferred_element_type=jnp.float32
    ).reshape(SLOT_LENGTH, KEY_VALUE_HEADS, HEAD_SIZE)
    value_reduced = (
        jnp.dot(attention_input, full_value, preferred_element_type=jnp.float32)
        .astype(jnp.bfloat16)
        .reshape(SLOT_LENGTH, KEY_VALUE_HEADS, HEAD_SIZE)
    )
    query_scale = rms_scale(query_raw)
    query_unit = query_raw * query_scale
    query_normed = query_unit * gain_query
    key_scale = rms_scale(key_unrotated)
    key_unit = key_unrotated * key_scale
    key_normed = key_unit * gain_key
    cosine_table, sine_table = rope_tables(SLOT_LENGTH, HEAD_SIZE)
    query_rotated = (query_normed * cosine_table + rotate_half(query_normed) * sine_table).astype(
        jnp.bfloat16
    )
    key_rot = (key_normed * cosine_table + rotate_half(key_normed) * sine_table).astype(
        jnp.bfloat16
    )
    query_grouped = query_rotated.reshape(SLOT_LENGTH, KEY_VALUE_HEADS, group_factor, HEAD_SIZE)
    visible = (positions[None, :] <= positions[:, None]) & (positions[None, :] < seq_length)

    def scores_of():
        raw_scores = (
            jnp.einsum("ikgd,jkd->kgij", query_grouped, key_rot, preferred_element_type=jnp.float32)
            * softmax_scale
        )
        return jnp.where(visible, raw_scores, NEG_LARGE)

    scores = scores_of()
    row_max = jnp.max(scores, axis=-1, keepdims=True)
    exp_scores = jnp.exp(scores - row_max)
    row_sum = jnp.sum(exp_scores, axis=-1, keepdims=True)
    log_total = row_max + jnp.log(row_sum)
    attention = (exp_scores / row_sum).astype(jnp.bfloat16)
    context = jnp.einsum(
        "kgij,jkd->ikgd", attention, value_reduced, preferred_element_type=jnp.float32
    )
    context_low = context.reshape(SLOT_LENGTH, QUERY_HEADS * HEAD_SIZE).astype(jnp.bfloat16)
    hidden_one = resid + jnp.dot(context_low, full_out, preferred_element_type=jnp.float32)
    full_gate, full_up, full_down, gain_two = (
        lax.all_gather(w_gate, "fsdp", axis=0, tiled=True),
        lax.all_gather(w_up, "fsdp", axis=0, tiled=True),
        lax.all_gather(w_down, "fsdp", axis=0, tiled=True),
        lax.all_gather(mlp_gain, "fsdp", axis=0, tiled=True),
    )
    gain_two = gain_two.astype(jnp.float32)
    scale_two = rms_scale(hidden_one)
    normed_two = hidden_one * scale_two
    mlp_in = (normed_two * gain_two).astype(jnp.bfloat16)
    gate_pre = jnp.dot(mlp_in, full_gate, preferred_element_type=jnp.float32)
    up_pre = jnp.dot(mlp_in, full_up, preferred_element_type=jnp.float32)
    activ = (jax.nn.silu(gate_pre) * up_pre).astype(jnp.bfloat16)
    result = (hidden_one + jnp.dot(activ, full_down, preferred_element_type=jnp.float32)).astype(
        jnp.bfloat16
    )
    back_gate, back_up, back_down = (
        lax.all_gather(w_gate, "fsdp", axis=0, tiled=True),
        lax.all_gather(w_up, "fsdp", axis=0, tiled=True),
        lax.all_gather(w_down, "fsdp", axis=0, tiled=True),
    )
    upstream = slot_grads.astype(jnp.float32)
    grad_activ = jnp.einsum("sd,fd->sf", slot_grads, back_down, preferred_element_type=jnp.float32)
    sigmoid_gate = jax.nn.sigmoid(gate_pre)
    grad_gate = (
        grad_activ * up_pre * sigmoid_gate * (1.0 + gate_pre * (1.0 - sigmoid_gate))
    ).astype(jnp.bfloat16)
    grad_up = (grad_activ * (gate_pre * sigmoid_gate)).astype(jnp.bfloat16)
    row_block = activ
    down_share = lax.psum_scatter(
        jnp.einsum("sf,sd->fd", row_block, slot_grads, preferred_element_type=jnp.float32).astype(
            jnp.bfloat16
        ),
        "fsdp",
        scatter_dimension=0,
        tiled=True,
    ).astype(jnp.float32)
    row_block = mlp_in
    gate_share = lax.psum_scatter(
        jnp.einsum("sd,sf->df", row_block, grad_gate, preferred_element_type=jnp.float32).astype(
            jnp.bfloat16
        ),
        "fsdp",
        scatter_dimension=0,
        tiled=True,
    ).astype(jnp.float32)
    row_block = mlp_in
    up_share = lax.psum_scatter(
        jnp.einsum("sd,sf->df", row_block, grad_up, preferred_element_type=jnp.float32).astype(
            jnp.bfloat16
        ),
        "fsdp",
        scatter_dimension=0,
        tiled=True,
    ).astype(jnp.float32)
    grad_mlp_in = jnp.einsum("sf,df->sd", grad_gate, back_gate, preferred_element_type=jnp.float32)
    grad_mlp_in = grad_mlp_in + jnp.einsum(
        "sf,df->sd", grad_up, back_up, preferred_element_type=jnp.float32
    )
    grad_norm_two, gain_two_grad = norm_back(grad_mlp_in, normed_two, scale_two, gain_two)
    grad_hidden = upstream + grad_norm_two
    back_query, back_key, back_value, back_out = (
        lax.all_gather(w_query, "fsdp", axis=0, tiled=True),
        lax.all_gather(key_projection, "fsdp", axis=0, tiled=True),
        lax.all_gather(value_projection, "fsdp", axis=0, tiled=True),
        lax.all_gather(w_out, "fsdp", axis=0, tiled=True),
    )
    grad_hidden_low = grad_hidden.astype(jnp.bfloat16)
    out_term = jnp.einsum(
        "se,sd->ed", context_low, grad_hidden_low, preferred_element_type=jnp.float32
    )
    context_gradient = jnp.einsum(
        "sd,ed->se", grad_hidden_low, back_out, preferred_element_type=jnp.float32
    )
    context_gradient = context_gradient.astype(jnp.bfloat16).reshape(
        SLOT_LENGTH, KEY_VALUE_HEADS, group_factor, HEAD_SIZE
    )
    probs_again = jnp.exp(scores_of() - log_total)
    grad_probs = jnp.einsum(
        "ikgd,jkd->kgij", context_gradient, value_reduced, preferred_element_type=jnp.float32
    )
    value_gradient = jnp.einsum(
        "kgij,ikgd->jkd",
        probs_again.astype(jnp.bfloat16),
        context_gradient,
        preferred_element_type=jnp.float32,
    )
    value_gradient = value_gradient.astype(jnp.bfloat16).reshape(
        SLOT_LENGTH, KEY_VALUE_HEADS * HEAD_SIZE
    )
    inner_sum = jnp.sum(grad_probs * probs_again, axis=-1, keepdims=True)
    grad_scores = (probs_again * (grad_probs - inner_sum)).astype(jnp.bfloat16)
    grad_query = (
        jnp.einsum("kgij,jkd->ikgd", grad_scores, key_rot, preferred_element_type=jnp.float32)
        * softmax_scale
    )
    grad_query = grad_query.reshape(SLOT_LENGTH, QUERY_HEADS, HEAD_SIZE)
    grad_key = (
        jnp.einsum("kgij,ikgd->jkd", grad_scores, query_grouped, preferred_element_type=jnp.float32)
        * softmax_scale
    )
    grad_query_normed = grad_query * cosine_table + rotate_back(grad_query * sine_table)
    grad_key_normed = grad_key * cosine_table + rotate_back(grad_key * sine_table)
    grad_query_raw, query_gain_term = norm_back(
        grad_query_normed, query_unit, query_scale, gain_query
    )
    key_gradient_unrotated, key_gain_term = norm_back(
        grad_key_normed, key_unit, key_scale, gain_key
    )
    grad_query_low = grad_query_raw.astype(jnp.bfloat16).reshape(
        SLOT_LENGTH, QUERY_HEADS * HEAD_SIZE
    )
    key_gradient_reduced = key_gradient_unrotated.astype(jnp.bfloat16).reshape(
        SLOT_LENGTH, KEY_VALUE_HEADS * HEAD_SIZE
    )
    query_term = jnp.einsum(
        "sd,se->de", attention_input, grad_query_low, preferred_element_type=jnp.float32
    )
    key_term = jnp.einsum(
        "sd,se->de", attention_input, key_gradient_reduced, preferred_element_type=jnp.float32
    )
    value_term = jnp.einsum(
        "sd,se->de", attention_input, value_gradient, preferred_element_type=jnp.float32
    )
    grad_attn_in = jnp.einsum(
        "se,de->sd", grad_query_low, back_query, preferred_element_type=jnp.float32
    )
    grad_attn_in = grad_attn_in + jnp.einsum(
        "se,de->sd", key_gradient_reduced, back_key, preferred_element_type=jnp.float32
    )
    grad_attn_in = grad_attn_in + jnp.einsum(
        "se,de->sd", value_gradient, back_value, preferred_element_type=jnp.float32
    )
    grad_norm_one, gain_one_grad = norm_back(grad_attn_in, normed_one, scale_one, gain_one)
    input_slot = (grad_hidden + grad_norm_one).astype(jnp.bfloat16)
    (
        query_share,
        key_share,
        value_share,
        out_share,
        gain_one_share,
        query_gain_share,
        key_gain_share,
        gain_two_share,
    ) = (
        lax.psum_scatter(
            query_term.astype(jnp.bfloat16), "fsdp", scatter_dimension=0, tiled=True
        ).astype(jnp.float32),
        lax.psum_scatter(
            key_term.astype(jnp.bfloat16), "fsdp", scatter_dimension=0, tiled=True
        ).astype(jnp.float32),
        lax.psum_scatter(
            value_term.astype(jnp.bfloat16), "fsdp", scatter_dimension=0, tiled=True
        ).astype(jnp.float32),
        lax.psum_scatter(
            out_term.astype(jnp.bfloat16), "fsdp", scatter_dimension=0, tiled=True
        ).astype(jnp.float32),
        lax.psum_scatter(
            gain_one_grad.astype(jnp.bfloat16), "fsdp", scatter_dimension=0, tiled=True
        ).astype(jnp.float32),
        lax.psum_scatter(
            query_gain_term.astype(jnp.bfloat16), "fsdp", scatter_dimension=0, tiled=True
        ).astype(jnp.float32),
        lax.psum_scatter(
            key_gain_term.astype(jnp.bfloat16), "fsdp", scatter_dimension=0, tiled=True
        ).astype(jnp.float32),
        lax.psum_scatter(
            gain_two_grad.astype(jnp.bfloat16), "fsdp", scatter_dimension=0, tiled=True
        ).astype(jnp.float32),
    )
    (
        query_share,
        key_share,
        value_share,
        out_share,
        gain_one_share,
        query_gain_share,
        key_gain_share,
        gain_two_share,
        gate_share,
        up_share,
        down_share,
    ) = lax.psum(
        (
            query_share,
            key_share,
            value_share,
            out_share,
            gain_one_share,
            query_gain_share,
            key_gain_share,
            gain_two_share,
            gate_share,
            up_share,
            down_share,
        ),
        "rep",
    )
    block_pos = column_start[:, None] + slot_ids[None, :]
    block_live = (slot_ids[None, :] < column[:, None]) & (block_pos < filled)
    block_index = jnp.where(block_live, block_pos, SLOT_LENGTH).reshape(-1)
    back_rows = jnp.take(pad_rows(result), block_index, axis=0).reshape(
        groups, capacity, model_width
    )
    back_grads = jnp.take(pad_rows(input_slot), block_index, axis=0).reshape(
        groups, capacity, model_width
    )
    home_rows, home_grads = (
        lax.all_to_all(back_rows, "fsdp", split_axis=0, concat_axis=0, tiled=True),
        lax.all_to_all(back_grads, "fsdp", split_axis=0, concat_axis=0, tiled=True),
    )
    input_ids = jnp.arange(in_rows, dtype=jnp.int32)
    my_ends = my_starts + my_counts
    run_index = jnp.minimum(
        jnp.sum((my_ends[None, :] <= input_ids[:, None]).astype(jnp.int32), axis=1), groups - 1
    )
    index_hot = (run_index[:, None] == rank_ids[None, :]).astype(jnp.int32)
    inside = input_ids - jnp.sum(index_hot * my_starts[None, :], axis=1)
    owner_dev = jnp.sum(index_hot * run_owner[None, :], axis=1)
    home_index = owner_dev * capacity + inside
    output = jnp.take(home_rows.reshape(groups * capacity, model_width), home_index, axis=0)
    input_grad = jnp.take(home_grads.reshape(groups * capacity, model_width), home_index, axis=0)
    return (
        output,
        input_grad,
        gain_one_share,
        query_share,
        key_share,
        value_share,
        query_gain_share,
        key_gain_share,
        out_share,
        gain_two_share,
        gate_share,
        up_share,
        down_share,
    )


def solution(mesh):
    placed = (
        P(("rep", "fsdp"), None),
        P(("rep", "fsdp"), None),
        P("rep", None, None),
        P("rep", None),
        P("rep", "fsdp"),
        P("fsdp"),
        P("fsdp", None),
        P("fsdp", None),
        P("fsdp", None),
        P("fsdp"),
        P("fsdp"),
        P("fsdp", None),
        P("fsdp"),
        P("fsdp", None),
        P("fsdp", None),
        P("fsdp", None),
    )
    return jax.shard_map(
        on_device,
        mesh=mesh,
        in_specs=placed,
        out_specs=(
            P(("rep", "fsdp"), None),
            P(("rep", "fsdp"), None),
            P("fsdp"),
            P("fsdp", None),
            P("fsdp", None),
            P("fsdp", None),
            P("fsdp"),
            P("fsdp"),
            P("fsdp", None),
            P("fsdp"),
            P("fsdp", None),
            P("fsdp", None),
            P("fsdp", None),
        ),
        check_vma=False,
    )
```

profile of v0, /device:TPU:0, one launch (start us, length us, event | category | flops | bytes accessed | tf_op | source)
XLA Modules:
  0.0 2270.3 jit_solution(16657169215130439250)
XLA Ops:
  24.6 5.3 all-to-all-start
  30.6 30.6 %all-gather = bf16[8,1,256]{2,1,0:T(2,128)(2,1)S(1)} all-gather(bf16[1,1,256]{2,1,0:T(2,128)(2,1)S(1)} %reshape.433), channel_id=1, replica_groups=mesh['rep'=4,'fsdp'=8] {'fsdp'}, dimensions={0}, use_global_device_ids=true | all-gather | bytes 4608 | tf_op jit(solution)/shard_map/all_gather | solution.py:123
  64.2 13.6 all-reduce.14
  77.8 8.1 all-gather.1
  86.0 4.3 all-to-all-start.2
  97.2 15.1 all-to-all-done.2
  119.4 4.0 fusion.74
  124.1 3.6 fusion.37
  131.0 34.9 %all-gather.14.cloned.1.call-done = bf16[2048,2048]{1,0:T(8,128)(2,1)} async-done(((bf16[256,2048]{1,0:T(8,128)(2,1)}), bf16[2048,2048]{1,0:T(8,128)(2,1)}) %all-gather.14.cloned.1.call-update) | async-done | bytes 8388624 | tf_op jit(solution)/shard_map/all_gather | solution.py:119
  165.9 7.4 fusion.72
  175.7 4.3 reshape.342
  202.9 19.0 all-gather.16.cloned.1.call-done
  221.9 5.6 multiply_reduce_fusion.5
  229.2 119.7 %all-gather.18.cloned.1.call-done = bf16[2048,6144]{1,0:T(8,128)(2,1)} async-done(((bf16[256,6144]{1,0:T(8,128)(2,1)}), bf16[2048,6144]{1,0:T(8,128)(2,1)}) %all-gather.18.cloned.1.call-update) | async-done | bytes 25165840 | tf_op jit(solution)/shard_map/all_gather | solution.py:182
  348.9 15.8 fusion.81
  364.7 111.1 %all-gather.20.cloned.1.call-done = bf16[2048,6144]{1,0:T(8,128)(2,1)} async-done(((bf16[256,6144]{1,0:T(8,128)(2,1)}), bf16[2048,6144]{1,0:T(8,128)(2,1)}) %all-gather.20.cloned.1.call-update) | async-done | bytes 25165840 | tf_op jit(solution)/shard_map/all_gather | solution.py:183
  475.8 14.8 fusion.82
  490.6 112.3 %all-gather.22.cloned.1.call-done = bf16[6144,2048]{1,0:T(8,128)(2,1)} async-done(((bf16[768,2048]{1,0:T(8,128)(2,1)}), bf16[6144,2048]{1,0:T(8,128)(2,1)}) %all-gather.22.cloned.1.call-update) | async-done | bytes 25165840 | tf_op jit(solution)/shard_map/all_gather | solution.py:184
  602.9 21.0 multiply_convert_fusion
  623.9 14.3 fusion.83
  638.2 16.8 multiply_reduce_fusion.1
  659.5 7.1 convolution_convert_fusion.7
  666.6 3.5 reshape.348
  670.1 4.5 fusion.38
  675.4 4.6 convolution_convert_fusion.5
  680.1 4.7 fusion
  684.9 5.1 fusion.2
  696.2 4.6 convolution_convert_fusion.6
  704.1 3.6 copy.144
  710.1 3.3 copy.138
  721.8 4.8 reshape.349
  731.7 4.0 fusion.25
  736.7 7.1 convolution_convert_fusion.4
  745.7 8.2 convolution_convert_fusion.3
  754.0 20.2 convolution_convert_fusion.2
  774.2 20.0 convolution_convert_fusion.1
  794.9 21.0 convolution_convert_fusion
  820.6 6.1 fusion.84
  835.6 13.8 fusion.14
  855.3 3.6 all-to-all-start.1
  861.5 15.5 all-to-all-done.1
  877.0 4.3 all-to-all-start.3
  881.5 32.8 %all-reduce.13 = (bf16[2048]{0:T(1024)(128)(2,1)S(1)}, bf16[128]{0:T(256)(128)(2,1)S(1)}, bf16[128]{0:T(256)(128)(2,1)S(1)}, bf16[2048]{0:T(1024)(128)(2,1)S(1)}) all-reduce(bf16[2048]{0:T(1024)(128)(2,1)S(1)} %copy-done.59, bf16[128]{0:T(256)(128)(2,1)S(1)} %copy-done.62, ...), channel_id=2, replica_groups=mesh['rep'=4,'fsdp'=8] {'fsdp'}, use_global_device_ids=true, to_apply=%region_26.30.clone | all-reduce | flops 4352 | bytes 17408
  920.7 23.0 %reduce-scatter.14.cloned.1.call-done = bf16[256,2048]{1,0:T(8,128)(2,1)} async-done(((bf16[2048,2048]{1,0:T(8,128)(2,1)}), bf16[256,2048]{1,0:T(8,128)(2,1)}) %reduce-scatter.14.cloned.1.call-update) | async-done | bytes 1048592 | tf_op jit(solution)/shard_map/reduce_scatter | solution.py:335
  943.7 159.8 %reduce-scatter.16.cloned.1.call-done = bf16[256,6144]{1,0:T(8,128)(2,1)} async-done(((bf16[2048,6144]{1,0:T(8,128)(2,1)}), bf16[256,6144]{1,0:T(8,128)(2,1)}) %reduce-scatter.16.cloned.1.call-update) | async-done | bytes 3145744 | tf_op jit(solution)/shard_map/reduce_scatter | solution.py:219
  1103.5 160.0 %reduce-scatter.18.cloned.1.call-done = bf16[256,6144]{1,0:T(8,128)(2,1)} async-done(((bf16[2048,6144]{1,0:T(8,128)(2,1)}), bf16[256,6144]{1,0:T(8,128)(2,1)}) %reduce-scatter.18.cloned.1.call-update) | async-done | bytes 3145744 | tf_op jit(solution)/shard_map/reduce_scatter | solution.py:228
  1263.5 159.8 %reduce-scatter.20.cloned.1.call-done = bf16[768,2048]{1,0:T(8,128)(2,1)} async-done(((bf16[6144,2048]{1,0:T(8,128)(2,1)}), bf16[768,2048]{1,0:T(8,128)(2,1)}) %reduce-scatter.20.cloned.1.call-update) | async-done | bytes 3145744 | tf_op jit(solution)/shard_map/reduce_scatter | solution.py:210
  1423.3 840.0 %all-reduce.16 = (f32[256]{0:T(256)}, f32[256,2048]{1,0:T(8,128)}, f32[256,1024]{1,0:T(8,128)}, f32[256,1024]{1,0:T(8,128)}, f32[16]{0:T(128)}, /*index=5*/f32[1...) all-reduce(f32[256]{0:T(256)S(1)} %dynamic-slice_convert_fusion.3, ...), channel_id=1, replica_groups=mesh['rep'=4,'fsdp'=8] {'rep'}, use_global_device_ids=true, to_apply=%region_27.31 | all-reduce | flops 6292000 | bytes 37753088 | tf_op jit(solution)/shard_map/psum | solution.py:363
  (314 shorter events, 125.0 us)
Async XLA Ops:
  7.2 112.2 %all-gather.12.cloned.1.call-start = ((), (), s32[]{:S(2)}) async-start(), calls=%async_computation.12 | async-start | bytes 4718592 | tf_op jit(solution)/shard_map/all_gather | solution.py:120
  7.9 116.2 %all-gather.10.cloned.1.call-start = ((), (), s32[]{:S(2)}) async-start(), calls=%async_computation.11 | async-start | bytes 4718592 | tf_op jit(solution)/shard_map/all_gather | solution.py:121
  8.7 157.2 %all-gather.14.cloned.1.call-start = ((), (), s32[]{:S(2)}) async-start(), calls=%async_computation.13 | async-start | bytes 9437184 | tf_op jit(solution)/shard_map/all_gather | solution.py:119
  9.4 212.5 %all-gather.16.cloned.1.call-start = ((), (), s32[]{:S(2)}) async-start(), calls=%async_computation.14 | async-start | bytes 9437184 | tf_op jit(solution)/shard_map/all_gather | solution.py:122
  10.0 338.9 %all-gather.18.cloned.1.call-start = ((), (), s32[]{:S(2)}) async-start(), calls=%async_computation.15 | async-start | bytes 28311552 | tf_op jit(solution)/shard_map/all_gather | solution.py:182
  10.6 465.3 %all-gather.20.cloned.1.call-start = ((), (), s32[]{:S(2)}) async-start(), calls=%async_computation.16 | async-start | bytes 28311552 | tf_op jit(solution)/shard_map/all_gather | solution.py:183
  11.2 591.8 %all-gather.22.cloned.1.call-start = ((), (), s32[]{:S(2)}) async-start(), calls=%async_computation.17 | async-start | bytes 28311552 | tf_op jit(solution)/shard_map/all_gather | solution.py:184
  14.6 77.6 %copy-start.55 = (s32[8]{0:T(128)}, s32[8]{0:T(128)S(1)}, u32[]{:S(2)}) copy-start(s32[8]{0:T(128)S(1)} %get-tuple-element.90) | copy-start | bytes 100
  23.4 7.2 copy-start.72
  23.4 37.8 %copy-start.73 = (bf16[256]{0:T(256)(128)(2,1)S(1)}, bf16[256]{0:T(256)(128)(2,1)}, u32[]{:S(2)}) copy-start(bf16[256]{0:T(256)(128)(2,1)} %param.34) | copy-start | bytes 1540
  24.6 37.8 %copy-start.64 = (u32[32]{0:T(128)S(1)}, u32[32]{0:T(128)}, u32[]{:S(2)}) copy-start(u32[32]{0:T(128)} %constant.115) | copy-start | bytes 388
  24.6 39.1 %copy-start.74 = (bf16[16]{0:T(256)(128)(2,1)S(1)}, bf16[16]{0:T(256)(128)(2,1)}, u32[]{:S(2)}) copy-start(bf16[16]{0:T(256)(128)(2,1)} %param.32) | copy-start | bytes 100
  24.6 39.4 %copy-start.75 = (bf16[16]{0:T(256)(128)(2,1)S(1)}, bf16[16]{0:T(256)(128)(2,1)}, u32[]{:S(2)}) copy-start(bf16[16]{0:T(256)(128)(2,1)} %param.31) | copy-start | bytes 100
  24.6 61.5 %all-to-all-start = ((bf16[8,36,2048]{2,1,0:T(8,128)(2,1)}), bf16[8,36,2048]{2,1,0:T(8,128)(2,1)S(1)}, u32[]{:S(2)}, u32[]{:S(2)}) async-start(bf16[8,36,2048]{2,1,0:T(8,128)(2,1)} %reshape.336), calls=%async_computation | async-start | bytes 2621440 | tf_op jit(solution)/shard_map/all_to_all | solution.py:102
  61.2 104.7 %copy-start.41 = (f32[8,1,256]{2,1,0:T(1,128)}, f32[8,1,256]{2,1,0:T(1,128)S(1)}, u32[]{:S(2)}) copy-start(f32[8,1,256]{2,1,0:T(1,128)S(1)} %convert_element_type.231) | copy-start | bytes 24580
  86.0 26.3 %all-to-all-start.2 = ((bf16[8,36,2048]{2,1,0:T(8,128)(2,1)}), bf16[8,36,2048]{2,1,0:T(8,128)(2,1)}, u32[]{:S(2)}, u32[]{:S(2)}) async-start(bf16[8,36,2048]{2,1,0:T(8,128)(2,1)} %reshape.346), calls=%async_computation.2 | async-start | bytes 2621440 | tf_op jit(solution)/shard_map/all_to_all | solution.py:103
  90.3 830.4 %reduce-scatter.12.cloned.1.call-start = ((), (), s32[]{:S(2)}) async-start(), calls=%async_computation.20 | async-start | bytes 4718592 | tf_op jit(solution)/shard_map/reduce_scatter | solution.py:332
  90.9 38.6 %copy-start.53 = (f32[128]{0:T(128)}, f32[128]{0:T(128)S(1)}, u32[]{:S(2)}) copy-start(f32[128]{0:T(128)S(1)} %convert_element_type.184) | copy-start | bytes 1540
  92.3 562.7 %copy-start.43 = (pred[288]{0:T(512)(128)(4,1)}, pred[288]{0:T(512)(128)(4,1)S(1)}, u32[]{:S(2)}) copy-start(pred[288]{0:T(512)(128)(4,1)S(1)} %get-tuple-element.53) | copy-start | bytes 868
  93.7 96.4 %copy-start.21 = (f32[288,128]{1,0:T(8,128)}, f32[288,128]{1,0:T(8,128)S(1)}, u32[]{:S(2)}) copy-start(f32[288,128]{1,0:T(8,128)S(1)} %get-tuple-element.69) | copy-start | bytes 442372
  93.7 96.4 %copy-start.23 = (f32[288,128]{1,0:T(8,128)}, f32[288,128]{1,0:T(8,128)S(1)}, u32[]{:S(2)}) copy-start(f32[288,128]{1,0:T(8,128)S(1)} %get-tuple-element.68) | copy-start | bytes 442372
  97.2 68.7 %copy-start.9 = (bf16[288,2048]{1,0:T(8,128)(2,1)}, bf16[288,2048]{1,0:T(8,128)(2,1)S(1)}, u32[]{:S(2)}) copy-start(bf16[288,2048]{1,0:T(8,128)(2,1)S(1)} %gather_fusion.1) | copy-start | bytes 3538948
  119.4 46.5 %copy-start.49 = (f32[288]{0:T(512)}, f32[288]{0:T(512)S(1)}, u32[]{:S(2)}) copy-start(f32[288]{0:T(512)S(1)} %add_rsqrt_fusion.3) | copy-start | bytes 3460
  123.4 6.1 copy-start.1
  200.2 21.7 copy-start.10
  202.9 26.0 %copy-start.40 = (f32[8,1,256]{2,1,0:T(1,128)S(1)}, f32[8,1,256]{2,1,0:T(1,128)}, u32[]{:S(2)}) copy-start(f32[8,1,256]{2,1,0:T(1,128)} %convert_element_type.232) | copy-start | bytes 24580
  227.5 452.6 %copy-start.35 = (f32[2,8,288]{2,1,0:T(8,128)}, f32[2,8,288]{2,1,0:T(8,128)S(1)}, u32[]{:S(2)}) copy-start(f32[2,8,288]{2,1,0:T(8,128)S(1)} %log_add_fusion) | copy-start | bytes 55300
  229.1 119.7 %copy-start.28 = (bf16[288,2048]{1,0:T(8,128)(2,1)}, bf16[288,2048]{1,0:T(8,128)(2,1)S(1)}, u32[]{:S(2)}) copy-start(bf16[288,2048]{1,0:T(8,128)(2,1)S(1)} %multiply_convert_fusion.3) | copy-start | bytes 3538948
  364.7 238.2 %copy-start.19 = (bf16[288,2048]{1,0:T(8,128)(2,1)S(1)}, bf16[288,2048]{1,0:T(8,128)(2,1)}, u32[]{:S(2)}) copy-start(bf16[288,2048]{1,0:T(8,128)(2,1)} %gather_fusion.5) | copy-start | bytes 3538948
  670.1 5.3 copy-start.42
  670.1 5.3 copy-start.44
  680.1 240.6 %reduce-scatter.10.cloned.1.call-start = ((), (), s32[]{:S(2)}) async-start(), calls=%async_computation.19 | async-start | bytes 4718592 | tf_op jit(solution)/shard_map/reduce_scatter | solution.py:329
  700.8 219.9 %reduce-scatter.8.cloned.1.call-start = ((), (), s32[]{:S(2)}) async-start(), calls=%async_computation.18 | async-start | bytes 9437184 | tf_op jit(solution)/shard_map/reduce_scatter | solution.py:326
  743.8 199.9 %reduce-scatter.14.cloned.1.call-start = ((), (), s32[]{:S(2)}) async-start(), calls=%async_computation.21 | async-start | bytes 9437184 | tf_op jit(solution)/shard_map/reduce_scatter | solution.py:335
  754.0 349.6 %reduce-scatter.16.cloned.1.call-start = ((), (), s32[]{:S(2)}) async-start(), calls=%async_computation.22 | async-start | bytes 28311552 | tf_op jit(solution)/shard_map/reduce_scatter | solution.py:219
  774.2 489.3 %reduce-scatter.18.cloned.1.call-start = ((), (), s32[]{:S(2)}) async-start(), calls=%async_computation.23 | async-start | bytes 28311552 | tf_op jit(solution)/shard_map/reduce_scatter | solution.py:228
  794.3 629.1 %reduce-scatter.20.cloned.1.call-start = ((), (), s32[]{:S(2)}) async-start(), calls=%async_computation.24 | async-start | bytes 28311552 | tf_op jit(solution)/shard_map/reduce_scatter | solution.py:210
  820.6 6.1 copy-start.34
  820.6 6.1 copy-start.70
  854.1 6.1 copy-start.67
  855.3 21.7 all-to-all-start.1
  860.3 21.0 copy-start.57
  860.3 21.0 copy-start.69
  860.3 21.2 copy-start.58
  860.3 21.2 copy-start.59
  860.3 21.2 copy-start.61
  860.3 21.2 copy-start.62
  877.0 39.4 %all-to-all-start.3 = ((bf16[8,36,2048]{2,1,0:T(8,128)(2,1)}), bf16[8,36,2048]{2,1,0:T(8,128)(2,1)}, u32[]{:S(2)}, u32[]{:S(2)}) async-start(bf16[8,36,2048]{2,1,0:T(8,128)(2,1)} %reshape.353), calls=%async_computation.3 | async-start | bytes 2621440 | tf_op jit(solution)/shard_map/all_to_all | solution.py:390
  (46 other events, 103.0 us)
Sparse Core Ops, SparseCore 0:
  9.9 49.9 all-gather.11
  61.8 41.0 all-gather.9
  104.7 61.0 all-gather.13
  167.6 54.2 all-gather.15
  223.6 125.1 all-gather.17
  350.6 125.1 all-gather.19
  477.7 125.1 all-gather.21
  680.2 51.1 reduce-scatter.11
  735.3 51.1 reduce-scatter.9
  789.8 71.5 reduce-scatter.7
  864.8 78.7 reduce-scatter.13
  947.2 156.3 reduce-scatter.15
  1107.1 156.3 reduce-scatter.17
  1267.0 156.3 reduce-scatter.19
where the time goes:
time: 2280 us; the launch traced here: 2270 us
  waiting for transfers between devices  935 us (41%)
  blocking collectives  925 us (41%)
  matrix products  237 us (10%)
  local copies, waits for them, and re-layouts  87.9 us (4%)
  other arithmetic  48.9 us (2%)
    psum x1, blocking collectives, on_device(): lax.psum((query_share, key_share, value_share, out_share, gain_one_share,...  840 us
    reduce_scatter x1, waiting for transfers between devices, on_device(): lax.psum_scatter(jnp.einsum('sd,sf->df', row_block, grad_up, preferred_el...  160 us
    reduce_scatter x1, waiting for transfers between devices, on_device(): lax.psum_scatter(jnp.einsum('sf,sd->fd', row_block, slot_grads, preferred...  160 us
    reduce_scatter x1, waiting for transfers between devices, on_device(): lax.psum_scatter(jnp.einsum('sd,sf->df', row_block, grad_gate, preferred_...  160 us
    all_gather x1, waiting for transfers between devices, on_device(): lax.all_gather(w_gate, 'fsdp', axis=0, tiled=True)  120 us
    all_gather x1, waiting for transfers between devices, on_device(): lax.all_gather(w_down, 'fsdp', axis=0, tiled=True)  112 us
    all_gather x1, waiting for transfers between devices, on_device(): lax.all_gather(w_up, 'fsdp', axis=0, tiled=True)  111 us
    unnamed x2, blocking collectives  46.4 us
  transfers between devices with their start and end apart: 18, of which 11 were waited for; matrix products, arithmetic and copies ran while one was open for 12% of the time, Pallas kernels for 0%

commit v1 on v0

v1 whole, which is shorter than its diff:
```python
import jax
import jax.numpy as jnp
from jax import lax
from jax.sharding import PartitionSpec as P

QUERY_HEADS = 16
KEY_VALUE_HEADS = 8
HEAD_SIZE = 128
SLOT_LENGTH = 288

EPSILON = 1e-06
ROPE_BASE = 1000000.0
NEG_LARGE = -1e30

F32 = jnp.float32
BF16 = jnp.bfloat16


def rms_scale(values):
    return lax.rsqrt(jnp.mean(values * values, axis=-1, keepdims=True) + EPSILON)


def dot(left, right):
    return jnp.dot(left, right, preferred_element_type=F32)


def dot_bt(left, right):
    return lax.dot_general(left, right, (((1,), (1,)), ((), ())), preferred_element_type=F32)


def dot_at(left, right):
    return lax.dot_general(left, right, (((0,), (0,)), ((), ())), preferred_element_type=F32)


def rotate_half(values):
    halfway = values.shape[-1] // 2
    return jnp.concatenate([-values[..., halfway:], values[..., :halfway]], axis=-1)


def rotate_back(values):
    halfway = values.shape[-1] // 2
    return jnp.concatenate([values[..., halfway:], -values[..., :halfway]], axis=-1)


def norm_back(grad_normed, unit_rows, scale_rows, gain_rows):
    scaled = grad_normed * gain_rows
    lead_axes = tuple(range(grad_normed.ndim - 1))
    grad_gain = jnp.sum(grad_normed * unit_rows, axis=lead_axes)
    grad_raw = scale_rows * (
        scaled - unit_rows * jnp.mean(scaled * unit_rows, axis=-1, keepdims=True)
    )
    return (grad_raw, grad_gain)


def pad_rows(values):
    return jnp.concatenate([values, jnp.zeros((1, values.shape[1]), values.dtype)], axis=0)


def on_device(
    tokens,
    cotangent,
    counts,
    deal_order,
    seq_lengths,
    input_gain,
    w_query,
    key_projection,
    value_projection,
    query_gain,
    key_gain,
    w_out,
    mlp_gain,
    w_gate,
    w_up,
    w_down,
):
    groups = lax.axis_size("fsdp")
    replicas = lax.axis_size("rep")
    device = lax.axis_index("fsdp")
    in_rows, width = tokens.shape
    cap = SLOT_LENGTH // groups
    shard = width // groups
    heads = QUERY_HEADS // groups
    kv_heads = max(1, KEY_VALUE_HEADS // groups)
    spread = max(1, groups // KEY_VALUE_HEADS)
    per_kv = heads // kv_heads
    q_cols, kv_cols = heads * HEAD_SIZE, kv_heads * HEAD_SIZE
    ff_cols = w_gate.shape[1] // groups

    def gather(values):
        return lax.all_gather(values, "fsdp", axis=0, tiled=True)

    def scatter_sum(values):
        return lax.psum_scatter(
            values.astype(BF16), "fsdp", scatter_dimension=0, tiled=True
        ).astype(F32)

    all_tokens = gather(tokens)
    gains = gather(jnp.concatenate([input_gain, mlp_gain, query_gain, key_gain])[None]).astype(F32)
    head_part = HEAD_SIZE // groups
    gain_one = gains[:, :shard].reshape(width)
    gain_two = gains[:, shard : 2 * shard].reshape(width)
    gain_query = gains[:, 2 * shard : 2 * shard + head_part].reshape(HEAD_SIZE)
    gain_key = gains[:, 2 * shard + head_part :].reshape(HEAD_SIZE)

    def kv_columns(weight):
        return jnp.repeat(
            weight.reshape(shard, KEY_VALUE_HEADS // kv_heads, kv_cols), spread, axis=1
        )

    send_attn = jnp.concatenate(
        [
            w_query.reshape(shard, groups, q_cols),
            kv_columns(key_projection),
            kv_columns(value_projection),
        ],
        axis=2,
    )
    w_qkv = lax.all_to_all(send_attn, "fsdp", split_axis=1, concat_axis=0, tiled=True).reshape(
        width, q_cols + 2 * kv_cols
    )
    send_ff = jnp.concatenate(
        [w_gate.reshape(shard, groups, ff_cols), w_up.reshape(shard, groups, ff_cols)], axis=2
    )
    w_ff = lax.all_to_all(send_ff, "fsdp", split_axis=1, concat_axis=0, tiled=True).reshape(
        width, 2 * ff_cols
    )
    all_grads = gather(cotangent)

    table = counts[0]
    run_start = jnp.cumsum(table, axis=1) - table
    seq_start = jnp.cumsum(table, axis=0) - table
    ids = jnp.arange(groups, dtype=jnp.int32)
    inner = jnp.arange(cap, dtype=jnp.int32)
    live = inner[None, None, :] < table.T[:, :, None]
    packed = ids[None, :, None] * in_rows + run_start.T[:, :, None] + inner[None, None, :]
    slot_index = jnp.where(live, packed, groups * in_rows).reshape(-1)
    place = (seq_start.T[:, :, None] + inner[None, None, :]).reshape(groups, SLOT_LENGTH)
    live = live.reshape(groups, SLOT_LENGTH)
    row_ids = jnp.arange(in_rows, dtype=jnp.int32)
    run_of = jnp.minimum(
        jnp.sum(((run_start + table)[:, None, :] <= row_ids[None, :, None]).astype(jnp.int32), 2),
        groups - 1,
    )
    run_hot = (run_of[:, :, None] == ids[None, None, :]).astype(jnp.int32)
    inside = row_ids[None, :] - jnp.sum(run_hot * run_start[:, None, :], axis=2)
    home_index = (run_of * SLOT_LENGTH + ids[:, None] * cap + inside).reshape(-1)

    def to_slots(values):
        return jnp.take(pad_rows(values), slot_index, axis=0)

    def to_packed(values):
        return jnp.take(values, home_index, axis=0)

    resid = tokens.astype(F32)
    scale_one = rms_scale(resid)
    normed_one = resid * scale_one
    all_resid = all_tokens.astype(F32)
    attention_input = (all_resid * rms_scale(all_resid) * gain_one).astype(BF16)
    raw = to_slots(dot(attention_input, w_qkv))
    query_raw = raw[:, :q_cols].reshape(groups, SLOT_LENGTH, heads, HEAD_SIZE)
    key_raw = raw[:, q_cols : q_cols + kv_cols].reshape(groups, SLOT_LENGTH, kv_heads, HEAD_SIZE)
    value = raw[:, q_cols + kv_cols :].astype(BF16).reshape(
        groups, SLOT_LENGTH, kv_heads, HEAD_SIZE
    )
    query_scale = rms_scale(query_raw)
    query_unit = query_raw * query_scale
    key_scale = rms_scale(key_raw)
    key_unit = key_raw * key_scale
    inverse = ROPE_BASE ** (-jnp.arange(0, HEAD_SIZE, 2, dtype=F32) / HEAD_SIZE)
    angles = place.astype(F32)[:, :, None] * inverse
    cosine = jnp.cos(angles)
    sine = jnp.sin(angles)
    cosine = jnp.concatenate([cosine, cosine], axis=-1)[:, :, None, :]
    sine = jnp.concatenate([sine, sine], axis=-1)[:, :, None, :]
    query_normed = query_unit * gain_query
    key_normed = key_unit * gain_key
    query = (query_normed * cosine + rotate_half(query_normed) * sine).astype(BF16)
    key = (key_normed * cosine + rotate_half(key_normed) * sine).astype(BF16)
    query = query.reshape(groups, SLOT_LENGTH, kv_heads, per_kv, HEAD_SIZE)
    visible = (place[:, None, :] <= place[:, :, None]) & live[:, None, :]
    visible = visible[:, None, None]
    softmax_scale = HEAD_SIZE ** (-0.5)
    scores = jnp.where(
        visible,
        jnp.einsum("sikgd,sjkd->skgij", query, key, preferred_element_type=F32) * softmax_scale,
        NEG_LARGE,
    )
    row_max = jnp.max(scores, axis=-1, keepdims=True)
    exp_scores = jnp.exp(scores - row_max)
    row_sum = jnp.sum(exp_scores, axis=-1, keepdims=True)
    probs = exp_scores / row_sum
    probs_low = probs.astype(BF16)
    context = jnp.einsum("skgij,sjkd->sikgd", probs_low, value, preferred_element_type=F32)
    context = to_packed(context.astype(BF16).reshape(groups * SLOT_LENGTH, q_cols))
    hidden_one = resid + scatter_sum(dot(context, w_out))

    scale_two = rms_scale(hidden_one)
    normed_two = hidden_one * scale_two
    mlp_in = gather((normed_two * gain_two).astype(BF16))
    gate_pre = dot(mlp_in, w_ff[:, :ff_cols])
    up_pre = dot(mlp_in, w_ff[:, ff_cols:])
    sigmoid_gate = jax.nn.sigmoid(gate_pre)
    activ = (gate_pre * sigmoid_gate * up_pre).astype(BF16)
    output = (hidden_one + scatter_sum(dot(activ, w_down))).astype(BF16)

    grad_activ = dot_bt(all_grads, w_down)
    grad_gate = (
        grad_activ * up_pre * sigmoid_gate * (1.0 + gate_pre * (1.0 - sigmoid_gate))
    ).astype(BF16)
    grad_up = (grad_activ * (gate_pre * sigmoid_gate)).astype(BF16)
    grad_ff = jnp.concatenate([grad_gate, grad_up], axis=1)
    down_term = dot_at(activ, all_grads).astype(BF16)
    ff_term = dot_at(mlp_in, grad_ff).astype(BF16)
    grad_mlp_in = scatter_sum(dot_bt(grad_ff, w_ff))
    grad_norm_two, gain_two_grad = norm_back(grad_mlp_in, normed_two, scale_two, gain_two)
    grad_hidden = cotangent.astype(F32) + grad_norm_two

    all_hidden = gather(grad_hidden.astype(BF16))
    out_term = dot_at(context, all_hidden).astype(BF16)
    grad_context = to_slots(dot_bt(all_hidden, w_out).astype(BF16)).reshape(
        groups, SLOT_LENGTH, kv_heads, per_kv, HEAD_SIZE
    )
    grad_probs = jnp.einsum("sikgd,sjkd->skgij", grad_context, value, preferred_element_type=F32)
    grad_value = jnp.einsum(
        "skgij,sikgd->sjkd", probs_low, grad_context, preferred_element_type=F32
    ).astype(BF16)
    inner_sum = jnp.sum(grad_probs * probs, axis=-1, keepdims=True)
    grad_scores = (probs * (grad_probs - inner_sum)).astype(BF16)
    grad_query = (
        jnp.einsum("skgij,sjkd->sikgd", grad_scores, key, preferred_element_type=F32)
        * softmax_scale
    ).reshape(groups, SLOT_LENGTH, heads, HEAD_SIZE)
    grad_key = (
        jnp.einsum("skgij,sikgd->sjkd", grad_scores, query, preferred_element_type=F32)
        * softmax_scale
    )
    grad_query_normed = grad_query * cosine + rotate_back(grad_query * sine)
    grad_key_normed = grad_key * cosine + rotate_back(grad_key * sine)
    grad_query_raw, query_gain_term = norm_back(
        grad_query_normed, query_unit, query_scale, gain_query
    )
    grad_key_raw, key_gain_term = norm_back(grad_key_normed, key_unit, key_scale, gain_key)
    rows = groups * SLOT_LENGTH
    grad_qkv = to_packed(
        jnp.concatenate(
            [
                grad_query_raw.astype(BF16).reshape(rows, q_cols),
                grad_key_raw.astype(BF16).reshape(rows, kv_cols),
                grad_value.reshape(rows, kv_cols),
            ],
            axis=1,
        )
    )
    qkv_term = dot_at(attention_input, grad_qkv).astype(BF16)
    grad_attn_in = scatter_sum(dot_bt(grad_qkv, w_qkv))
    grad_norm_one, gain_one_grad = norm_back(grad_attn_in, normed_one, scale_one, gain_one)
    input_grad = (grad_hidden + grad_norm_one).astype(BF16)

    def over_replicas(term):
        part = lax.psum_scatter(term, "rep", scatter_dimension=0, tiled=True)
        return lax.all_gather(part, "rep", axis=0, tiled=True).astype(F32)

    def columns_back(term):
        cols = term.shape[1]
        part = lax.psum_scatter(
            term.reshape(groups, shard, cols), "rep", scatter_dimension=1, tiled=True
        )
        part = lax.all_to_all(part, "fsdp", split_axis=0, concat_axis=0, tiled=True)
        full = lax.all_gather(part, "rep", axis=1, tiled=True)
        return jnp.swapaxes(full.astype(F32), 0, 1)

    down_share = over_replicas(down_term)
    ff_share = columns_back(ff_term)
    out_share = over_replicas(out_term)
    qkv_share = columns_back(qkv_term)

    def kv_share(part):
        part = part.reshape(shard, groups // spread, spread, kv_cols)
        return jnp.sum(part, axis=2).reshape(shard, KEY_VALUE_HEADS * HEAD_SIZE)

    gain_sums = lax.psum(
        jnp.concatenate([gain_one_grad, gain_two_grad, query_gain_term, key_gain_term]),
        ("rep", "fsdp"),
    )

    def own(start, length):
        return lax.dynamic_slice(gain_sums, (start + device * length,), (length,))

    return (
        output,
        input_grad,
        own(0, shard),
        qkv_share[:, :, :q_cols].reshape(shard, groups * q_cols),
        kv_share(qkv_share[:, :, q_cols : q_cols + kv_cols]),
        kv_share(qkv_share[:, :, q_cols + kv_cols :]),
        own(2 * width, head_part),
        own(2 * width + HEAD_SIZE, head_part),
        out_share,
        own(width, shard),
        ff_share[:, :, :ff_cols].reshape(shard, groups * ff_cols),
        ff_share[:, :, ff_cols:].reshape(shard, groups * ff_cols),
        down_share,
    )


def solution(mesh):
    rows = P(("rep", "fsdp"), None)
    vec = P("fsdp")
    mat = P("fsdp", None)
    return jax.shard_map(
        on_device,
        mesh=mesh,
        in_specs=(
            rows,
            rows,
            P("rep", None, None),
            P("rep", None),
            P("rep", "fsdp"),
            vec,
            mat,
            mat,
            mat,
            vec,
            vec,
            mat,
            vec,
            mat,
            mat,
            mat,
        ),
        out_specs=(rows, rows, vec, mat, mat, mat, vec, vec, mat, vec, mat, mat, mat),
        check_vma=False,
    )
```

time: 2280 us -> 1240 us (0.54)
  blocking collectives: 925 us -> 226 us
  waiting for transfers between devices: 935 us -> 590 us
  matrix products: 237 us -> 164 us
  local copies, waits for them, and re-layouts: 87.9 us -> 135 us
  other arithmetic: 48.9 us -> 95.9 us
    psum x1, blocking collectives: 840 us -> 40.3 us  [on_device(): lax.psum(jnp.concatenate([gain_one_grad, gain_two_grad, query_gain_term,...]
    all_gather x7 -> x8, waiting for transfers between devices: 397 us -> 223 us  [the longest x2 152 us: columns_back(): full = lax.all_gather(part, 'rep', axis=1, tiled=True)]
    reduce_scatter x7 -> x8, waiting for transfers between devices: 503 us -> 365 us  [the longest x4 234 us: scatter_sum(): lax.psum_scatter(values.astype(BF16), 'fsdp', scatter_dimension=0, tiled=...]
    all_to_all x0 -> x3, blocking collectives: none -> 135 us  [the longest x1 96 us: on_device(): lax.all_to_all(send_ff, 'fsdp', split_axis=1, concat_axis=0, tiled=True)]
    dot_general x27 -> x19, matrix products: 237 us -> 164 us  [the longest x5 53.5 us: dot(): return jnp.dot(left, right, preferred_element_type=F32)]
    all_gather x2 -> x0, blocking collectives: 38.7 us -> none  [the longest x1 30.6 us: on_device(): lax.all_gather(input_gain, 'fsdp', axis=0, tiled=True)]
    all_to_all x4 -> x1, waiting for transfers between devices: 30.6 us -> 0.01 us  [on_device(): lax.all_to_all(send_attn, 'fsdp', split_axis=1, concat_axis=0, tiled=True)]
    unnamed x2 -> x1, blocking collectives: 46.4 us -> 50.5 us
  transfers between devices with their start and end apart: 18 -> 17, of which waited for: 11 -> 12; matrix products, arithmetic and copies ran while one was open for 12% -> 20% of each run, Pallas kernels for 0% -> 0%
where the time goes in v1:
time: 1240 us; the launch traced here: 1230 us
  waiting for transfers between devices  590 us (48%)
  blocking collectives  226 us (18%)
  matrix products  164 us (13%)
  local copies, waits for them, and re-layouts  135 us (11%)
  other arithmetic  95.9 us (8%)
  between operations  16 us (1%)
    reduce_scatter x4, waiting for transfers between devices, scatter_sum(): lax.psum_scatter(values.astype(BF16), 'fsdp', scatter_dimension=0, tiled=...  234 us
    all_gather x2, waiting for transfers between devices, columns_back(): full = lax.all_gather(part, 'rep', axis=1, tiled=True)  152 us
    reduce_scatter x2, waiting for transfers between devices, columns_back(): lax.psum_scatter(term.reshape(groups, shard, cols), 'rep', scatter_dimens...  126 us
    all_to_all x1, blocking collectives, on_device(): lax.all_to_all(send_ff, 'fsdp', split_axis=1, concat_axis=0, tiled=True)  96 us
    dot_general x5, matrix products, dot(): return jnp.dot(left, right, preferred_element_type=F32)  53.5 us
    unnamed x1, blocking collectives  50.5 us
    dot_general x4, matrix products, dot_bt(): lax.dot_general(left, right, (((1,), (1,)), ((), ())), preferred_element_...  44.5 us
    dot_general x4, matrix products, dot_at(): lax.dot_general(left, right, (((0,), (0,)), ((), ())), preferred_element_...  44.1 us
  transfers between devices with their start and end apart: 17, of which 12 were waited for; matrix products, arithmetic and copies ran while one was open for 20% of the time, Pallas kernels for 0%

profile of v1, /device:TPU:0, one launch (start us, length us, event | category | flops | bytes accessed | tf_op | source)
XLA Modules:
  0.0 1233.5 jit_solution(1976919909505578063)
XLA Ops:
  17.5 5.3 all-to-all-start
  24.7 50.5 %all-reduce.2 = bf16[4352]{0:T(1024)(128)(2,1)S(1)} all-reduce(bf16[4352]{0:T(1024)(128)(2,1)S(1)} %dynamic-update-slice), channel_id=2, replica_groups=mesh['rep'=4,'fsdp'=8] {'fsdp'}, use_global_device_ids=true, to_apply=%add.2 | all-reduce | flops 4352 | bytes 17408
  78.0 6.2 multiply_cosine_fusion
  90.2 5.0 fusion
  95.6 6.1 fusion.33
  104.1 10.0 gather_fusion
  129.2 5.3 multiply_reduce_fusion.2
  154.2 7.2 gather_fusion.1
  161.4 6.9 convolution_convert_fusion.3
  169.1 69.0 %reduce-scatter.9.cloned.1.call-done = bf16[240,2048]{1,0:T(8,128)(2,1)} async-done(((bf16[1920,2048]{1,0:T(8,128)(2,1)}), bf16[240,2048]{1,0:T(8,128)(2,1)}) %reduce-scatter.9.cloned.1.call-update) | async-done | bytes 983056 | tf_op jit(solution)/shard_map/reduce_scatter | solution.py:94
  241.7 4.6 copy.174
  246.3 4.9 copy.173
  254.4 96.0 %all_to_all.40 = bf16[256,8,1536]{0,2,1:T(8,128)(2,1)} all-to-all(bf16[256,8,1536]{0,2,1:T(8,128)(2,1)S(1)} %pad_maximum_fusion), channel_id=1, replica_groups=mesh['rep'=4,'fsdp'=8] {'fsdp'}, dimensions={1} | all-to-all | bytes 12582912 | tf_op jit(solution)/shard_map/all_to_all | solution.py:125
  350.5 8.6 copy.175
  359.1 10.6 fusion.88
  369.7 22.0 %all-gather.12.cloned.1.call-done = bf16[1920,2048]{1,0:T(8,128)(2,1)} async-done(((bf16[240,2048]{1,0:T(8,128)(2,1)}), bf16[1920,2048]{1,0:T(8,128)(2,1)}) %all-gather.12.cloned.1.call-update) | async-done | bytes 7864336 | tf_op jit(solution)/shard_map/all_gather | solution.py:91
  391.7 12.3 fusion.15
  404.0 17.9 %multiply_convert_fusion.1 = (bf16[1920,768]{0,1:T(8,128)(2,1)}, bf16[1920,768]{0,1:T(8,128)(2,1)}, bf16[1920,768]{0,1:T(8,128)(2,1)}) fusion(f32[1920,768]{0,1:T(8,128)} %fusion.88, f32[1920,768]{0,1:T(8,128)} %fusion.15, bf16[1920,2048]{1,0:T(8,128)(2,1)} %all-gather.12.cloned.1.call-done, bf16[2048,1536]{1,0:T(8,128)(2,1)} %bitcast.256), kind=kOutput, calls=%fused_computation.29 | convolution fusion | flops 6061916160 | bytes 31653888 | tf_op jit(solution)/shard_map/dot_general | solution.py:24
  421.9 18.6 %convolution_convert_fusion.2 = bf16[1920,2048]{1,0:T(8,128)(2,1)} fusion(bf16[2048,1536]{1,0:T(8,128)(2,1)} %bitcast.257, bf16[1920,768]{0,1:T(8,128)(2,1)} %get-tuple-element.31, bf16[1920,768]{0,1:T(8,128)(2,1)} %get-tuple-element.30), kind=kOutput, calls=%fused_computation.12 | convolution fusion | flops 12095324160 | bytes 20054016 | tf_op jit(solution)/shard_map/dot_general | solution.py:28
  440.6 69.6 %reduce-scatter.13.cloned.1.call-done = bf16[240,2048]{1,0:T(8,128)(2,1)} async-done(((bf16[1920,2048]{1,0:T(8,128)(2,1)}), bf16[240,2048]{1,0:T(8,128)(2,1)}) %reduce-scatter.13.cloned.1.call-update) | async-done | bytes 983056 | tf_op jit(solution)/shard_map/reduce_scatter | solution.py:94
  517.6 11.0 convolution_convert_fusion.5
  528.7 19.4 %convolution_convert_fusion.4 = bf16[2048,1536]{1,0:T(8,128)(2,1)} fusion(bf16[1920,2048]{1,0:T(8,128)(2,1)} %all-gather.12.cloned.1.call-done, bf16[1920,768]{0,1:T(8,128)(2,1)} %get-tuple-element.31, bf16[1920,768]{0,1:T(8,128)(2,1)} %get-tuple-element.30), kind=kOutput, calls=%fused_computation.14 | convolution fusion | flops 12094537728 | bytes 20054016 | tf_op jit(solution)/shard_map/dot_general | solution.py:32
  550.3 19.4 %all-gather.16.cloned.1.call-done = bf16[1920,2048]{1,0:T(8,128)(2,1)} async-done(((bf16[240,2048]{1,0:T(8,128)(2,1)}), bf16[1920,2048]{1,0:T(8,128)(2,1)}) %all-gather.16.cloned.1.call-update) | async-done | bytes 7864336 | tf_op jit(solution)/shard_map/all_gather | solution.py:91
  569.7 5.7 convolution_convert_fusion.8
  576.5 7.8 gather_fusion.2
  587.9 7.0 fusion.3
  606.5 5.0 copy.181
  622.5 7.1 fusion.59
  645.9 8.9 gather_fusion.3
  654.8 10.2 convolution_convert_fusion.6
  665.8 80.9 %reduce-scatter.21.cloned.1.call-done = bf16[8,64,1536]{2,1,0:T(8,128)(2,1)} async-done(((bf16[8,256,1536]{2,1,0:T(8,128)(2,1)}), bf16[8,64,1536]{2,1,0:T(8,128)(2,1)}) %reduce-scatter.21.cloned.1.call-update) | async-done | bytes 1572880 | tf_op jit(solution)/shard_map/reduce_scatter | solution.py:266
  746.6 25.2 %all_to_all.41 = bf16[8,64,1536]{2,1,0:T(8,128)(2,1)} all-to-all(bf16[8,64,1536]{2,1,0:T(8,128)(2,1)} %reduce-scatter.21.cloned.1.call-done), channel_id=1, replica_groups=mesh['rep'=4,'fsdp'=8] {'fsdp'}, dimensions={0} | all-to-all | bytes 3145728 | tf_op jit(solution)/shard_map/all_to_all | solution.py:269
  772.0 5.4 reduce-scatter.19.cloned.1.call-done
  777.4 44.8 %reduce-scatter.17.cloned.1.call-done = bf16[8,64,512]{2,1,0:T(8,128)(2,1)} async-done(((bf16[8,256,512]{2,1,0:T(8,128)(2,1)}), bf16[8,64,512]{2,1,0:T(8,128)(2,1)}) %reduce-scatter.17.cloned.1.call-update) | async-done | bytes 524304 | tf_op jit(solution)/shard_map/reduce_scatter | solution.py:266
  822.2 13.8 %all_to_all.42 = bf16[8,64,512]{2,1,0:T(8,128)(2,1)} all-to-all(bf16[8,64,512]{2,1,0:T(8,128)(2,1)} %reduce-scatter.17.cloned.1.call-done), channel_id=1, replica_groups=mesh['rep'=4,'fsdp'=8] {'fsdp'}, dimensions={0} | all-to-all | bytes 1048576 | tf_op jit(solution)/shard_map/all_to_all | solution.py:269
  836.3 9.6 convolution_convert_fusion.1
  845.9 10.3 convolution_convert_fusion
  856.3 30.1 %all-gather.24.cloned.1.call-done = bf16[768,2048]{1,0:T(8,128)(2,1)} async-done(((bf16[192,2048]{1,0:T(8,128)(2,1)}), bf16[768,2048]{1,0:T(8,128)(2,1)}) %all-gather.24.cloned.1.call-update) | async-done | bytes 3145744 | tf_op jit(solution)/shard_map/all_gather | solution.py:262
  886.4 5.4 convert_element_type.179
  891.9 110.0 %all-gather.22.cloned.1.call-done = bf16[8,256,1536]{2,1,0:T(8,128)(2,1)} async-done(((bf16[8,64,1536]{2,1,0:T(8,128)(2,1)}), bf16[8,256,1536]{2,1,0:T(8,128)(2,1)}) %all-gather.22.cloned.1.call-update) | async-done | bytes 6291472 | tf_op jit(solution)/shard_map/all_gather | solution.py:270
  1001.9 9.1 convert_bitcast_fusion
  1011.0 10.5 slice_bitcast_fusion
  1021.5 6.5 copy.203
  1034.4 41.7 %all-gather.18.cloned.1.call-done = bf16[8,256,512]{2,1,0:T(8,128)(2,1)} async-done(((bf16[8,64,512]{2,1,0:T(8,128)(2,1)}), bf16[8,256,512]{2,1,0:T(8,128)(2,1)}) %all-gather.18.cloned.1.call-update) | async-done | bytes 2097168 | tf_op jit(solution)/shard_map/all_gather | solution.py:270
  1081.9 65.8 %reduce-scatter.15.cloned.1.call-done = bf16[240,2048]{1,0:T(8,128)(2,1)} async-done(((bf16[1920,2048]{1,0:T(8,128)(2,1)}), bf16[240,2048]{1,0:T(8,128)(2,1)}) %reduce-scatter.15.cloned.1.call-update) | async-done | bytes 983056 | tf_op jit(solution)/shard_map/reduce_scatter | solution.py:94
  1150.1 40.3 %psum.7 = f32[4352]{0:T(1024)S(1)} all-reduce(f32[4352]{0:T(1024)S(1)} %pad_maximum_fusion.9), channel_id=1, replica_groups=mesh['rep'=4,'fsdp'=8] {'rep','fsdp'}, use_global_device_ids=true, to_apply=%region_24.25 | all-reduce | flops 4352 | bytes 34816 | tf_op jit(solution)/shard_map/psum | solution.py:282
  1191.6 29.6 %reduce-scatter.11.cloned.1.call-done = bf16[240,2048]{1,0:T(8,128)(2,1)} async-done(((bf16[1920,2048]{1,0:T(8,128)(2,1)}), bf16[240,2048]{1,0:T(8,128)(2,1)}) %reduce-scatter.11.cloned.1.call-update) | async-done | bytes 983056 | tf_op jit(solution)/shard_map/reduce_scatter | solution.py:94
  1221.1 5.6 fusion.37
  (331 shorter events, 134.5 us)
Async XLA Ops:
  7.2 351.9 %copy-start = (bf16[768,2048]{1,0:T(8,128)(2,1)S(1)}, bf16[768,2048]{1,0:T(8,128)(2,1)}, u32[]{:S(2)}) copy-start(bf16[768,2048]{1,0:T(8,128)(2,1)} %param.29) | copy-start | bytes 9437188
  7.2 83.0 %all-gather.10.cloned.1.call-start = ((), (), s32[]{:S(2)}) async-start(), calls=%async_computation.12 | async-start | bytes 8847360 | tf_op jit(solution)/shard_map/all_gather | solution.py:91
  17.5 6.9 copy-start.75
  17.5 6.9 copy-start.76
  17.5 6.9 copy-start.77
  17.5 6.9 copy-start.78
  17.5 68.7 %all-to-all-start = ((bf16[256,8,512]{0,2,1:T(8,128)(2,1)}), bf16[256,8,512]{0,2,1:T(8,128)(2,1)}, u32[]{:S(2)}, u32[]{:S(2)}) async-start(bf16[256,8,512]{0,2,1:T(8,128)(2,1)} %pad_maximum_fusion.6), calls=%async_computation | async-start | bytes 4194304 | tf_op jit(solution)/shard_map/all_to_all | solution.py:119
  22.8 215.3 %reduce-scatter.9.cloned.1.call-start = ((), (), s32[]{:S(2)}) async-start(), calls=%async_computation.13 | async-start | bytes 8847360 | tf_op jit(solution)/shard_map/reduce_scatter | solution.py:94
  76.4 18.8 %copy-start.57 = (f32[1,2,8,128]{3,1,2,0:T(2,128)}, f32[1,2,8,128]{3,1,2,0:T(2,128)S(1)}, u32[]{:S(2)}) copy-start(f32[1,2,8,128]{3,1,2,0:T(2,128)S(1)} %copy.205) | copy-start | bytes 24580
  77.2 62.4 %copy-start.65 = (f32[128]{0:T(128)}, f32[128]{0:T(128)S(1)}, u32[]{:S(2)}) copy-start(f32[128]{0:T(128)S(1)} %mul.485) | copy-start | bytes 1540
  77.3 65.4 %copy-start.69 = (f32[128]{0:T(128)}, f32[128]{0:T(128)S(1)}, u32[]{:S(2)}) copy-start(f32[128]{0:T(128)S(1)} %mul.502) | copy-start | bytes 1540
  77.3 76.9 %copy-start.59 = (s32[2048]{0:T(1024)}, s32[2048]{0:T(1024)S(1)}, u32[]{:S(2)}) copy-start(s32[2048]{0:T(1024)S(1)} %pad_clamp_fusion.1) | copy-start | bytes 24580
  77.4 26.7 %copy-start.51 = (s32[3072]{0:T(1024)}, s32[3072]{0:T(1024)S(1)}, u32[]{:S(2)}) copy-start(s32[3072]{0:T(1024)S(1)} %pad_clamp_fusion) | copy-start | bytes 36868
  77.4 84.0 %copy-start.53 = (pred[1920]{0:T(1024)(128)(4,1)}, pred[1920]{0:T(1024)(128)(4,1)S(1)}, u32[]{:S(2)}) copy-start(pred[1920]{0:T(1024)(128)(4,1)S(1)} %compare_and_fusion.3) | copy-start | bytes 5764
  95.2 6.6 copy-start.71
  121.6 18.0 %copy-start.43 = (f32[8,288]{1,0:T(8,128)}, f32[8,288]{1,0:T(8,128)S(1)}, u32[]{:S(2)}) copy-start(f32[8,288]{1,0:T(8,128)S(1)} %rsqrt.45) | copy-start | bytes 27652
  168.3 190.8 %all-gather.14.cloned.1.call-start = ((), (), s32[]{:S(2)}) async-start(), calls=%async_computation.16 | async-start | bytes 8847360 | tf_op jit(solution)/shard_map/all_gather | solution.py:91
  169.1 222.6 %all-gather.12.cloned.1.call-start = ((), (), s32[]{:S(2)}) async-start(), calls=%async_computation.14 | async-start | bytes 8847360 | tf_op jit(solution)/shard_map/all_gather | solution.py:91
  169.1 344.7 %copy-start.49 = (f32[1,2,8,128]{3,1,2,0:T(2,128)}, f32[1,2,8,128]{3,1,2,0:T(2,128)S(1)}, u32[]{:S(2)}) copy-start(f32[1,2,8,128]{3,1,2,0:T(2,128)S(1)} %copy.207) | copy-start | bytes 24580
  240.2 273.6 %copy-start.63 = (f32[240]{0:T(256)}, f32[240]{0:T(256)S(1)}, u32[]{:S(2)}) copy-start(f32[240]{0:T(256)S(1)} %add_rsqrt_fusion.4) | copy-start | bytes 2884
  241.6 268.5 %reduce-scatter.13.cloned.1.call-start = ((), (), s32[]{:S(2)}) async-start(), calls=%async_computation.17 | async-start | bytes 8847360 | tf_op jit(solution)/shard_map/reduce_scatter | solution.py:94
  440.5 129.2 %all-gather.16.cloned.1.call-start = ((), (), s32[]{:S(2)}) async-start(), calls=%async_computation.18 | async-start | bytes 8847360 | tf_op jit(solution)/shard_map/all_gather | solution.py:91
  517.5 147.5 %reduce-scatter.23.cloned.1.call-start = ((), (), s32[]{:S(2)}) async-start(), calls=%async_computation.26 | async-start | bytes 3932160 | tf_op jit(solution)/shard_map/reduce_scatter | solution.py:261
  528.6 218.0 %reduce-scatter.21.cloned.1.call-start = ((), (), s32[]{:S(2)}) async-start(), calls=%async_computation.24 | async-start | bytes 7864320 | tf_op jit(solution)/shard_map/reduce_scatter | solution.py:266
  548.1 229.2 %reduce-scatter.19.cloned.1.call-start = ((), (), s32[]{:S(2)}) async-start(), calls=%async_computation.22 | async-start | bytes 1310720 | tf_op jit(solution)/shard_map/reduce_scatter | solution.py:261
  550.3 26.2 %copy-start.52 = (s32[3072]{0:T(1024)S(1)}, s32[3072]{0:T(1024)}, u32[]{:S(2)}) copy-start(s32[3072]{0:T(1024)} %copy-done.51) | copy-start | bytes 36868
  587.8 7.0 slice-start
  587.9 7.0 slice-start.1
  587.9 7.0 copy-start.21
  611.8 7.2 slice-start.2
  622.5 7.2 copy-start.44
  622.5 7.2 copy-start.66
  629.6 192.5 %reduce-scatter.17.cloned.1.call-start = ((), (), s32[]{:S(2)}) async-start(), calls=%async_computation.20 | async-start | bytes 2621440 | tf_op jit(solution)/shard_map/reduce_scatter | solution.py:266
  629.7 12.1 slice-start.4
  634.3 7.5 slice-start.5
  645.9 8.9 copy-start.58
  645.9 8.9 copy-start.72
  665.0 221.4 %all-gather.24.cloned.1.call-start = ((), (), s32[]{:S(2)}) async-start(), calls=%async_computation.27 | async-start | bytes 3932160 | tf_op jit(solution)/shard_map/all_gather | solution.py:262
  665.7 336.1 %all-gather.22.cloned.1.call-start = ((), (), s32[]{:S(2)}) async-start(), calls=%async_computation.25 | async-start | bytes 7864320 | tf_op jit(solution)/shard_map/all_gather | solution.py:270
  771.9 259.7 %all-gather.20.cloned.1.call-start = ((), (), s32[]{:S(2)}) async-start(), calls=%async_computation.23 | async-start | bytes 1310720 | tf_op jit(solution)/shard_map/all_gather | solution.py:262
  777.4 298.8 %all-gather.18.cloned.1.call-start = ((), (), s32[]{:S(2)}) async-start(), calls=%async_computation.21 | async-start | bytes 2621440 | tf_op jit(solution)/shard_map/all_gather | solution.py:270
  836.0 311.7 %reduce-scatter.15.cloned.1.call-start = ((), (), s32[]{:S(2)}) async-start(), calls=%async_computation.19 | async-start | bytes 8847360 | tf_op jit(solution)/shard_map/reduce_scatter | solution.py:94
  845.9 375.3 %reduce-scatter.11.cloned.1.call-start = ((), (), s32[]{:S(2)}) async-start(), calls=%async_computation.15 | async-start | bytes 8847360 | tf_op jit(solution)/shard_map/reduce_scatter | solution.py:94
  856.3 35.6 %copy-start.73 = (f32[240]{0:T(256)S(1)}, f32[240]{0:T(256)}, u32[]{:S(2)}) copy-start(f32[240]{0:T(256)} %get-tuple-element.21) | copy-start | bytes 2884
  1080.3 69.7 %copy-start.62 = (f32[2048]{0:T(1024)S(1)}, f32[2048]{0:T(1024)}, u32[]{:S(2)}) copy-start(f32[2048]{0:T(1024)} %get-tuple-element.15) | copy-start | bytes 24580
  1080.3 140.8 %copy-start.50 = (f32[1,2,8,128]{3,1,2,0:T(2,128)S(1)}, f32[1,2,8,128]{3,1,2,0:T(2,128)}, u32[]{:S(2)}) copy-start(f32[1,2,8,128]{3,1,2,0:T(2,128)} %copy-done.49) | copy-start | bytes 24580
  1080.3 140.8 %copy-start.64 = (f32[240]{0:T(256)S(1)}, f32[240]{0:T(256)}, u32[]{:S(2)}) copy-start(f32[240]{0:T(256)} %copy-done.63) | copy-start | bytes 2884
  1080.3 140.8 %copy-start.68 = (f32[240]{0:T(256)S(1)}, f32[240]{0:T(256)}, u32[]{:S(2)}) copy-start(f32[240]{0:T(256)} %copy-done.67) | copy-start | bytes 2884
  (55 other events, 159.2 us)
Sparse Core Ops, SparseCore 0:
  9.9 73.6 all-gather.9
  168.4 69.6 reduce-scatter.8
  240.0 96.9 all-gather.13
  339.4 52.2 all-gather.11
  440.6 69.4 reduce-scatter.12
  517.7 52.0 all-gather.15
  572.6 60.3 reduce-scatter.22
  635.9 110.6 reduce-scatter.20
  749.5 27.7 reduce-scatter.18
  780.0 42.0 reduce-scatter.16
  823.7 62.6 all-gather.23
  887.9 113.9 all-gather.21
  1003.4 26.1 all-gather.19
  1031.1 45.0 all-gather.17
  1079.4 68.2 reduce-scatter.14
  1151.0 70.0 reduce-scatter.10

commit v2 on v1

v2 whole, which is shorter than its diff:
```python
import functools

import jax
import jax.numpy as jnp
from jax import lax
from jax.experimental import pallas as pl
from jax.experimental.pallas import tpu as pltpu
from jax.sharding import PartitionSpec as P


QUERY_HEADS = 16
KEY_VALUE_HEADS = 8
HEAD_SIZE = 128
SLOT_LENGTH = 288

EPSILON = 1e-06
ROPE_BASE = 1000000.0
NEG_LARGE = -1e30

F32 = jnp.float32
BF16 = jnp.bfloat16


def rms_scale(values):
    return lax.rsqrt(jnp.mean(values * values, axis=-1, keepdims=True) + EPSILON)


def dot(left, right):
    return jnp.dot(left, right, preferred_element_type=F32)


def dot_bt(left, right):
    return lax.dot_general(left, right, (((1,), (1,)), ((), ())), preferred_element_type=F32)


def dot_at(left, right):
    return lax.dot_general(left, right, (((0,), (0,)), ((), ())), preferred_element_type=F32)


def norm_back(grad_normed, unit_rows, scale_rows, gain_rows):
    scaled = grad_normed * gain_rows
    return scale_rows * (
        scaled - unit_rows * jnp.mean(scaled * unit_rows, axis=-1, keepdims=True)
    )


def partners(me):
    core, x_bit, y_bit = lax.rem(me, 2), lax.rem(me // 2, 2), me // 4
    along_x = me + 2 - 4 * x_bit
    along_y = me + 4 - 8 * y_bit
    return me + 1 - 2 * core, along_x, along_y, along_x + 4 - 8 * y_bit


def greet(devices):
    barrier = pltpu.get_barrier_semaphore()
    for device in devices:
        pl.semaphore_signal(
            barrier, inc=1, device_id={"fsdp": device}, device_id_type=pl.DeviceIdType.MESH
        )
    pl.semaphore_wait(barrier, len(devices))


def gather_kernel(own, out, send, recv, local):
    me = lax.axis_index("fsdp")
    sib, along_x, along_y, across = partners(me)
    half = own.shape[1] // 2
    left, right = pl.ds(0, half), pl.ds(half, half)
    greet((sib, along_x, along_y))

    def copy(src, dst, slot, device):
        made = pltpu.make_async_remote_copy(
            src_ref=src,
            dst_ref=dst,
            send_sem=send.at[slot],
            recv_sem=recv.at[slot],
            device_id={"fsdp": device},
            device_id_type=pl.DeviceIdType.MESH,
        )
        made.start()
        return made

    mine = pltpu.make_async_copy(own, out.at[me], local)
    copies = [
        copy(own.at[:, left], out.at[me, :, left], 0, along_x),
        copy(own.at[:, right], out.at[me, :, right], 1, along_y),
        copy(own.at[:, right], out.at[me, :, right], 2, along_x),
        copy(own.at[:, left], out.at[me, :, left], 3, along_y),
        copy(own, out.at[me], 4, sib),
    ]
    mine.start()
    copies[0].wait_recv()
    copies.append(copy(out.at[along_x, :, left], out.at[along_x, :, left], 5, along_y))
    copies[1].wait_recv()
    copies.append(copy(out.at[along_y, :, right], out.at[along_y, :, right], 6, along_x))
    copies[2].wait_recv()
    copies.append(copy(out.at[along_x], out.at[along_x], 7, sib))
    copies[3].wait_recv()
    copies.append(copy(out.at[along_y], out.at[along_y], 8, sib))
    copies[5].wait_recv()
    copies[6].wait_recv()
    copies.append(copy(out.at[across], out.at[across], 9, sib))
    for slot in (4, 7, 8, 9):
        copies[slot].wait_recv()
    mine.wait()
    for made in copies:
        made.wait_send()


def gather_rows(values, ident):
    rows, cols = values.shape
    return pl.pallas_call(
        gather_kernel,
        out_shape=jax.ShapeDtypeStruct((8, rows, cols), values.dtype),
        in_specs=[pl.BlockSpec(memory_space=pltpu.VMEM)],
        out_specs=pl.BlockSpec(memory_space=pl.ANY),
        scratch_shapes=[
            pltpu.SemaphoreType.DMA((10,)),
            pltpu.SemaphoreType.DMA((10,)),
            pltpu.SemaphoreType.DMA,
        ],
        compiler_params=pltpu.CompilerParams(collective_id=ident, has_side_effects=True),
        cost_estimate=pl.CostEstimate(
            flops=0, bytes_accessed=rows * cols * 180, transcendentals=0
        ),
        name="gather_rows",
    )(values).reshape(8 * rows, cols)


def scatter_kernel(parts, out, mine, other, first, second, send, recv, local):
    me = lax.axis_index("fsdp")
    sib, along_x, along_y, across = partners(me)
    rows, cols = out.shape
    half = cols // 2
    left, right = pl.ds(0, half), pl.ds(half, half)
    order = (across, along_x, along_y, me)
    loads = []
    for step, device in enumerate(order):
        load = pltpu.make_async_copy(parts.at[device], mine.at[step], local.at[step])
        load.start()
        loads.append(load)
    greet((sib, along_x, along_y))

    def copy(src, dst, slot, device):
        made = pltpu.make_async_remote_copy(
            src_ref=src,
            dst_ref=dst,
            send_sem=send.at[slot],
            recv_sem=recv.at[slot],
            device_id={"fsdp": device},
            device_id_type=pl.DeviceIdType.MESH,
        )
        made.start()
        return made

    copies = [
        copy(parts.at[device + sib - me], other.at[step], step, sib)
        for step, device in enumerate(order)
    ]

    def add(into, term, step_rows=16):
        @pl.loop(0, rows // step_rows)
        def _(index):
            at = pl.ds(pl.multiple_of(index * step_rows, step_rows), step_rows)
            into[at, :] = (into[at, :].astype(F32) + term[at, :].astype(F32)).astype(into.dtype)

    def own_chip(step):
        loads[step].wait()
        copies[step].wait_recv()
        add(mine.at[step], other.at[step])

    own_chip(0)
    copies.append(copy(mine.at[0, :, left], first.at[0], 4, along_x))
    copies.append(copy(mine.at[0, :, right], first.at[1], 5, along_y))
    own_chip(1)
    copies.append(copy(mine.at[1, :, left], first.at[2], 6, along_x))
    own_chip(2)
    copies.append(copy(mine.at[2, :, right], first.at[3], 7, along_y))
    own_chip(3)
    copies[4].wait_recv()
    add(mine.at[2, :, left], first.at[0])
    copies.append(copy(mine.at[2, :, left], second.at[0], 8, along_y))
    copies[5].wait_recv()
    add(mine.at[1, :, right], first.at[1])
    copies.append(copy(mine.at[1, :, right], second.at[1], 9, along_x))
    copies[6].wait_recv()
    copies[7].wait_recv()
    copies[8].wait_recv()
    copies[9].wait_recv()

    @pl.loop(0, rows // 16)
    def _(index):
        at = pl.ds(pl.multiple_of(index * 16, 16), 16)
        for side, cut in enumerate((left, right)):
            out[at, cut] = (
                mine[3, at, cut].astype(F32)
                + first[2 + side, at, :].astype(F32)
                + second[side, at, :].astype(F32)
            )

    for made in copies:
        made.wait_send()


def scatter_rows(values, ident):
    rows, cols = values.shape[0] // 8, values.shape[1]
    return pl.pallas_call(
        scatter_kernel,
        out_shape=jax.ShapeDtypeStruct((rows, cols), F32),
        in_specs=[pl.BlockSpec(memory_space=pl.ANY)],
        out_specs=pl.BlockSpec(memory_space=pltpu.VMEM),
        scratch_shapes=[
            pltpu.VMEM((4, rows, cols), BF16),
            pltpu.VMEM((4, rows, cols), BF16),
            pltpu.VMEM((4, rows, cols // 2), BF16),
            pltpu.VMEM((2, rows, cols // 2), BF16),
            pltpu.SemaphoreType.DMA((10,)),
            pltpu.SemaphoreType.DMA((10,)),
            pltpu.SemaphoreType.DMA((4,)),
        ],
        compiler_params=pltpu.CompilerParams(collective_id=ident, has_side_effects=True),
        cost_estimate=pl.CostEstimate(
            flops=0, bytes_accessed=rows * cols * 200, transcendentals=0
        ),
        name="scatter_rows",
    )(values.astype(BF16).reshape(8, rows, cols))


class Deal:
    def __init__(self, starts, places, counts, in_rows, cap):
        self.starts, self.places, self.counts = starts, places, counts
        self.in_rows = in_rows
        self.window = (cap + 14) // 8 * 8

    def sources(self, run):
        for source in range(self.starts.shape[0]):
            yield (
                source * self.in_rows + self.starts[source, run],
                self.places[source, run],
                self.counts[source, run],
            )

    def move(self, src, dst, src_at, dst_at, count):
        window = self.window
        src_base = jnp.minimum(src_at // 8 * 8, src.shape[0] - window)
        dst_base = jnp.minimum(dst_at // 8 * 8, dst.shape[0] - window)
        lead = dst_at - dst_base
        shift = lax.rem(lead - (src_at - src_base) + window, window)
        rows = src[pl.ds(pl.multiple_of(src_base, 8), window), :]
        rows = pltpu.roll(rows, shift, 0)
        into = pl.ds(pl.multiple_of(dst_base, 8), window)
        row = lax.broadcasted_iota(jnp.int32, rows.shape, 0)
        keep = (row >= lead) & (row < lead + count)
        dst[into, :] = jnp.where(keep, rows, dst[into, :])

    def load(self, packed, slot, run):
        for start, place, count in self.sources(run):
            self.move(packed, slot, start, place, count)

    def store(self, packed, slot, run):
        for start, place, count in self.sources(run):
            self.move(slot, packed, place, start, count)

    def length(self, run):
        total = 0
        for source in range(self.starts.shape[0]):
            total = total + self.counts[source, run]
        return total


KEY_SPAN = 384
BLOCKS = ((0, 128, 128), (128, 256, 256), (256, 288, KEY_SPAN))


def rotate(values, cosine, sine):
    return values * cosine + pltpu.roll(values, HEAD_SIZE // 2, 1) * sine


def unrotate(values, cosine, sine):
    return values * cosine + pltpu.roll(values * sine, HEAD_SIZE // 2, 1)


def block_probs(query, key, first, last, span, length):
    scores = dot_bt(query[first:last], key[:span]) * HEAD_SIZE ** (-0.5)
    row = first + lax.broadcasted_iota(jnp.int32, scores.shape, 0)
    column = lax.broadcasted_iota(jnp.int32, scores.shape, 1)
    scores = jnp.where((column <= row) & (column < length), scores, NEG_LARGE)
    exps = jnp.exp(scores - jnp.max(scores, axis=-1, keepdims=True))
    return exps / jnp.sum(exps, axis=-1, keepdims=True)


def attention_kernel(in_rows, cap, starts, places, counts, raw, gains, trig, out, slot, result, packed):
    deal = Deal(starts, places, counts, in_rows, cap)
    heads = out.shape[1] // HEAD_SIZE
    slot[...] = jnp.zeros_like(slot)
    length_rows = SLOT_LENGTH

    @pl.loop(0, starts.shape[0])
    def _(run):
        deal.load(raw, slot, run)
        length = deal.length(run)
        cosine, sine = trig[0], trig[1]
        key_at = heads * HEAD_SIZE
        key_raw = slot[:KEY_SPAN, key_at : key_at + HEAD_SIZE]
        key = rotate(key_raw * rms_scale(key_raw) * gains[1:2, :], cosine, sine).astype(BF16)
        value = slot[:KEY_SPAN, key_at + HEAD_SIZE :].astype(BF16)
        for head in range(heads):
            cut = slice(head * HEAD_SIZE, (head + 1) * HEAD_SIZE)
            query_raw = slot[:length_rows, cut]
            query = rotate(
                query_raw * rms_scale(query_raw) * gains[0:1, :],
                cosine[:length_rows],
                sine[:length_rows],
            ).astype(BF16)
            for first, last, span in BLOCKS:
                probs = block_probs(query, key, first, last, span, length)
                result[first:last, cut] = dot(probs.astype(BF16), value[:span])
        deal.store(packed, result, run)

    out[...] = packed[...].astype(BF16)


def attention_back_kernel(
    in_rows, cap, starts, places, counts, raw, grads, gains, trig, out, gain_out,
    slot, grad_slot, result, packed, key_sum, value_sum,
):
    deal = Deal(starts, places, counts, in_rows, cap)
    heads = grads.shape[1] // HEAD_SIZE
    slot[...] = jnp.zeros_like(slot)
    grad_slot[...] = jnp.zeros_like(grad_slot)
    gain_out[...] = jnp.zeros_like(gain_out)
    rows = SLOT_LENGTH

    def norm_and_store(grad, raw_rows, gain_row, cut, cosine, sine, gain_at):
        scale = rms_scale(raw_rows)
        unit = raw_rows * scale
        normed = unrotate(grad * HEAD_SIZE ** (-0.5), cosine, sine)
        gain_out[gain_at : gain_at + 1, :] += jnp.sum(normed * unit, axis=0, keepdims=True)
        result[:rows, cut] = norm_back(normed, unit, scale, gain_row)

    @pl.loop(0, starts.shape[0])
    def _(run):
        deal.load(raw, slot, run)
        deal.load(grads, grad_slot, run)
        length = deal.length(run)
        cosine, sine = trig[0], trig[1]
        key_at = heads * HEAD_SIZE
        key_raw = slot[:KEY_SPAN, key_at : key_at + HEAD_SIZE]
        key = rotate(key_raw * rms_scale(key_raw) * gains[1:2, :], cosine, sine).astype(BF16)
        value = slot[:KEY_SPAN, key_at + HEAD_SIZE :].astype(BF16)
        key_sum[...] = jnp.zeros_like(key_sum)
        value_sum[...] = jnp.zeros_like(value_sum)
        inside = lax.broadcasted_iota(jnp.int32, (rows, HEAD_SIZE), 0) < length
        for head in range(heads):
            cut = slice(head * HEAD_SIZE, (head + 1) * HEAD_SIZE)
            query_raw = slot[:rows, cut]
            query = rotate(
                query_raw * rms_scale(query_raw) * gains[0:1, :], cosine[:rows], sine[:rows]
            ).astype(BF16)
            grad_context = jnp.where(inside, grad_slot[:rows, cut], 0.0).astype(BF16)
            pieces = []
            for first, last, span in BLOCKS:
                probs = block_probs(query, key, first, last, span, length)
                grad_rows = grad_context[first:last]
                grad_probs = dot_bt(grad_rows, value[:span])
                value_sum[:span, :] += dot_at(probs.astype(BF16), grad_rows)
                inner = jnp.sum(grad_probs * probs, axis=-1, keepdims=True)
                grad_scores = (probs * (grad_probs - inner)).astype(BF16)
                pieces.append(dot(grad_scores, key[:span]))
                key_sum[:span, :] += dot_at(grad_scores, query[first:last])
            norm_and_store(
                jnp.concatenate(pieces), query_raw, gains[0:1, :], cut, cosine[:rows], sine[:rows], 0
            )
        norm_and_store(
            key_sum[:rows, :],
            key_raw[:rows],
            gains[1:2, :],
            slice(key_at, key_at + HEAD_SIZE),
            cosine[:rows],
            sine[:rows],
            1,
        )
        result[:rows, key_at + HEAD_SIZE :] = value_sum[:rows, :]
        deal.store(packed, result, run)

    out[...] = packed[...].astype(BF16)


def call_attention(kernel, tables, arrays, outs, scratch, in_rows, flops):
    cap = SLOT_LENGTH // tables[0].shape[0]
    vmem = pl.BlockSpec(memory_space=pltpu.VMEM)
    moved = sum(a.size * a.dtype.itemsize for a in arrays)
    return pl.pallas_call(
        functools.partial(kernel, in_rows, cap),
        out_shape=outs,
        in_specs=[pl.BlockSpec(memory_space=pltpu.SMEM)] * 3 + [vmem] * len(arrays),
        out_specs=jax.tree.map(lambda _: vmem, outs),
        scratch_shapes=[pltpu.VMEM(shape, F32) for shape in scratch],
        compiler_params=pltpu.CompilerParams(vmem_limit_bytes=48 << 20),
        cost_estimate=pl.CostEstimate(flops=flops, bytes_accessed=moved, transcendentals=1 << 20),
    )(*tables, *arrays)


def on_device(
    tokens,
    cotangent,
    counts,
    deal_order,
    seq_lengths,
    input_gain,
    w_query,
    key_projection,
    value_projection,
    query_gain,
    key_gain,
    w_out,
    mlp_gain,
    w_gate,
    w_up,
    w_down,
):
    groups = lax.axis_size("fsdp")
    replicas = lax.axis_size("rep")
    in_rows, width = tokens.shape
    shard = width // groups
    heads = QUERY_HEADS // groups
    kv_heads = max(1, KEY_VALUE_HEADS // groups)
    spread = max(1, groups // KEY_VALUE_HEADS)
    q_cols, kv_cols = heads * HEAD_SIZE, kv_heads * HEAD_SIZE
    ff_cols = w_gate.shape[1] // groups

    def gather(values):
        if groups == 8:
            return gather_rows(values, 0 if values.shape[0] == in_rows else 2)
        return lax.all_gather(values, "fsdp", axis=0, tiled=True)

    def scatter_sum(values):
        if groups == 8:
            return scatter_rows(values, 1)
        return lax.psum_scatter(
            values.astype(BF16), "fsdp", scatter_dimension=0, tiled=True
        ).astype(F32)

    def replica_scatter(term, axis):
        return lax.psum_scatter(term, "rep", scatter_dimension=axis, tiled=True)

    def replica_gather(part):
        return lax.all_gather(part, "rep", axis=0, tiled=False)

    def columns_home(part):
        part = lax.all_to_all(part, "fsdp", split_axis=0, concat_axis=0, tiled=True)
        return replica_gather(part)

    head_part = HEAD_SIZE // groups
    gain_row = jnp.concatenate([input_gain, mlp_gain, query_gain, key_gain])
    gain_row = jnp.pad(gain_row[None], ((0, 15), (0, width - gain_row.shape[0])))
    got = gather(jnp.concatenate([tokens, gain_row])).reshape(groups, in_rows + 16, width)

    def kv_columns(weight):
        return jnp.repeat(
            weight.reshape(shard, KEY_VALUE_HEADS // kv_heads, kv_cols), spread, axis=1
        )

    send_attn = jnp.concatenate(
        [
            w_query.reshape(shard, groups, q_cols),
            kv_columns(key_projection),
            kv_columns(value_projection),
        ],
        axis=2,
    )
    w_qkv = lax.all_to_all(send_attn, "fsdp", split_axis=1, concat_axis=0, tiled=True).reshape(
        width, q_cols + 2 * kv_cols
    )
    send_ff = jnp.concatenate(
        [w_gate.reshape(shard, groups, ff_cols), w_up.reshape(shard, groups, ff_cols)], axis=2
    )
    piece = shard // replicas
    got, send_ff, cotangent_late = lax.optimization_barrier((got, send_ff, cotangent))
    all_grads = lax.all_gather(cotangent_late, "fsdp", axis=0, tiled=True)
    send_ff = lax.dynamic_slice(
        send_ff, (lax.axis_index("rep") * piece, 0, 0), (piece, groups, 2 * ff_cols)
    )
    w_ff = lax.all_to_all(send_ff, "fsdp", split_axis=1, concat_axis=0, tiled=False)
    w_ff = lax.all_gather(w_ff, "rep", axis=1, tiled=True).reshape(width, 2 * ff_cols)
    all_tokens = got[:, :in_rows].reshape(groups * in_rows, width)
    gains = got[:, in_rows].astype(F32)
    gain_one = gains[:, :shard].reshape(width)
    gain_two = gains[:, shard : 2 * shard].reshape(width)
    gain_query = gains[:, 2 * shard : 2 * shard + head_part].reshape(HEAD_SIZE)
    gain_key = gains[:, 2 * shard + head_part : 2 * (shard + head_part)].reshape(HEAD_SIZE)

    table = counts[0]
    tables = (
        jnp.cumsum(table, axis=1) - table,
        jnp.cumsum(table, axis=0) - table,
        table,
    )

    resid = tokens.astype(F32)
    scale_one = rms_scale(resid)
    normed_one = resid * scale_one
    all_resid = all_tokens.astype(F32)
    attention_input = (all_resid * rms_scale(all_resid) * gain_one).astype(BF16)
    raw = dot(attention_input, w_qkv)
    inverse = ROPE_BASE ** (-jnp.arange(0, HEAD_SIZE, 2, dtype=F32) / HEAD_SIZE)
    angles = jnp.arange(KEY_SPAN, dtype=F32)[:, None] * inverse
    cosine, sine = jnp.cos(angles), jnp.sin(angles)
    trig = jnp.stack(
        [jnp.concatenate([cosine, cosine], 1), jnp.concatenate([-sine, sine], 1)]
    )
    head_gains = jnp.stack([gain_query, gain_key])
    all_rows = groups * in_rows
    slot_rows = SLOT_LENGTH + HEAD_SIZE
    qkv_cols = q_cols + 2 * kv_cols
    context = call_attention(
        attention_kernel,
        tables,
        (raw, head_gains, trig),
        jax.ShapeDtypeStruct((all_rows, q_cols), BF16),
        ((slot_rows, qkv_cols), (slot_rows, q_cols), (all_rows, q_cols)),
        in_rows,
        4 * groups * heads * SLOT_LENGTH * SLOT_LENGTH * HEAD_SIZE,
    )
    hidden_one = resid + scatter_sum(dot(context, w_out))

    scale_two = rms_scale(hidden_one)
    normed_two = hidden_one * scale_two
    mlp_in = gather((normed_two * gain_two).astype(BF16))
    gate_pre = dot(mlp_in, w_ff[:, :ff_cols])
    up_pre = dot(mlp_in, w_ff[:, ff_cols:])
    sigmoid_gate = jax.nn.sigmoid(gate_pre)
    activ = (gate_pre * sigmoid_gate * up_pre).astype(BF16)

    grad_activ = dot_bt(all_grads, w_down)
    grad_gate = (
        grad_activ * up_pre * sigmoid_gate * (1.0 + gate_pre * (1.0 - sigmoid_gate))
    ).astype(BF16)
    grad_up = (grad_activ * (gate_pre * sigmoid_gate)).astype(BF16)
    grad_ff = jnp.concatenate([grad_gate, grad_up], axis=1)
    down_term = dot_at(activ, all_grads).astype(BF16)
    grad_ff, down_term = lax.optimization_barrier((grad_ff, down_term))
    down_part = replica_scatter(down_term, 0)
    ff_term = dot_at(mlp_in, grad_ff).astype(BF16)
    grad_ff, ff_term = lax.optimization_barrier((grad_ff, ff_term))
    ff_part = replica_scatter(ff_term.reshape(groups, shard, 2 * ff_cols), 1)
    grad_mlp_in = scatter_sum(dot_bt(grad_ff, w_ff))
    grad_norm_two = norm_back(grad_mlp_in, normed_two, scale_two, gain_two)
    grad_hidden = cotangent.astype(F32) + grad_norm_two

    all_hidden = gather(grad_hidden.astype(BF16))
    out_term = dot_at(context, all_hidden).astype(BF16)
    all_hidden, out_term = lax.optimization_barrier((all_hidden, out_term))
    out_part = replica_scatter(out_term, 0)
    grad_qkv, head_terms = call_attention(
        attention_back_kernel,
        tables,
        (raw, dot_bt(all_hidden, w_out), head_gains, trig),
        (
            jax.ShapeDtypeStruct((all_rows, qkv_cols), BF16),
            jax.ShapeDtypeStruct((8, HEAD_SIZE), F32),
        ),
        (
            (slot_rows, qkv_cols),
            (slot_rows, q_cols),
            (slot_rows, qkv_cols),
            (all_rows, qkv_cols),
            (KEY_SPAN, HEAD_SIZE),
            (KEY_SPAN, HEAD_SIZE),
        ),
        in_rows,
        10 * groups * heads * SLOT_LENGTH * SLOT_LENGTH * HEAD_SIZE,
    )
    qkv_term = dot_at(attention_input, grad_qkv).astype(BF16)

    def gain_column(weight, term, gain):
        return jnp.sum(weight.astype(F32) * term.astype(F32), axis=1) / gain

    def head_column(term):
        return jnp.pad(
            term.reshape(groups, head_part), ((0, 0), (0, shard - head_part))
        ).reshape(width)

    gain_terms = jnp.stack(
        [
            gain_column(w_qkv, qkv_term, gain_one),
            gain_column(w_ff, ff_term, gain_two),
            head_column(head_terms[0]),
            head_column(head_terms[1]),
        ],
        axis=1,
    )
    gain_terms = jnp.pad(gain_terms, ((0, 0), (0, HEAD_SIZE - 4)))
    small_term = jnp.concatenate([qkv_term, gain_terms.astype(BF16)], axis=1)
    grad_qkv, small_term, ff_part = lax.optimization_barrier((grad_qkv, small_term, ff_part))
    small_cols = small_term.shape[1]
    small_part = replica_scatter(small_term.reshape(groups, shard, small_cols), 1)
    ff_full = columns_home(ff_part)
    grad_attn_in = scatter_sum(dot_bt(grad_qkv, w_qkv))
    grad_norm_one = norm_back(grad_attn_in, normed_one, scale_one, gain_one)
    input_grad = (grad_hidden + grad_norm_one).astype(BF16)
    activ, grad_attn_in = lax.optimization_barrier((activ, grad_attn_in))
    output = (hidden_one + scatter_sum(dot(activ, w_down))).astype(BF16)

    down_share = replica_gather(down_part).reshape(w_down.shape).astype(F32)
    out_share = replica_gather(out_part).reshape(w_out.shape).astype(F32)
    small_full = columns_home(small_part)

    def columns(full, start, length):
        part = full[:, :, :, start : start + length].astype(F32)
        return jnp.swapaxes(part, 1, 2).reshape(shard, groups, length)

    def kv_share(start):
        part = columns(small_full, start, kv_cols)
        part = part.reshape(shard, groups // spread, spread, kv_cols)
        return jnp.sum(part, axis=2).reshape(shard, KEY_VALUE_HEADS * HEAD_SIZE)

    gain_sums = jnp.sum(small_full[:, :, :, qkv_cols:].astype(F32), axis=1)
    gain_sums = gain_sums.reshape(shard, HEAD_SIZE)
    ff_full = [columns(ff_full, start, ff_cols).reshape(shard, -1) for start in (0, ff_cols)]

    return (
        output,
        input_grad,
        gain_sums[:, 0],
        columns(small_full, 0, q_cols).reshape(shard, groups * q_cols),
        kv_share(q_cols),
        kv_share(q_cols + kv_cols),
        gain_sums[:head_part, 2],
        gain_sums[:head_part, 3],
        out_share,
        gain_sums[:, 1],
        ff_full[0],
        ff_full[1],
        down_share,
    )


def solution(mesh):
    rows = P(("rep", "fsdp"), None)
    vec = P("fsdp")
    mat = P("fsdp", None)
    return jax.shard_map(
        on_device,
        mesh=mesh,
        in_specs=(
            rows,
            rows,
            P("rep", None, None),
            P("rep", None),
            P("rep", "fsdp"),
            vec,
            mat,
            mat,
            mat,
            vec,
            vec,
            mat,
            vec,
            mat,
            mat,
            mat,
        ),
        out_specs=(rows, rows, vec, mat, mat, mat, vec, vec, mat, vec, mat, mat, mat),
        check_vma=False,
    )
```

time: 1240 us -> 905 us (0.73)
  waiting for transfers between devices: 590 us -> 170 us
  Pallas kernels: 0 us -> 357 us
  blocking collectives: 226 us -> 64.2 us
  local copies, waits for them, and re-layouts: 135 us -> 64.4 us
  matrix products: 164 us -> 137 us
    pallas_call x0 -> x9, Pallas kernels: none -> 357 us  [the longest x4 157 us: scatter_rows(): pl.pallas_call(scatter_kernel, out_shape=jax.ShapeDtypeStruct((rows, cols...]
    reduce_scatter x8 -> x4, waiting for transfers between devices: 365 us -> 67.5 us  [replica_scatter(): return lax.psum_scatter(term, 'rep', scatter_dimension=axis, tiled=True)]
    all_gather x8 -> x6, waiting for transfers between devices: 223 us -> 93.2 us  [the longest x4 93.2 us: replica_gather(): return lax.all_gather(part, 'rep', axis=0, tiled=False)]
    all_to_all x3, blocking collectives: 135 us -> 64.2 us  [the longest x2 40.1 us: columns_home(): part = lax.all_to_all(part, 'fsdp', split_axis=0, concat_axis=0, tiled=True)]
    unnamed x1 -> x0, blocking collectives: 50.5 us -> none
    psum x1 -> x0, blocking collectives: 40.3 us -> none  [on_device(): lax.psum(jnp.concatenate([gain_one_grad, gain_two_grad, query_gain_term,...]
    gather x5 -> x0, local copies, waits for them, and re-layouts: 37.5 us -> none  [the longest x3 21.4 us: to_slots(): return jnp.take(pad_rows(values), slot_index, axis=0)]
    dot_general x6 -> x0, matrix products: 21.9 us -> none  [the longest x1 7.15 us: on_device(): jnp.einsum('skgij,sikgd->sjkd', probs_low, grad_context, preferred_elemen...]
  transfers between devices with their start and end apart: 17 -> 11, of which waited for: 12 -> 5; matrix products, arithmetic and copies ran while one was open for 20% -> 21% of each run, Pallas kernels for 0% -> 35%
where the time goes in v2:
time: 905 us; the launch traced here: 898 us
  Pallas kernels  357 us (39%)
  waiting for transfers between devices  170 us (19%)
  matrix products  137 us (15%)
  other arithmetic  85.8 us (9%)
  local copies, waits for them, and re-layouts  64.4 us (7%)
  blocking collectives  64.2 us (7%)
  between operations  15.1 us (2%)
    pallas_call x4, Pallas kernels, scatter_rows(): pl.pallas_call(scatter_kernel, out_shape=jax.ShapeDtypeStruct((rows, cols...  157 us
    pallas_call x3, Pallas kernels, gather_rows(): pl.pallas_call(gather_kernel, out_shape=jax.ShapeDtypeStruct((8, rows, co...  144 us
    all_gather x4, waiting for transfers between devices, replica_gather(): return lax.all_gather(part, 'rep', axis=0, tiled=False)  93.2 us
    reduce_scatter x4, waiting for transfers between devices, replica_scatter(): return lax.psum_scatter(term, 'rep', scatter_dimension=axis, tiled=True)  67.5 us
    pallas_call x2, Pallas kernels, call_attention(): pl.pallas_call(functools.partial(kernel, in_rows, cap), out_shape=outs, i...  55.2 us
    dot_general x5, matrix products, dot(): return jnp.dot(left, right, preferred_element_type=F32)  53.6 us
    dot_general x4, matrix products, dot_at(): lax.dot_general(left, right, (((0,), (0,)), ((), ())), preferred_element_...  42.4 us
    dot_general x4, matrix products, dot_bt(): lax.dot_general(left, right, (((1,), (1,)), ((), ())), preferred_element_...  41.1 us
  transfers between devices with their start and end apart: 11, of which 5 were waited for; matrix products, arithmetic and copies ran while one was open for 21% of the time, Pallas kernels for 35%

profile of v2, /device:TPU:0, one launch (start us, length us, event | category | flops | bytes accessed | tf_op | source)
XLA Modules:
  0.0 898.4 jit_solution(11510315749828252212)
XLA Ops:
  10.5 42.7 %gather_rows.3 = bf16[8,256,2048]{2,1,0:T(8,128)(2,1)} custom-call(bf16[256,2048]{1,0:T(8,128)(2,1)} %fusion.16.own), custom_call_target="tpu_custom_call" | custom-call | bytes 94371840 | tf_op jit(solution)/shard_map/gather_rows/pallas_call | solution.py:111
  53.2 3.5 copy_bitcast_fusion
  61.5 24.1 %all_to_all.40 = bf16[1,64,8,1536]{3,1,0,2:T(8,128)(2,1)} all-to-all(bf16[1,64,8,1536]{3,1,0,2:T(8,128)(2,1)S(1)} %dynamic-slice_bitcast_fusion), channel_id=1, replica_groups=mesh['rep'=4,'fsdp'=8] {'fsdp'}, dimensions={2} | all-to-all | bytes 3145728 | tf_op jit(solution)/shard_map/all_to_all | solution.py:483
  96.0 4.5 all-to-all-start
  105.4 4.8 multiply_reduce_fusion
  110.9 8.3 multiply_convert_fusion
  119.2 7.9 all-to-all-done
  129.0 7.4 fusion.29.raw
  136.4 22.3 %shard_map.237 = bf16[1920,256]{1,0:T(8,128)(2,1)S(1)} custom-call(s32[8,8]{1,0:T(8,128)S(1)} %get-tuple-element.68.starts, s32[8,8]{1,0:T(8,128)S(1)} %get-tuple-element.67.places, s32[8,8]{1,0:T(8,128)S(1)} %bitcast.140, f32[1920,512]{1,0:T(8,128)S(1)} %fusion.29.raw, f32[2,128]{1,0:T(2,128)S(1)} %pad_maximum_fusion.6.gains, ...), custom_call_target="tpu_custom_call" | custom-call | flops 679477248 | bytes 4326400 | tf_op jit(solution)/shard_map/pallas_call | solution.py:392
  158.8 5.4 convolution_convert_fusion.3
  164.2 37.9 %scatter_rows.4 = f32[240,2048]{1,0:T(8,128)} custom-call(bf16[8,240,2048]{2,1,0:T(8,128)(2,1)} %bitcast.144), custom_call_target="tpu_custom_call" | custom-call | bytes 98304000 | tf_op jit(solution)/shard_map/scatter_rows/pallas_call | solution.py:206
  206.9 63.1 %gather_rows.4 = bf16[8,240,2048]{2,1,0:T(8,128)(2,1)} custom-call(bf16[240,2048]{1,0:T(8,128)(2,1)} %multiply_convert_fusion.4.own), custom_call_target="tpu_custom_call" | custom-call | bytes 88473600 | tf_op jit(solution)/shard_map/gather_rows/pallas_call | solution.py:111
  270.0 12.4 %fusion.3 = f32[1920,768]{0,1:T(8,128)} fusion(bf16[1920,2048]{1,0:T(8,128)(2,1)} %bitcast.155, bf16[2048,1536]{1,0:T(8,128)(2,1)} %bitcast.161), kind=kOutput, calls=%fused_computation.24 | convolution fusion | flops 6039797760 | bytes 16908288 | tf_op jit(solution)/shard_map/dot_general | solution.py:29
  282.4 10.8 %fusion.30 = f32[1920,768]{0,1:T(8,128)} fusion(bf16[1920,2048]{1,0:T(8,128)(2,1)} %all-gather.12.cloned.1.call-done, bf16[768,2048]{1,0:T(8,128)(2,1)S(1)} %copy-done), kind=kOutput, calls=%fused_computation.102 | convolution fusion | flops 6039797760 | bytes 16908288 | tf_op jit(solution)/shard_map/dot_general | solution.py:33
  293.2 18.2 %multiply_convert_fusion.2 = (bf16[1920,768]{0,1:T(8,128)(2,1)}, bf16[1920,768]{0,1:T(8,128)(2,1)}, bf16[1920,768]{0,1:T(8,128)(2,1)}) fusion(f32[1920,768]{0,1:T(8,128)} %fusion.30, f32[1920,768]{0,1:T(8,128)} %fusion.3, bf16[1920,2048]{1,0:T(8,128)(2,1)} %bitcast.156, bf16[2048,1536]{1,0:T(8,128)(2,1)} %bitcast.162), kind=kOutput, calls=%fused_computation.16 | convolution fusion | flops 6061916160 | bytes 31653888 | tf_op jit(solution)/shard_map/dot_general | solution.py:29
  311.4 6.3 pad_maximum_fusion.1
  319.3 8.0 convolution_convert_fusion.5
  327.4 19.4 %convolution_convert_fusion.4 = bf16[2048,1536]{1,0:T(8,128)(2,1)} fusion(bf16[1920,2048]{1,0:T(8,128)(2,1)} %bitcast.157, bf16[1920,1536]{0,1:T(8,128)(2,1)} %pad_maximum_fusion.1), kind=kOutput, calls=%fused_computation.10 | convolution fusion | flops 12082741248 | bytes 20054016 | tf_op jit(solution)/shard_map/dot_general | solution.py:37
  346.8 18.3 %convolution_convert_fusion.2 = bf16[1920,2048]{1,0:T(8,128)(2,1)} fusion(bf16[1920,1536]{0,1:T(8,128)(2,1)} %pad_maximum_fusion.1, bf16[2048,1536]{1,0:T(8,128)(2,1)} %bitcast.163), kind=kOutput, calls=%fused_computation.8 | convolution fusion | flops 12083527680 | bytes 20054016 | tf_op jit(solution)/shard_map/dot_general | solution.py:33
  365.2 39.6 %scatter_rows.5 = f32[240,2048]{1,0:T(8,128)} custom-call(bf16[8,240,2048]{2,1,0:T(8,128)(2,1)} %bitcast.153), custom_call_target="tpu_custom_call" | custom-call | bytes 98304000 | tf_op jit(solution)/shard_map/scatter_rows/pallas_call | solution.py:206
  404.8 3.8 fusion.15
  412.0 38.7 %gather_rows.5 = bf16[8,240,2048]{2,1,0:T(8,128)(2,1)} custom-call(bf16[240,2048]{1,0:T(8,128)(2,1)} %fusion.27.own), custom_call_target="tpu_custom_call" | custom-call | bytes 88473600 | tf_op jit(solution)/shard_map/gather_rows/pallas_call | solution.py:111
  450.7 6.9 convolution_convert_fusion.7
  461.9 8.3 fusion.1
  470.2 5.6 fusion.31.grads
  475.8 33.0 %shard_map.238 = (bf16[1920,512]{1,0:T(8,128)(2,1)S(1)}, f32[8,128]{1,0:T(8,128)S(1)}) custom-call(s32[8,8]{1,0:T(8,128)S(1)} %get-tuple-element.68.starts, s32[8,8]{1,0:T(8,128)S(1)} %get-tuple-element.67.places, s32[8,8]{1,0:T(8,128)S(1)} %bitcast.141, f32[1920,512]{1,0:T(8,128)} %copy-done.1, f32[1920,256]{1,0:T(8,128)S(1)} %fusion.31.grads, ...), custom_call_target="tpu_custom_call" | custom-call | flops 1698693120 | bytes 6292480 | tf_op jit(solution)/shard_map/pallas_call | solution.py:392
  510.3 6.5 multiply_reduce_fusion.1
  516.9 8.1 multiply_reduce_fusion.2
  526.9 4.1 copy.95
  531.0 5.3 copy.75
  537.1 12.6 %reduce-scatter.11.cloned.1.call-done = bf16[192,2048]{1,0:T(8,128)(2,1)} async-done(((bf16[768,2048]{1,0:T(8,128)(2,1)}), bf16[192,2048]{1,0:T(8,128)(2,1)}) %reduce-scatter.11.cloned.1.call-update) | async-done | bytes 786448 | tf_op jit(solution)/shard_map/reduce_scatter | solution.py:444
  549.8 54.9 %reduce-scatter.7.cloned.1.call-done = bf16[8,64,640]{2,0,1:T(8,128)(2,1)} async-done(((bf16[8,256,640]{2,0,1:T(8,128)(2,1)}), bf16[8,64,640]{2,0,1:T(8,128)(2,1)}) %reduce-scatter.7.cloned.1.call-update) | async-done | bytes 655376 | tf_op jit(solution)/shard_map/reduce_scatter | solution.py:444
  605.8 14.6 %all_to_all.41 = bf16[8,64,640]{2,1,0:T(8,128)(2,1)} all-to-all(bf16[8,64,640]{2,1,0:T(8,128)(2,1)S(1)} %copy.76), channel_id=1, replica_groups=mesh['rep'=4,'fsdp'=8] {'fsdp'}, dimensions={0} | all-to-all | bytes 1310720 | tf_op jit(solution)/shard_map/all_to_all | solution.py:450
  620.5 25.5 %all_to_all.42 = bf16[8,64,1536]{2,1,0:T(8,128)(2,1)} all-to-all(bf16[8,64,1536]{2,1,0:T(8,128)(2,1)} %reduce-scatter.5.cloned.1.call-done), channel_id=1, replica_groups=mesh['rep'=4,'fsdp'=8] {'fsdp'}, dimensions={0} | all-to-all | bytes 3145728 | tf_op jit(solution)/shard_map/all_to_all | solution.py:450
  648.9 49.3 %all-gather.22.cloned.1.call-done = bf16[768,2048]{1,0:T(8,128)(2,1)} async-done(((bf16[192,2048]{1,0:T(8,128)(2,1)}), bf16[768,2048]{1,0:T(8,128)(2,1)}) %all-gather.22.cloned.1.call-update) | async-done | bytes 3145744 | tf_op jit(solution)/shard_map/all_gather | solution.py:447
  698.2 5.6 convert_element_type.154
  703.8 6.4 convolution_convert_fusion.1
  710.1 39.5 %scatter_rows.6 = f32[240,2048]{1,0:T(8,128)} custom-call(bf16[8,240,2048]{2,1,0:T(8,128)(2,1)} %bitcast.152), custom_call_target="tpu_custom_call" | custom-call | bytes 98304000 | tf_op jit(solution)/shard_map/scatter_rows/pallas_call | solution.py:206
  749.6 10.3 %convolution_convert_fusion = bf16[1920,2048]{1,0:T(8,128)(2,1)} fusion(bf16[1920,768]{0,1:T(8,128)(2,1)} %get-tuple-element.38, bf16[768,2048]{1,0:T(8,128)(2,1)S(1)} %copy-done), kind=kOutput, calls=%fused_computation.6 | convolution fusion | flops 6043729920 | bytes 13959168 | tf_op jit(solution)/shard_map/dot_general | solution.py:29
  760.0 39.9 %scatter_rows.7 = f32[240,2048]{1,0:T(8,128)} custom-call(bf16[8,240,2048]{2,1,0:T(8,128)(2,1)} %bitcast.154), custom_call_target="tpu_custom_call" | custom-call | bytes 98304000 | tf_op jit(solution)/shard_map/scatter_rows/pallas_call | solution.py:206
  802.6 5.8 fusion.14
  818.0 3.3 copy.85
  824.8 43.9 %all-gather.20.cloned.1.call-done = bf16[32,64,1536]{2,1,0:T(8,128)(2,1)} async-done(((bf16[8,64,1536]{2,1,0:T(8,128)(2,1)}), bf16[32,64,1536]{2,1,0:T(8,128)(2,1)}) %all-gather.20.cloned.1.call-update) | async-done | bytes 6291472 | tf_op jit(solution)/shard_map/all_gather | solution.py:447
  868.7 4.6 convert_bitcast_fusion
  873.3 3.8 copy.83
  877.1 5.3 copy.100
  882.4 3.6 copy.82
  886.1 5.3 copy.99
  (164 shorter events, 64.1 us)
Async XLA Ops:
  7.2 275.2 %copy-start = (bf16[768,2048]{1,0:T(8,128)(2,1)S(1)}, bf16[768,2048]{1,0:T(8,128)(2,1)}, u32[]{:S(2)}) copy-start(bf16[768,2048]{1,0:T(8,128)(2,1)} %param.29) | copy-start | bytes 9437188
  7.2 262.8 %all-gather.14.cloned.1.call-start = ((), (), s32[]{:S(2)}) async-start(), calls=%async_computation.13 | async-start | bytes 7864320 | tf_op jit(solution)/shard_map/all_gather | solution.py:484
  85.6 196.8 %all-gather.12.cloned.1.call-start = ((), (), s32[]{:S(2)}) async-start(), calls=%async_computation.8 | async-start | bytes 8847360 | tf_op jit(solution)/shard_map/all_gather | solution.py:479
  96.0 4.5 copy-start.3
  96.0 31.1 %all-to-all-start = ((bf16[256,8,512]{0,2,1:T(8,128)(2,1)}), bf16[256,8,512]{0,2,1:T(8,128)(2,1)}, u32[]{:S(2)}, u32[]{:S(2)}) async-start(bf16[256,8,512]{0,2,1:T(8,128)(2,1)} %pad_maximum_fusion.3), calls=%async_computation | async-start | bytes 4194304 | tf_op jit(solution)/shard_map/all_to_all | solution.py:471
  100.5 426.4 %reduce-scatter.5.cloned.1.call-start = ((), (), s32[]{:S(2)}) async-start(), calls=%async_computation.9 | async-start | bytes 7864320 | tf_op jit(solution)/shard_map/reduce_scatter | solution.py:444
  104.4 5.9 copy-start.22
  105.4 4.9 copy-start.30
  105.4 4.9 copy-start.31
  110.3 0.6 copy-start.24
  129.0 7.4 copy-start.15
  136.4 27.7 %copy-start.1 = (f32[1920,512]{1,0:T(8,128)}, f32[1920,512]{1,0:T(8,128)S(1)}, u32[]{:S(2)}) copy-start(f32[1920,512]{1,0:T(8,128)S(1)} %fusion.29.raw) | copy-start | bytes 11796484
  136.4 22.3 %copy-start.18 = (bf16[256,2048]{1,0:T(8,128)(2,1)S(1)}, bf16[256,2048]{1,0:T(8,128)(2,1)}, u32[]{:S(2)}) copy-start(bf16[256,2048]{1,0:T(8,128)(2,1)} %param.25) | copy-start | bytes 3145732
  158.7 5.4 copy-start.2
  202.0 2.9 copy-start.7
  202.1 2.9 copy-start.10
  204.4 0.6 copy-start.27
  311.4 6.6 copy-start.35
  311.4 7.9 copy-start.36
  346.8 189.6 %reduce-scatter.9.cloned.1.call-start = ((), (), s32[]{:S(2)}) async-start(), calls=%async_computation.11 | async-start | bytes 1310720 | tf_op jit(solution)/shard_map/reduce_scatter | solution.py:444
  404.8 4.4 copy-start.8
  404.8 4.4 copy-start.11
  404.8 4.4 copy-start.13
  404.8 4.4 copy-start.20
  404.8 4.4 copy-start.28
  408.6 0.6 copy-start.32
  457.6 92.1 %reduce-scatter.11.cloned.1.call-start = ((), (), s32[]{:S(2)}) async-start(), calls=%async_computation.12 | async-start | bytes 3932160 | tf_op jit(solution)/shard_map/reduce_scatter | solution.py:444
  461.6 143.0 %reduce-scatter.7.cloned.1.call-start = ((), (), s32[]{:S(2)}) async-start(), calls=%async_computation.10 | async-start | bytes 3276800 | tf_op jit(solution)/shard_map/reduce_scatter | solution.py:444
  461.9 8.3 copy-start.19
  508.7 1.3 copy-start.4
  510.3 6.6 copy-start.26
  510.3 6.6 copy-start.5
  510.3 6.6 copy-start.16
  516.9 8.1 copy-start.25
  536.3 109.8 %all-gather.18.cloned.1.call-start = ((), (), s32[]{:S(2)}) async-start(), calls=%async_computation.15 | async-start | bytes 1310720 | tf_op jit(solution)/shard_map/all_gather | solution.py:447
  537.1 161.1 %all-gather.22.cloned.1.call-start = ((), (), s32[]{:S(2)}) async-start(), calls=%async_computation.17 | async-start | bytes 3932160 | tf_op jit(solution)/shard_map/all_gather | solution.py:447
  549.7 258.6 %all-gather.16.cloned.1.call-start = ((), (), s32[]{:S(2)}) async-start(), calls=%async_computation.14 | async-start | bytes 3276800 | tf_op jit(solution)/shard_map/all_gather | solution.py:447
  605.8 40.2 %copy-start.34 = (f32[240]{0:T(256)S(1)}, f32[240]{0:T(256)}, u32[]{:S(2)}) copy-start(f32[240]{0:T(256)} %get-tuple-element.43) | copy-start | bytes 2884
  620.5 248.2 %all-gather.20.cloned.1.call-start = ((), (), s32[]{:S(2)}) async-start(), calls=%async_computation.16 | async-start | bytes 7864320 | tf_op jit(solution)/shard_map/all_gather | solution.py:447
  698.2 5.6 copy-start.6
  698.2 5.6 copy-start.17
  760.0 39.9 %copy-start.23 = (f32[1,2,8,128]{3,1,2,0:T(2,128)S(1)}, f32[1,2,8,128]{3,1,2,0:T(2,128)}, u32[]{:S(2)}) copy-start(f32[1,2,8,128]{3,1,2,0:T(2,128)} %copy-done.22) | copy-start | bytes 24580
  760.0 42.4 %copy-start.21 = (f32[1,2,8,128]{3,1,2,0:T(2,128)S(1)}, f32[1,2,8,128]{3,1,2,0:T(2,128)}, u32[]{:S(2)}) copy-start(f32[1,2,8,128]{3,1,2,0:T(2,128)} %copy.90) | copy-start | bytes 24580
  760.0 42.4 %copy-start.29 = (f32[240]{0:T(256)S(1)}, f32[240]{0:T(256)}, u32[]{:S(2)}) copy-start(f32[240]{0:T(256)} %copy-done.27) | copy-start | bytes 2884
  760.0 42.4 %copy-start.33 = (f32[240]{0:T(256)S(1)}, f32[240]{0:T(256)}, u32[]{:S(2)}) copy-start(f32[240]{0:T(256)} %copy-done.32) | copy-start | bytes 2884
  799.9 2.5 copy-start.9
  799.9 2.7 copy-start.12
  811.1 2.2 copy-start.14
Sparse Core Ops, SparseCore 0:
  85.7 114.6 all-gather.13
  202.3 74.2 all-gather.11
  346.9 111.0 reduce-scatter.4
  460.8 27.8 reduce-scatter.8
  490.8 58.9 reduce-scatter.10
  552.4 52.1 reduce-scatter.6
  606.2 27.5 all-gather.17
  635.3 62.8 all-gather.21
  699.8 53.3 all-gather.15
  754.6 114.0 all-gather.19

commit v3 on v2

--- a/solution.py
+++ b/solution.py
@@ -60,24 +60,27 @@
     pl.semaphore_wait(barrier, len(devices))
 
 
-def gather_kernel(own, out, send, recv, local):
+def send(src, dst, send_sem, recv_sem, device):
+    made = pltpu.make_async_remote_copy(
+        src_ref=src,
+        dst_ref=dst,
+        send_sem=send_sem,
+        recv_sem=recv_sem,
+        device_id={"fsdp": device},
+        device_id_type=pl.DeviceIdType.MESH,
+    )
+    made.start()
+    return made
+
+
+def exchange_rows(own, out, sends, recvs, local, between=None):
     me = lax.axis_index("fsdp")
     sib, along_x, along_y, across = partners(me)
     half = own.shape[1] // 2
     left, right = pl.ds(0, half), pl.ds(half, half)
-    greet((sib, along_x, along_y))
 
     def copy(src, dst, slot, device):
-        made = pltpu.make_async_remote_copy(
-            src_ref=src,
-            dst_ref=dst,
-            send_sem=send.at[slot],
-            recv_sem=recv.at[slot],
-            device_id={"fsdp": device},
-            device_id_type=pl.DeviceIdType.MESH,
-        )
-        made.start()
-        return made
+        return send(src, dst, sends.at[slot], recvs.at[slot], device)
 
     mine = pltpu.make_async_copy(own, out.at[me], local)
     copies = [
@@ -92,6 +95,8 @@
     copies.append(copy(out.at[along_x, :, left], out.at[along_x, :, left], 5, along_y))
     copies[1].wait_recv()
     copies.append(copy(out.at[along_y, :, right], out.at[along_y, :, right], 6, along_x))
+    if between:
+        between()
     copies[2].wait_recv()
     copies.append(copy(out.at[along_x], out.at[along_x], 7, sib))
     copies[3].wait_recv()
@@ -104,6 +109,11 @@
     mine.wait()
     for made in copies:
         made.wait_send()
+
+
+def gather_kernel(own, out, sends, recvs, local):
+    greet(partners(lax.axis_index("fsdp"))[:3])
+    exchange_rows(own, out, sends, recvs, local)
 
 
 def gather_rows(values, ident):
@@ -124,6 +134,114 @@
         ),
         name="gather_rows",
     )(values).reshape(8 * rows, cols)
+
+
+def start_kernel(
+    own, w_query, w_key, w_value, w_gate, w_up, out, w_qkv, w_ff,
+    own_qkv, own_ff, sends, recvs, local, w_sends, w_recvs, w_local,
+):
+    me = lax.axis_index("fsdp")
+    core, x_bit, y_bit = lax.rem(me, 2), lax.rem(me // 2, 2), me // 4
+    shard = w_query.shape[0]
+    piece = w_ff.shape[1]
+    rows = pl.ds(pl.multiple_of(me * shard, shard), shard)
+    part = pl.ds(pl.multiple_of(lax.axis_index("rep") * piece, piece), piece)
+    pairs = []
+    at = 0
+    for weight in (w_query, w_key, w_value):
+        cols = weight.shape[1] // 8
+        pairs.append((weight, slice(None), cols, w_qkv.at[rows, at : at + cols], own_qkv, at))
+        at += cols
+    at = 0
+    for weight in (w_gate, w_up):
+        cols = weight.shape[1] // 8
+        pairs.append((weight, part, cols, w_ff.at[me, :, at : at + cols], own_ff, at))
+        at += cols
+
+    def source(pair, device):
+        weight, taken, cols = pair[:3]
+        return weight.at[taken, pl.ds(pl.multiple_of(device * cols, cols), cols)]
+
+    peers = []
+    for flip in (6, 2, 4, 7, 3, 5, 1):
+        bits = [
+            1 - bit if flip >> place & 1 else bit
+            for place, bit in enumerate((core, x_bit, y_bit))
+        ]
+        peers.append((flip - 1, bits[0] + 2 * bits[1] + 4 * bits[2]))
+    into = [
+        pltpu.make_async_copy(
+            source(pair, me), pair[4].at[:, pair[5] : pair[5] + pair[2]], w_local.at[index]
+        )
+        for index, pair in enumerate(pairs)
+    ]
+    for made in into:
+        made.start()
+    greet([device for _, device in peers])
+    copies = []
+
+    def between():
+        for chosen in ((0, 1, 2), (3, 4)):
+            for slot, device in peers:
+                for index in chosen:
+                    copies.append(
+                        send(
+                            source(pairs[index], device),
+                            pairs[index][3],
+                            w_sends.at[slot, index],
+                            w_recvs.at[slot, index],
+                            device,
+                        )
+                    )
+
+    exchange_rows(own, out, sends, recvs, local, between)
+    for made in into:
+        made.wait()
+    home = [
+        pltpu.make_async_copy(own_qkv, w_qkv.at[rows, :], w_local.at[0]),
+        pltpu.make_async_copy(own_ff, w_ff.at[me], w_local.at[1]),
+    ]
+    for made in home:
+        made.start()
+    for made in copies:
+        made.wait_recv()
+    for made in copies:
+        made.wait_send()
+    for made in home:
+        made.wait()
+
+
+def start(values, weights, replicas, ident):
+    rows, cols = values.shape
+    shard = weights[0].shape[0]
+    qkv_cols = sum(w.shape[1] for w in weights[:3]) // 8
+    ff_cols = sum(w.shape[1] for w in weights[3:]) // 8
+    anywhere = pl.BlockSpec(memory_space=pl.ANY)
+    return pl.pallas_call(
+        start_kernel,
+        out_shape=(
+            jax.ShapeDtypeStruct((8, rows, cols), values.dtype),
+            jax.ShapeDtypeStruct((8 * shard, qkv_cols), BF16),
+            jax.ShapeDtypeStruct((8, shard // replicas, ff_cols), BF16),
+        ),
+        in_specs=[pl.BlockSpec(memory_space=pltpu.VMEM)] + [anywhere] * 5,
+        out_specs=(anywhere,) * 3,
+        scratch_shapes=[
+            pltpu.VMEM((shard, qkv_cols), BF16),
+            pltpu.VMEM((shard // replicas, ff_cols), BF16),
+            pltpu.SemaphoreType.DMA((10,)),
+            pltpu.SemaphoreType.DMA((10,)),
+            pltpu.SemaphoreType.DMA,
+            pltpu.SemaphoreType.DMA((7, 5)),
+            pltpu.SemaphoreType.DMA((7, 5)),
+            pltpu.SemaphoreType.DMA((5,)),
+        ],
+        compiler_params=pltpu.CompilerParams(collective_id=ident, has_side_effects=True),
+        cost_estimate=pl.CostEstimate(
+            flops=0, bytes_accessed=rows * cols * 360, transcendentals=0
+        ),
+        name="start",
+    )(values, *weights)
 
 
 def scatter_kernel(parts, out, mine, other, first, second, send, recv, local):
@@ -223,6 +341,36 @@
         ),
         name="scatter_rows",
     )(values.astype(BF16).reshape(8, rows, cols))
+
+
+def place_kernel(widths, shared, got, *outs):
+    at = 0
+    for width, share, out in zip(widths, shared, outs):
+        for place in range(got.shape[0] // share):
+            total = got[place * share, :, at : at + width].astype(F32)
+            for source in range(place * share + 1, (place + 1) * share):
+                total = total + got[source, :, at : at + width].astype(F32)
+            out[:, place * width : (place + 1) * width] = total
+        at += width
+
+
+def place_columns(full, widths, shared):
+    replicas, groups, rows, cols = full.shape
+    return pl.pallas_call(
+        functools.partial(place_kernel, widths, shared),
+        out_shape=[
+            jax.ShapeDtypeStruct((replicas * rows, groups // share * width), F32)
+            for width, share in zip(widths, shared)
+        ],
+        grid=(replicas,),
+        in_specs=[pl.BlockSpec((None, groups, rows, cols), lambda i: (i, 0, 0, 0))],
+        out_specs=[
+            pl.BlockSpec((rows, groups // share * width), lambda i: (i, 0))
+            for width, share in zip(widths, shared)
+        ],
+        cost_estimate=pl.CostEstimate(flops=0, bytes_accessed=full.size * 6, transcendentals=0),
+        name="place_columns",
+    )(full)
 
 
 class Deal:
@@ -420,6 +568,7 @@
 ):
     groups = lax.axis_size("fsdp")
     replicas = lax.axis_size("rep")
+    device = lax.axis_index("fsdp")
     in_rows, width = tokens.shape
     shard = width // groups
     heads = QUERY_HEADS // groups
@@ -428,23 +577,23 @@
     q_cols, kv_cols = heads * HEAD_SIZE, kv_heads * HEAD_SIZE
     ff_cols = w_gate.shape[1] // groups
 
+    def replica_gather(part):
+        return lax.all_gather(part, "rep", axis=0, tiled=False)
+
     def gather(values):
-        if groups == 8:
-            return gather_rows(values, 0 if values.shape[0] == in_rows else 2)
-        return lax.all_gather(values, "fsdp", axis=0, tiled=True)
+        if groups != 8:
+            return lax.all_gather(values, "fsdp", axis=0, tiled=True)
+        return gather_rows(values, 0)
 
     def scatter_sum(values):
-        if groups == 8:
-            return scatter_rows(values, 1)
-        return lax.psum_scatter(
-            values.astype(BF16), "fsdp", scatter_dimension=0, tiled=True
-        ).astype(F32)
+        if groups != 8:
+            return lax.psum_scatter(
+                values.astype(BF16), "fsdp", scatter_dimension=0, tiled=True
+            ).astype(F32)
+        return scatter_rows(values, 1)
 
     def replica_scatter(term, axis):
         return lax.psum_scatter(term, "rep", scatter_dimension=axis, tiled=True)
-
-    def replica_gather(part):
-        return lax.all_gather(part, "rep", axis=0, tiled=False)
 
     def columns_home(part):
         part = lax.all_to_all(part, "fsdp", split_axis=0, concat_axis=0, tiled=True)
@@ -453,34 +602,36 @@
     head_part = HEAD_SIZE // groups
     gain_row = jnp.concatenate([input_gain, mlp_gain, query_gain, key_gain])
     gain_row = jnp.pad(gain_row[None], ((0, 15), (0, width - gain_row.shape[0])))
-    got = gather(jnp.concatenate([tokens, gain_row])).reshape(groups, in_rows + 16, width)
-
-    def kv_columns(weight):
-        return jnp.repeat(
-            weight.reshape(shard, KEY_VALUE_HEADS // kv_heads, kv_cols), spread, axis=1
+    start_rows = jnp.concatenate([tokens, gain_row])
+    if groups == 8:
+        got, w_qkv, w_ff = start(
+            start_rows,
+            (w_query, key_projection, value_projection, w_gate, w_up),
+            replicas,
+            2,
         )
-
-    send_attn = jnp.concatenate(
-        [
-            w_query.reshape(shard, groups, q_cols),
-            kv_columns(key_projection),
-            kv_columns(value_projection),
-        ],
-        axis=2,
-    )
-    w_qkv = lax.all_to_all(send_attn, "fsdp", split_axis=1, concat_axis=0, tiled=True).reshape(
-        width, q_cols + 2 * kv_cols
-    )
-    send_ff = jnp.concatenate(
-        [w_gate.reshape(shard, groups, ff_cols), w_up.reshape(shard, groups, ff_cols)], axis=2
-    )
-    piece = shard // replicas
-    got, send_ff, cotangent_late = lax.optimization_barrier((got, send_ff, cotangent))
+    else:
+        got = gather(start_rows)
+        kv_shape = (shard, KEY_VALUE_HEADS // kv_heads, kv_cols)
+        keys = jnp.repeat(key_projection.reshape(kv_shape), spread, axis=1)
+        values = jnp.repeat(value_projection.reshape(kv_shape), spread, axis=1)
+        send_qkv = jnp.concatenate(
+            [w_query.reshape(shard, groups, q_cols), keys, values], axis=2
+        )
+        w_qkv = lax.all_to_all(send_qkv, "fsdp", split_axis=1, concat_axis=0, tiled=True)
+        w_qkv = w_qkv.reshape(width, q_cols + 2 * kv_cols)
+        send_ff = jnp.concatenate(
+            [w_gate.reshape(shard, groups, ff_cols), w_up.reshape(shard, groups, ff_cols)], axis=2
+        )
+        piece = shard // replicas
+        send_ff = lax.dynamic_slice(
+            send_ff, (lax.axis_index("rep") * piece, 0, 0), (piece, groups, 2 * ff_cols)
+        )
+        w_ff = lax.all_to_all(send_ff, "fsdp", split_axis=1, concat_axis=0, tiled=False)
+        w_ff = w_ff.reshape(groups, piece, 2 * ff_cols)
+    got = got.reshape(groups, in_rows + 16, width)
+    got, cotangent_late = lax.optimization_barrier((got, cotangent))
     all_grads = lax.all_gather(cotangent_late, "fsdp", axis=0, tiled=True)
-    send_ff = lax.dynamic_slice(
-        send_ff, (lax.axis_index("rep") * piece, 0, 0), (piece, groups, 2 * ff_cols)
-    )
-    w_ff = lax.all_to_all(send_ff, "fsdp", split_axis=1, concat_axis=0, tiled=False)
     w_ff = lax.all_gather(w_ff, "rep", axis=1, tiled=True).reshape(width, 2 * ff_cols)
     all_tokens = got[:, :in_rows].reshape(groups * in_rows, width)
     gains = got[:, in_rows].astype(F32)
@@ -575,22 +726,7 @@
     def gain_column(weight, term, gain):
         return jnp.sum(weight.astype(F32) * term.astype(F32), axis=1) / gain
 
-    def head_column(term):
-        return jnp.pad(
-            term.reshape(groups, head_part), ((0, 0), (0, shard - head_part))
-        ).reshape(width)
-
-    gain_terms = jnp.stack(
-        [
-            gain_column(w_qkv, qkv_term, gain_one),
-            gain_column(w_ff, ff_term, gain_two),
-            head_column(head_terms[0]),
-            head_column(head_terms[1]),
-        ],
-        axis=1,
-    )
-    gain_terms = jnp.pad(gain_terms, ((0, 0), (0, HEAD_SIZE - 4)))
-    small_term = jnp.concatenate([qkv_term, gain_terms.astype(BF16)], axis=1)
+    small_term = qkv_term
     grad_qkv, small_term, ff_part = lax.optimization_barrier((grad_qkv, small_term, ff_part))
     small_cols = small_term.shape[1]
     small_part = replica_scatter(small_term.reshape(groups, shard, small_cols), 1)
@@ -599,39 +735,43 @@
     grad_norm_one = norm_back(grad_attn_in, normed_one, scale_one, gain_one)
     input_grad = (grad_hidden + grad_norm_one).astype(BF16)
     activ, grad_attn_in = lax.optimization_barrier((activ, grad_attn_in))
-    output = (hidden_one + scatter_sum(dot(activ, w_down))).astype(BF16)
-
-    down_share = replica_gather(down_part).reshape(w_down.shape).astype(F32)
-    out_share = replica_gather(out_part).reshape(w_out.shape).astype(F32)
+    last_sum = scatter_sum(dot(activ, w_down))
+    output = (hidden_one + last_sum).astype(BF16)
+    small_part, last_sum = lax.optimization_barrier((small_part, last_sum))
     small_full = columns_home(small_part)
-
-    def columns(full, start, length):
-        part = full[:, :, :, start : start + length].astype(F32)
-        return jnp.swapaxes(part, 1, 2).reshape(shard, groups, length)
-
-    def kv_share(start):
-        part = columns(small_full, start, kv_cols)
-        part = part.reshape(shard, groups // spread, spread, kv_cols)
-        return jnp.sum(part, axis=2).reshape(shard, KEY_VALUE_HEADS * HEAD_SIZE)
-
-    gain_sums = jnp.sum(small_full[:, :, :, qkv_cols:].astype(F32), axis=1)
-    gain_sums = gain_sums.reshape(shard, HEAD_SIZE)
-    ff_full = [columns(ff_full, start, ff_cols).reshape(shard, -1) for start in (0, ff_cols)]
+    down_full = replica_gather(down_part)
+    out_full = replica_gather(out_part)
+
+    gate_share, up_share = place_columns(ff_full, (ff_cols, ff_cols), (1, 1))
+    query_share, key_share, value_share = place_columns(
+        small_full, (q_cols, kv_cols, kv_cols), (1, spread, spread)
+    )
+    gain_terms = (
+        gain_column(w_qkv, qkv_term, gain_one),
+        gain_column(w_ff, ff_term, gain_two),
+        head_terms[0],
+        head_terms[1],
+    )
+    gain_terms, _ = lax.optimization_barrier((jnp.concatenate(gain_terms), last_sum))
+    gain_sums = lax.psum(gain_terms, ("rep", "fsdp"))
+
+    def own(first, length):
+        return lax.dynamic_slice(gain_sums, (first + device * length,), (length,))
 
     return (
         output,
         input_grad,
-        gain_sums[:, 0],
-        columns(small_full, 0, q_cols).reshape(shard, groups * q_cols),
-        kv_share(q_cols),
-        kv_share(q_cols + kv_cols),
-        gain_sums[:head_part, 2],
-        gain_sums[:head_part, 3],
-        out_share,
-        gain_sums[:, 1],
-        ff_full[0],
-        ff_full[1],
-        down_share,
+        own(0, shard),
+        query_share,
+        key_share,
+        value_share,
+        own(2 * width, head_part),
+        own(2 * width + HEAD_SIZE, head_part),
+        out_full.reshape(w_out.shape).astype(F32),
+        own(width, shard),
+        gate_share,
+        up_share,
+        down_full.reshape(w_down.shape).astype(F32),
     )
 
 

time: 905 us -> 858 us (0.948)
  local copies, waits for them, and re-layouts: 64.4 us -> 11.1 us
  Pallas kernels: 357 us -> 394 us
  waiting for transfers between devices: 170 us -> 146 us
  other arithmetic: 85.8 us -> 65 us
  blocking collectives: 64.2 us -> 82.6 us
    pallas_call x0 -> x3, Pallas kernels: none -> 92.2 us  [the longest x1 80.4 us: start(): pl.pallas_call(start_kernel, out_shape=(jax.ShapeDtypeStruct((8, rows, co...]
    pallas_call x3 -> x2, Pallas kernels: 144 us -> 88.7 us  [gather_rows(): pl.pallas_call(gather_kernel, out_shape=jax.ShapeDtypeStruct((8, rows, co...]
    psum x0 -> x1, blocking collectives: none -> 43.6 us  [on_device(): gain_sums = lax.psum(gain_terms, ('rep', 'fsdp'))]
    unnamed x95 -> x74, local copies, waits for them, and re-layouts: 39.6 us -> 8.19 us
    reduce_scatter x4, waiting for transfers between devices: 67.5 us -> 40.2 us  [replica_scatter(): return lax.psum_scatter(term, 'rep', scatter_dimension=axis, tiled=True)]
    all_to_all x1 -> x0, blocking collectives: 24.1 us -> none  [on_device(): lax.all_to_all(send_ff, 'fsdp', split_axis=1, concat_axis=0, tiled=False)]
    convert_element_type x2 -> x3, other arithmetic: 8.38 us -> 19.7 us  [the longest x1 10.7 us: on_device(): all_resid = all_tokens.astype(F32)]
    reshape x4 -> x0, local copies, waits for them, and re-layouts: 10 us -> none  [the longest x1 5.3 us: on_device(): small_term.reshape(groups, shard, small_cols)]
  transfers between devices with their start and end apart: 11 -> 10, of which waited for: 5 -> 3; matrix products, arithmetic and copies ran while one was open for 21% -> 17% of each run, Pallas kernels for 35% -> 36%
where the time goes in v3:
time: 858 us; the launch traced here: 853 us
  Pallas kernels  394 us (46%)
  waiting for transfers between devices  146 us (17%)
  matrix products  139 us (16%)
  blocking collectives  82.6 us (10%)
  other arithmetic  65 us (8%)
  between operations  15.2 us (2%)
  local copies, waits for them, and re-layouts  11.1 us (1%)
    pallas_call x4, Pallas kernels, scatter_rows(): pl.pallas_call(scatter_kernel, out_shape=jax.ShapeDtypeStruct((rows, cols...  157 us
    all_gather x4, waiting for transfers between devices, replica_gather(): return lax.all_gather(part, 'rep', axis=0, tiled=False)  94.3 us
    pallas_call x2, Pallas kernels, gather_rows(): pl.pallas_call(gather_kernel, out_shape=jax.ShapeDtypeStruct((8, rows, co...  88.7 us
    pallas_call x1, Pallas kernels, start(): pl.pallas_call(start_kernel, out_shape=(jax.ShapeDtypeStruct((8, rows, co...  80.4 us
    pallas_call x2, Pallas kernels, call_attention(): pl.pallas_call(functools.partial(kernel, in_rows, cap), out_shape=outs, i...  55.4 us
    dot_general x5, matrix products, dot(): return jnp.dot(left, right, preferred_element_type=F32)  50.5 us
    dot_general x4, matrix products, dot_bt(): lax.dot_general(left, right, (((1,), (1,)), ((), ())), preferred_element_...  44.4 us
    dot_general x4, matrix products, dot_at(): lax.dot_general(left, right, (((0,), (0,)), ((), ())), preferred_element_...  43.8 us
  transfers between devices with their start and end apart: 10, of which 3 were waited for; matrix products, arithmetic and copies ran while one was open for 17% of the time, Pallas kernels for 36%

profile of v3, /device:TPU:0, one launch (start us, length us, event | category | flops | bytes accessed | tf_op | source)
XLA Modules:
  0.0 853.1 jit_solution(15431141458131933076)
XLA Ops:
  7.2 0.9 pad_maximum_fusion.3
  8.2 2.3 fusion.16.own
  10.5 80.4 %start.1 = (bf16[8,256,2048]{2,1,0:T(8,128)(2,1)}, bf16[2048,512]{1,0:T(8,128)(2,1)}, bf16[8,64,1536]{2,1,0:T(8,128)(2,1)}) custom-call(bf16[256,2048]{1,0:T(8,128)(2,1)} %fusion.16.own, bf16[256,2048]{1,0:T(8,128)(2,1)} %w_query.1, bf16[256,1024]{1,0:T(8,128)(2,1)} %w_key.1, bf16[256,1024]{1,0:T(8,128)(2,1)} %w_value.1, bf16[256,6144]{1,0:T(8,128)(2,1)} %w_gate.1, ...), custom_call_target="tpu_custom_call" | custom-call | bytes 188743680 | tf_op jit(solution)/shard_map/start/pallas_call | solution.py:220
  93.0 1.0 slice_convert_fusion.1
  95.3 5.1 multiply_reduce_fusion
  103.0 10.7 %slice_convert_fusion = f32[8,240,2048]{2,1,0:T(8,128)} fusion(bf16[8,256,2048]{2,1,0:T(8,128)(2,1)} %get-tuple-element.37), kind=kLoop, calls=%fused_computation.5 | loop fusion | flops 3932160 | bytes 23592960 | tf_op jit(solution)/shard_map/convert_element_type | solution.py:653
  113.7 7.0 fusion.1
  120.8 4.3 fusion.24.raw
  125.1 22.3 %shard_map.237 = bf16[1920,256]{1,0:T(8,128)(2,1)S(1)} custom-call(s32[8,8]{1,0:T(8,128)S(1)} %get-tuple-element.77.starts, s32[8,8]{1,0:T(8,128)S(1)} %get-tuple-element.76.places, s32[8,8]{1,0:T(8,128)S(1)} %bitcast.64, f32[1920,512]{1,0:T(8,128)S(1)} %fusion.24.raw, f32[2,128]{1,0:T(2,128)S(1)} %pad_maximum_fusion.4.gains, ...), custom_call_target="tpu_custom_call" | custom-call | flops 679477248 | bytes 4326400 | tf_op jit(solution)/shard_map/pallas_call | solution.py:540
  147.4 5.3 convolution_convert_fusion.3
  152.7 39.5 %scatter_rows.4 = f32[240,2048]{1,0:T(8,128)} custom-call(bf16[8,240,2048]{2,1,0:T(8,128)(2,1)} %bitcast.68), custom_call_target="tpu_custom_call" | custom-call | bytes 98304000 | tf_op jit(solution)/shard_map/scatter_rows/pallas_call | solution.py:324
  193.1 2.2 multiply_reduce_fusion.4
  195.9 1.3 multiply_convert_fusion.3.own
  197.1 50.2 %gather_rows.2 = bf16[8,240,2048]{2,1,0:T(8,128)(2,1)} custom-call(bf16[240,2048]{1,0:T(8,128)(2,1)} %multiply_convert_fusion.3.own), custom_call_target="tpu_custom_call" | custom-call | bytes 88473600 | tf_op jit(solution)/shard_map/gather_rows/pallas_call | solution.py:121
  247.4 12.6 %fusion.3 = f32[1920,768]{0,1:T(8,128)} fusion(bf16[1920,2048]{1,0:T(8,128)(2,1)} %bitcast.73, bf16[2048,1536]{1,0:T(8,128)(2,1)} %bitcast.77), kind=kOutput, calls=%fused_computation.19 | convolution fusion | flops 6039797760 | bytes 16908288 | tf_op jit(solution)/shard_map/dot_general | solution.py:29
  260.0 9.5 %all-gather.13.cloned.1.call-done = bf16[1920,2048]{1,0:T(8,128)(2,1)} async-done(((bf16[240,2048]{1,0:T(8,128)(2,1)}), bf16[1920,2048]{1,0:T(8,128)(2,1)}) %all-gather.13.cloned.1.call-update) | async-done | bytes 7864336 | tf_op jit(solution)/shard_map/all_gather | solution.py:634
  269.5 10.6 %fusion.25 = f32[1920,768]{0,1:T(8,128)} fusion(bf16[1920,2048]{1,0:T(8,128)(2,1)} %all-gather.13.cloned.1.call-done, bf16[768,2048]{1,0:T(8,128)(2,1)S(1)} %copy-done), kind=kOutput, calls=%fused_computation.73 | convolution fusion | flops 6039797760 | bytes 16908288 | tf_op jit(solution)/shard_map/dot_general | solution.py:33
  280.1 17.9 %multiply_convert_fusion.1 = (bf16[1920,768]{0,1:T(8,128)(2,1)}, bf16[1920,768]{0,1:T(8,128)(2,1)}, bf16[1920,768]{0,1:T(8,128)(2,1)}) fusion(f32[1920,768]{0,1:T(8,128)} %fusion.25, f32[1920,768]{0,1:T(8,128)} %fusion.3, bf16[1920,2048]{1,0:T(8,128)(2,1)} %bitcast.74, bf16[2048,1536]{1,0:T(8,128)(2,1)} %bitcast.78), kind=kOutput, calls=%fused_computation.13 | convolution fusion | flops 6061916160 | bytes 31653888 | tf_op jit(solution)/shard_map/dot_general | solution.py:29
  298.0 6.3 pad_maximum_fusion
  304.7 1.3 copy-done.34
  306.0 8.4 convolution_convert_fusion.5
  314.4 19.0 %convolution_convert_fusion.4 = bf16[2048,1536]{1,0:T(8,128)(2,1)} fusion(bf16[1920,2048]{1,0:T(8,128)(2,1)} %bitcast.75, bf16[1920,1536]{0,1:T(8,128)(2,1)} %pad_maximum_fusion), kind=kOutput, calls=%fused_computation.10 | convolution fusion | flops 12082741248 | bytes 20054016 | tf_op jit(solution)/shard_map/dot_general | solution.py:37
  333.5 18.5 %convolution_convert_fusion.2 = bf16[1920,2048]{1,0:T(8,128)(2,1)} fusion(bf16[1920,1536]{0,1:T(8,128)(2,1)} %pad_maximum_fusion, bf16[2048,1536]{1,0:T(8,128)(2,1)} %bitcast.79), kind=kOutput, calls=%fused_computation.8 | convolution fusion | flops 12083527680 | bytes 20054016 | tf_op jit(solution)/shard_map/dot_general | solution.py:33
  351.9 39.4 %scatter_rows.5 = f32[240,2048]{1,0:T(8,128)} custom-call(bf16[8,240,2048]{2,1,0:T(8,128)(2,1)} %bitcast.71), custom_call_target="tpu_custom_call" | custom-call | bytes 98304000 | tf_op jit(solution)/shard_map/scatter_rows/pallas_call | solution.py:324
  391.4 3.7 fusion.15
  395.8 2.8 fusion.20.own
  398.6 38.5 %gather_rows.3 = bf16[8,240,2048]{2,1,0:T(8,128)(2,1)} custom-call(bf16[240,2048]{1,0:T(8,128)(2,1)} %fusion.20.own), custom_call_target="tpu_custom_call" | custom-call | bytes 88473600 | tf_op jit(solution)/shard_map/gather_rows/pallas_call | solution.py:121
  437.1 6.9 convolution_convert_fusion.7
  444.8 5.7 fusion.26.grads
  450.6 33.1 %shard_map.238 = (bf16[1920,512]{1,0:T(8,128)(2,1)S(1)}, f32[8,128]{1,0:T(8,128)S(1)}) custom-call(s32[8,8]{1,0:T(8,128)S(1)} %get-tuple-element.77.starts, s32[8,8]{1,0:T(8,128)S(1)} %get-tuple-element.76.places, s32[8,8]{1,0:T(8,128)S(1)} %bitcast.65, f32[1920,512]{1,0:T(8,128)} %copy-done.1, f32[1920,256]{1,0:T(8,128)S(1)} %fusion.26.grads, ...), custom_call_target="tpu_custom_call" | custom-call | flops 1698693120 | bytes 6292480 | tf_op jit(solution)/shard_map/pallas_call | solution.py:540
  484.2 1.3 copy-done.5
  485.5 9.5 %multiply_reduce_fusion.2 = (f32[2048]{0:T(1024)S(1)}, bf16[2048,512]{1,0:T(8,128)(2,1)}) fusion(bf16[2048,512]{1,0:T(8,128)(2,1)S(1)} %copy-done.33, bf16[1920,2048]{1,0:T(8,128)(2,1)} %copy-done.17, bf16[1920,512]{1,0:T(8,128)(2,1)S(1)} %get-tuple-element.46), kind=kOutput, calls=%fused_computation.17 | convolution fusion | flops 4031772672 | bytes 14032896 | tf_op jit(solution)/shard_map/dot_general | solution.py:37
  495.8 40.2 %reduce-scatter.11.cloned.1.call-done = bf16[192,2048]{1,0:T(8,128)(2,1)} async-done(((bf16[768,2048]{1,0:T(8,128)(2,1)}), bf16[192,2048]{1,0:T(8,128)(2,1)}) %reduce-scatter.11.cloned.1.call-update) | async-done | bytes 786448 | tf_op jit(solution)/shard_map/reduce_scatter | solution.py:596
  536.3 9.6 %convolution_convert_fusion.1 = bf16[1920,2048]{1,0:T(8,128)(2,1)} fusion(bf16[1920,512]{1,0:T(8,128)(2,1)} %copy-done.5, bf16[2048,512]{1,0:T(8,128)(2,1)} %get-tuple-element.38), kind=kOutput, calls=%fused_computation.7 | convolution fusion | flops 4030464000 | bytes 11927552 | tf_op jit(solution)/shard_map/dot_general | solution.py:33
  545.9 38.9 %scatter_rows.6 = f32[240,2048]{1,0:T(8,128)} custom-call(bf16[8,240,2048]{2,1,0:T(8,128)(2,1)} %bitcast.70), custom_call_target="tpu_custom_call" | custom-call | bytes 98304000 | tf_op jit(solution)/shard_map/scatter_rows/pallas_call | solution.py:324
  584.8 10.4 %convolution_convert_fusion = bf16[1920,2048]{1,0:T(8,128)(2,1)} fusion(bf16[1920,768]{0,1:T(8,128)(2,1)} %get-tuple-element.47, bf16[768,2048]{1,0:T(8,128)(2,1)S(1)} %copy-done), kind=kOutput, calls=%fused_computation.6 | convolution fusion | flops 6043729920 | bytes 13959168 | tf_op jit(solution)/shard_map/dot_general | solution.py:29
  595.3 39.4 %scatter_rows.7 = f32[240,2048]{1,0:T(8,128)} custom-call(bf16[8,240,2048]{2,1,0:T(8,128)(2,1)} %bitcast.72), custom_call_target="tpu_custom_call" | custom-call | bytes 98304000 | tf_op jit(solution)/shard_map/scatter_rows/pallas_call | solution.py:324
  634.7 13.8 %all_to_all.10 = bf16[8,64,512]{2,1,0:T(8,128)(2,1)} all-to-all(bf16[8,64,512]{2,1,0:T(8,128)(2,1)} %reduce-scatter.7.cloned.1.call-done), channel_id=1, replica_groups=mesh['rep'=4,'fsdp'=8] {'fsdp'}, dimensions={0} | all-to-all | bytes 1048576 | tf_op jit(solution)/shard_map/all_to_all | solution.py:599
  648.7 25.2 %all_to_all.11 = bf16[8,64,1536]{2,1,0:T(8,128)(2,1)} all-to-all(bf16[8,64,1536]{2,1,0:T(8,128)(2,1)} %reduce-scatter.5.cloned.1.call-done), channel_id=1, replica_groups=mesh['rep'=4,'fsdp'=8] {'fsdp'}, dimensions={0} | all-to-all | bytes 3145728 | tf_op jit(solution)/shard_map/all_to_all | solution.py:599
  674.0 6.4 multiply_reduce_fusion.1
  681.2 43.6 %psum.7 = f32[4352]{0:T(1024)S(1)} all-reduce(f32[4352]{0:T(1024)S(1)} %pad_maximum_fusion.2), channel_id=1, replica_groups=mesh['rep'=4,'fsdp'=8] {'rep','fsdp'}, use_global_device_ids=true, to_apply=%region_10.11 | all-reduce | flops 4352 | bytes 34816 | tf_op jit(solution)/shard_map/psum | solution.py:756
  726.0 2.8 convert_element_type.130
  728.9 6.2 convert_element_type.131
  735.6 1.1 copy-done.8
  736.9 2.8 fusion.14
  739.7 4.1 place_columns.2
  743.8 94.2 %all-gather.19.cloned.1.call-done = bf16[32,64,1536]{2,1,0:T(8,128)(2,1)} async-done(((bf16[8,64,1536]{2,1,0:T(8,128)(2,1)}), bf16[32,64,1536]{2,1,0:T(8,128)(2,1)}) %all-gather.19.cloned.1.call-update) | async-done | bytes 6291472 | tf_op jit(solution)/shard_map/all_gather | solution.py:581
  838.0 7.7 place_columns.3
  (123 shorter events, 14.0 us)
Async XLA Ops:
  7.2 262.3 %copy-start = (bf16[768,2048]{1,0:T(8,128)(2,1)S(1)}, bf16[768,2048]{1,0:T(8,128)(2,1)}, u32[]{:S(2)}) copy-start(bf16[768,2048]{1,0:T(8,128)(2,1)} %param.29) | copy-start | bytes 9437188
  7.2 240.2 %all-gather.11.cloned.1.call-start = ((), (), s32[]{:S(2)}) async-start(), calls=%async_computation.6 | async-start | bytes 7864320 | tf_op jit(solution)/shard_map/all_gather | solution.py:635
  10.5 81.2 %copy-start.3 = (s32[1,8,8]{2,1,0:T(8,128)S(1)}, s32[1,8,8]{2,1,0:T(8,128)}, u32[]{:S(2)}) copy-start(s32[1,8,8]{2,1,0:T(8,128)} %param.18) | copy-start | bytes 772
  90.9 178.6 %all-gather.13.cloned.1.call-start = ((), (), s32[]{:S(2)}) async-start(), calls=%async_computation.7 | async-start | bytes 8847360 | tf_op jit(solution)/shard_map/all_gather | solution.py:634
  91.6 403.3 %reduce-scatter.5.cloned.1.call-start = ((), (), s32[]{:S(2)}) async-start(), calls=%async_computation.8 | async-start | bytes 7864320 | tf_op jit(solution)/shard_map/reduce_scatter | solution.py:596
  103.0 10.7 %copy-start.22 = (f32[1,2,8,128]{3,1,2,0:T(2,128)S(1)}, f32[1,2,8,128]{3,1,2,0:T(2,128)}, u32[]{:S(2)}) copy-start(f32[1,2,8,128]{3,1,2,0:T(2,128)} %copy.31) | copy-start | bytes 24580
  103.0 10.7 %copy-start.24 = (f32[1920]{0:T(1024)S(1)}, f32[1920]{0:T(1024)}, u32[]{:S(2)}) copy-start(f32[1920]{0:T(1024)} %rsqrt.28) | copy-start | bytes 23044
  113.7 7.0 copy-start.32
  120.8 4.3 copy-start.17
  125.0 27.7 %copy-start.1 = (f32[1920,512]{1,0:T(8,128)}, f32[1920,512]{1,0:T(8,128)S(1)}, u32[]{:S(2)}) copy-start(f32[1920,512]{1,0:T(8,128)S(1)} %fusion.24.raw) | copy-start | bytes 11796484
  125.1 22.3 %copy-start.18 = (bf16[256,2048]{1,0:T(8,128)(2,1)S(1)}, bf16[256,2048]{1,0:T(8,128)(2,1)}, u32[]{:S(2)}) copy-start(bf16[256,2048]{1,0:T(8,128)(2,1)} %param.25) | copy-start | bytes 3145732
  147.4 5.3 copy-start.2
  192.2 3.6 copy-start.6
  192.2 3.6 copy-start.9
  193.1 2.2 copy-start.19
  195.3 0.6 copy-start.25
  298.0 6.6 copy-start.31
  298.0 7.9 copy-start.34
  333.4 161.7 %reduce-scatter.9.cloned.1.call-start = ((), (), s32[]{:S(2)}) async-start(), calls=%async_computation.10 | async-start | bytes 1310720 | tf_op jit(solution)/shard_map/reduce_scatter | solution.py:596
  391.4 4.4 copy-start.7
  391.4 4.4 copy-start.10
  391.4 4.4 copy-start.12
  391.4 4.3 copy-start.20
  391.4 4.3 copy-start.26
  395.2 0.6 copy-start.28
  444.0 92.0 %reduce-scatter.11.cloned.1.call-start = ((), (), s32[]{:S(2)}) async-start(), calls=%async_computation.11 | async-start | bytes 3932160 | tf_op jit(solution)/shard_map/reduce_scatter | solution.py:596
  444.6 190.2 %reduce-scatter.7.cloned.1.call-start = ((), (), s32[]{:S(2)}) async-start(), calls=%async_computation.9 | async-start | bytes 2621440 | tf_op jit(solution)/shard_map/reduce_scatter | solution.py:596
  450.6 34.9 %copy-start.33 = (bf16[2048,512]{1,0:T(8,128)(2,1)S(1)}, bf16[2048,512]{1,0:T(8,128)(2,1)}, u32[]{:S(2)}) copy-start(bf16[2048,512]{1,0:T(8,128)(2,1)} %get-tuple-element.38) | copy-start | bytes 6291460
  483.6 0.6 copy-start.4
  484.2 1.3 copy-start.5
  495.0 231.0 %all-gather.17.cloned.1.call-start = ((), (), s32[]{:S(2)}) async-start(), calls=%async_computation.13 | async-start | bytes 1310720 | tf_op jit(solution)/shard_map/all_gather | solution.py:581
  495.8 233.1 %all-gather.21.cloned.1.call-start = ((), (), s32[]{:S(2)}) async-start(), calls=%async_computation.15 | async-start | bytes 3932160 | tf_op jit(solution)/shard_map/all_gather | solution.py:581
  536.0 203.6 %all-gather.15.cloned.1.call-start = ((), (), s32[]{:S(2)}) async-start(), calls=%async_computation.12 | async-start | bytes 2621440 | tf_op jit(solution)/shard_map/all_gather | solution.py:581
  634.7 39.2 %copy-start.23 = (f32[1,2,8,128]{3,1,2,0:T(2,128)S(1)}, f32[1,2,8,128]{3,1,2,0:T(2,128)}, u32[]{:S(2)}) copy-start(f32[1,2,8,128]{3,1,2,0:T(2,128)} %copy.31) | copy-start | bytes 24580
  648.6 189.4 %all-gather.19.cloned.1.call-start = ((), (), s32[]{:S(2)}) async-start(), calls=%async_computation.14 | async-start | bytes 7864320 | tf_op jit(solution)/shard_map/all_gather | solution.py:581
  674.0 6.4 copy-start.21
  674.0 52.0 %copy-start.30 = (f32[240]{0:T(256)S(1)}, f32[240]{0:T(256)}, u32[]{:S(2)}) copy-start(f32[240]{0:T(256)} %get-tuple-element.59) | copy-start | bytes 2884
  728.8 6.7 copy-start.27
  728.8 6.7 copy-start.29
  728.8 6.2 copy-start.11
  728.8 6.2 copy-start.14
  728.8 6.7 copy-start.13
  728.8 6.7 copy-start.16
  735.0 1.6 copy-start.8
  735.0 1.8 copy-start.15
Sparse Core Ops, SparseCore 0:
  91.0 115.6 all-gather.10
  208.6 60.8 all-gather.12
  333.5 110.7 reduce-scatter.4
  447.1 27.8 reduce-scatter.8
  477.1 58.9 reduce-scatter.10
  538.7 43.5 reduce-scatter.6
  583.9 27.1 all-gather.16
  612.6 62.8 all-gather.20
  677.1 45.3 all-gather.14
  723.9 114.1 all-gather.18

commit v4 on v3

--- a/solution.py
+++ b/solution.py
@@ -1,4 +1,5 @@
 import functools
+import math
 
 import jax
 import jax.numpy as jnp
@@ -136,112 +137,152 @@
     )(values).reshape(8 * rows, cols)
 
 
+def flipped(me, flip):
+    bits = (lax.rem(me, 2), lax.rem(me // 2, 2), me // 4)
+    bits = [1 - bit if flip >> place & 1 else bit for place, bit in enumerate(bits)]
+    return bits[0] + 2 * bits[1] + 4 * bits[2]
+
+
+class Columns:
+    def __init__(self, weights, taken, out, staged, sends, recvs, local):
+        self.me = lax.axis_index("fsdp")
+        self.weights, self.taken, self.out, self.staged = weights, taken, out, staged
+        self.sends, self.recvs, self.local = sends, recvs, local
+        self.peers = [(flip - 1, flipped(self.me, flip)) for flip in (6, 2, 4, 7, 3, 5, 1)]
+        self.cuts = []
+        at = 0
+        for weight in weights:
+            cols = weight.shape[1] // 8
+            self.cuts.append(slice(at, at + cols))
+            at += cols
+        self.copies = []
+
+    def source(self, index, device):
+        cols = self.weights[index].shape[1] // 8
+        return self.weights[index].at[
+            self.taken, pl.ds(pl.multiple_of(device * cols, cols), cols)
+        ]
+
+    def stage(self):
+        self.staging = [
+            pltpu.make_async_copy(
+                self.source(index, self.me), self.staged.at[:, cut], self.local.at[index]
+            )
+            for index, cut in enumerate(self.cuts)
+        ]
+        for made in self.staging:
+            made.start()
+
+    def send(self):
+        for slot, device in self.peers:
+            for index, cut in enumerate(self.cuts):
+                self.copies.append(
+                    send(
+                        self.source(index, device),
+                        self.out.at[self.me, :, cut],
+                        self.sends.at[slot, index],
+                        self.recvs.at[slot, index],
+                        device,
+                    )
+                )
+
+    def finish(self):
+        for made in self.staging:
+            made.wait()
+        home = pltpu.make_async_copy(self.staged, self.out.at[self.me], self.local.at[0])
+        home.start()
+        for made in self.copies:
+            made.wait_recv()
+        for made in self.copies:
+            made.wait_send()
+        home.wait()
+
+
+def columns_kernel(w_gate, w_up, *refs):
+    piece = refs[0].shape[1]
+    taken = pl.ds(pl.multiple_of(lax.axis_index("rep") * piece, piece), piece)
+    parts = [
+        Columns((weight,), taken, refs[index], *refs[2 + 4 * index : 6 + 4 * index])
+        for index, weight in enumerate((w_gate, w_up))
+    ]
+    for columns in parts:
+        columns.stage()
+    greet([device for _, device in parts[0].peers])
+    for columns in parts:
+        columns.send()
+    for columns in parts:
+        columns.finish()
+
+
 def start_kernel(
-    own, w_query, w_key, w_value, w_gate, w_up, out, w_qkv, w_ff,
-    own_qkv, own_ff, sends, recvs, local, w_sends, w_recvs, w_local,
+    own, w_query, w_key, w_value, out, w_qkv,
+    staged, sends, recvs, local, w_sends, w_recvs, w_local,
 ):
-    me = lax.axis_index("fsdp")
-    core, x_bit, y_bit = lax.rem(me, 2), lax.rem(me // 2, 2), me // 4
-    shard = w_query.shape[0]
-    piece = w_ff.shape[1]
-    rows = pl.ds(pl.multiple_of(me * shard, shard), shard)
-    part = pl.ds(pl.multiple_of(lax.axis_index("rep") * piece, piece), piece)
-    pairs = []
-    at = 0
-    for weight in (w_query, w_key, w_value):
-        cols = weight.shape[1] // 8
-        pairs.append((weight, slice(None), cols, w_qkv.at[rows, at : at + cols], own_qkv, at))
-        at += cols
-    at = 0
-    for weight in (w_gate, w_up):
-        cols = weight.shape[1] // 8
-        pairs.append((weight, part, cols, w_ff.at[me, :, at : at + cols], own_ff, at))
-        at += cols
-
-    def source(pair, device):
-        weight, taken, cols = pair[:3]
-        return weight.at[taken, pl.ds(pl.multiple_of(device * cols, cols), cols)]
-
-    peers = []
-    for flip in (6, 2, 4, 7, 3, 5, 1):
-        bits = [
-            1 - bit if flip >> place & 1 else bit
-            for place, bit in enumerate((core, x_bit, y_bit))
-        ]
-        peers.append((flip - 1, bits[0] + 2 * bits[1] + 4 * bits[2]))
-    into = [
-        pltpu.make_async_copy(
-            source(pair, me), pair[4].at[:, pair[5] : pair[5] + pair[2]], w_local.at[index]
-        )
-        for index, pair in enumerate(pairs)
+    columns = Columns(
+        (w_query, w_key, w_value), slice(None), w_qkv, staged, w_sends, w_recvs, w_local
+    )
+    columns.stage()
+    greet([device for _, device in columns.peers])
+    exchange_rows(own, out, sends, recvs, local, columns.send)
+    columns.finish()
+
+
+def columns_specs(weights, rows):
+    cols = sum(w.shape[1] for w in weights) // 8
+    count = len(weights)
+    scratch = [
+        pltpu.VMEM((rows, cols), BF16),
+        pltpu.SemaphoreType.DMA((7, count)),
+        pltpu.SemaphoreType.DMA((7, count)),
+        pltpu.SemaphoreType.DMA((count,)),
     ]
-    for made in into:
-        made.start()
-    greet([device for _, device in peers])
-    copies = []
-
-    def between():
-        for chosen in ((0, 1, 2), (3, 4)):
-            for slot, device in peers:
-                for index in chosen:
-                    copies.append(
-                        send(
-                            source(pairs[index], device),
-                            pairs[index][3],
-                            w_sends.at[slot, index],
-                            w_recvs.at[slot, index],
-                            device,
-                        )
-                    )
-
-    exchange_rows(own, out, sends, recvs, local, between)
-    for made in into:
-        made.wait()
-    home = [
-        pltpu.make_async_copy(own_qkv, w_qkv.at[rows, :], w_local.at[0]),
-        pltpu.make_async_copy(own_ff, w_ff.at[me], w_local.at[1]),
-    ]
-    for made in home:
-        made.start()
-    for made in copies:
-        made.wait_recv()
-    for made in copies:
-        made.wait_send()
-    for made in home:
-        made.wait()
-
-
-def start(values, weights, replicas, ident):
-    rows, cols = values.shape
-    shard = weights[0].shape[0]
-    qkv_cols = sum(w.shape[1] for w in weights[:3]) // 8
-    ff_cols = sum(w.shape[1] for w in weights[3:]) // 8
+    return jax.ShapeDtypeStruct((8, rows, cols), BF16), scratch
+
+
+def send_columns(weights, rows, ident):
+    specs = [columns_specs((weight,), rows) for weight in weights]
     anywhere = pl.BlockSpec(memory_space=pl.ANY)
     return pl.pallas_call(
+        columns_kernel,
+        out_shape=[shape for shape, _ in specs],
+        in_specs=[anywhere] * len(weights),
+        out_specs=[anywhere] * len(weights),
+        scratch_shapes=sum([scratch for _, scratch in specs], []),
+        compiler_params=pltpu.CompilerParams(collective_id=ident, has_side_effects=True),
+        cost_estimate=pl.CostEstimate(
+            flops=0, bytes_accessed=rows * weights[0].shape[1] * 120, transcendentals=0
+        ),
+        name="send_columns",
+    )(*weights)
+
+
+def width_of(shape):
+    return shape.shape[-1]
+
+
+def start(values, weights, ident):
+    rows, cols = values.shape
+    shape, scratch = columns_specs(weights, weights[0].shape[0])
+    anywhere = pl.BlockSpec(memory_space=pl.ANY)
+    got, w_qkv = pl.pallas_call(
         start_kernel,
-        out_shape=(
-            jax.ShapeDtypeStruct((8, rows, cols), values.dtype),
-            jax.ShapeDtypeStruct((8 * shard, qkv_cols), BF16),
-            jax.ShapeDtypeStruct((8, shard // replicas, ff_cols), BF16),
-        ),
-        in_specs=[pl.BlockSpec(memory_space=pltpu.VMEM)] + [anywhere] * 5,
-        out_specs=(anywhere,) * 3,
+        out_shape=(jax.ShapeDtypeStruct((8, rows, cols), values.dtype), shape),
+        in_specs=[pl.BlockSpec(memory_space=pltpu.VMEM)] + [anywhere] * len(weights),
+        out_specs=(anywhere,) * 2,
         scratch_shapes=[
-            pltpu.VMEM((shard, qkv_cols), BF16),
-            pltpu.VMEM((shard // replicas, ff_cols), BF16),
+            scratch[0],
             pltpu.SemaphoreType.DMA((10,)),
             pltpu.SemaphoreType.DMA((10,)),
             pltpu.SemaphoreType.DMA,
-            pltpu.SemaphoreType.DMA((7, 5)),
-            pltpu.SemaphoreType.DMA((7, 5)),
-            pltpu.SemaphoreType.DMA((5,)),
-        ],
+        ]
+        + scratch[1:],
         compiler_params=pltpu.CompilerParams(collective_id=ident, has_side_effects=True),
         cost_estimate=pl.CostEstimate(
-            flops=0, bytes_accessed=rows * cols * 360, transcendentals=0
+            flops=0, bytes_accessed=rows * cols * 300, transcendentals=0
         ),
         name="start",
     )(values, *weights)
+    return got, w_qkv.reshape(-1, width_of(shape))
 
 
 def scatter_kernel(parts, out, mine, other, first, second, send, recv, local):
@@ -548,6 +589,121 @@
     )(*tables, *arrays)
 
 
+def project_kernel(got, gain, weight, normed, raw):
+    rows = got[: normed.shape[0], :].astype(F32)
+    low = (rows * rms_scale(rows) * gain[...]).astype(BF16)
+    normed[...] = low
+    raw[...] = dot(low, weight[...])
+
+
+def project(got, gain, weight, in_rows):
+    groups, block, width = got.shape
+    cols = weight.shape[1]
+    return pl.pallas_call(
+        project_kernel,
+        out_shape=(
+            jax.ShapeDtypeStruct((groups * in_rows, width), BF16),
+            jax.ShapeDtypeStruct((groups * in_rows, cols), F32),
+        ),
+        grid=(groups,),
+        in_specs=[
+            pl.BlockSpec((None, block, width), lambda i: (i, 0, 0)),
+            pl.BlockSpec((1, width), lambda i: (0, 0)),
+            pl.BlockSpec((width, cols), lambda i: (0, 0)),
+        ],
+        out_specs=(
+            pl.BlockSpec((in_rows, width), lambda i: (i, 0)),
+            pl.BlockSpec((in_rows, cols), lambda i: (i, 0)),
+        ),
+        cost_estimate=pl.CostEstimate(
+            flops=2 * groups * in_rows * width * cols,
+            bytes_accessed=4 * got.size,
+            transcendentals=0,
+        ),
+        name="project",
+    )(got, gain[None], weight)
+
+
+def feed_forward_kernel(rows, grads, w_gate, w_up, w_down, activ, grad_in):
+    cols = activ.shape[1]
+    step = cols // 3
+    for at in range(0, cols, step):
+        gate = dot(rows[...], w_gate[:, at : at + step])
+        up = dot(rows[...], w_up[:, at : at + step])
+        grad = dot_bt(grads[...], w_down[at : at + step, :])
+        sigmoid = jax.nn.sigmoid(gate)
+        silu = gate * sigmoid
+        activ[:, at : at + step] = (silu * up).astype(BF16)
+        grad_in[:, at : at + step] = (
+            grad * up * sigmoid * (1.0 + gate * (1.0 - sigmoid))
+        ).astype(BF16)
+        grad_in[:, cols + at : cols + at + step] = (grad * silu).astype(BF16)
+
+
+def feed_forward(rows, grads, w_gate, w_up, w_down, block):
+    total, width = rows.shape
+    cols = w_down.shape[0]
+    row_spec = pl.BlockSpec((block, width), lambda i: (i, 0))
+    return pl.pallas_call(
+        feed_forward_kernel,
+        out_shape=(
+            jax.ShapeDtypeStruct((total, cols), BF16),
+            jax.ShapeDtypeStruct((total, 2 * cols), BF16),
+        ),
+        grid=(total // block,),
+        in_specs=[
+            row_spec,
+            row_spec,
+            pl.BlockSpec(w_gate.shape, lambda i: (0, 0), pipeline_mode=pl.Buffered(1)),
+            pl.BlockSpec(w_up.shape, lambda i: (0, 0), pipeline_mode=pl.Buffered(1)),
+            pl.BlockSpec(w_down.shape, lambda i: (0, 0), pipeline_mode=pl.Buffered(1)),
+        ],
+        out_specs=(
+            pl.BlockSpec((block, cols), lambda i: (i, 0)),
+            pl.BlockSpec((block, 2 * cols), lambda i: (i, 0)),
+        ),
+        compiler_params=pltpu.CompilerParams(vmem_limit_bytes=48 << 20),
+        cost_estimate=pl.CostEstimate(
+            flops=6 * total * width * cols,
+            bytes_accessed=4 * rows.size + 6 * w_down.size,
+            transcendentals=total * cols,
+        ),
+        name="feed_forward",
+    )(rows, grads, w_gate, w_up, w_down)
+
+
+def input_grad_kernel(grads, w_gate, w_up, out):
+    cols = w_gate.shape[1]
+    gate, up = grads[:, :cols], grads[:, cols:]
+    step = 512
+    for at in range(0, out.shape[1], step):
+        rows = slice(at, at + step)
+        out[:, rows] = (dot_bt(gate, w_gate[rows, :]) + dot_bt(up, w_up[rows, :])).astype(BF16)
+
+
+def input_grad_of(grads, w_gate, w_up, block):
+    total, cols = grads.shape
+    width = w_gate.shape[0]
+    return pl.pallas_call(
+        input_grad_kernel,
+        out_shape=jax.ShapeDtypeStruct((total, width), BF16),
+        grid=(total // block,),
+        in_specs=[
+            pl.BlockSpec((block, cols), lambda i: (i, 0)),
+            pl.BlockSpec(w_gate.shape, lambda i: (0, 0), pipeline_mode=pl.Buffered(1)),
+            pl.BlockSpec(w_up.shape, lambda i: (0, 0), pipeline_mode=pl.Buffered(1)),
+        ],
+        out_specs=pl.BlockSpec((block, width), lambda i: (i, 0)),
+        compiler_params=pltpu.CompilerParams(vmem_limit_bytes=48 << 20),
+        cost_estimate=pl.CostEstimate(
+            flops=2 * total * width * cols,
+            bytes_accessed=2 * grads.size + 2 * total * width + 4 * w_gate.size,
+            transcendentals=0,
+        ),
+        name="input_grad",
+    )(grads, w_gate, w_up)
+
+
 def on_device(
     tokens,
     cotangent,
@@ -604,12 +760,9 @@
     gain_row = jnp.pad(gain_row[None], ((0, 15), (0, width - gain_row.shape[0])))
     start_rows = jnp.concatenate([tokens, gain_row])
     if groups == 8:
-        got, w_qkv, w_ff = start(
-            start_rows,
-            (w_query, key_projection, value_projection, w_gate, w_up),
-            replicas,
-            2,
-        )
+        w_ff = send_columns((w_gate, w_up), shard // replicas, 3)
+        start_rows, w_ff = lax.optimization_barrier((start_rows, w_ff))
+        got, w_qkv = start(start_rows, (w_query, key_projection, value_projection), 2)
     else:
         got = gather(start_rows)
         kv_shape = (shard, KEY_VALUE_HEADS // kv_heads, kv_cols)
@@ -629,11 +782,16 @@
         )
         w_ff = lax.all_to_all(send_ff, "fsdp", split_axis=1, concat_axis=0, tiled=False)
         w_ff = w_ff.reshape(groups, piece, 2 * ff_cols)
+        w_ff = (w_ff[:, :, :ff_cols], w_ff[:, :, ff_cols:])
     got = got.reshape(groups, in_rows + 16, width)
     got, cotangent_late = lax.optimization_barrier((got, cotangent))
     all_grads = lax.all_gather(cotangent_late, "fsdp", axis=0, tiled=True)
-    w_ff = lax.all_gather(w_ff, "rep", axis=1, tiled=True).reshape(width, 2 * ff_cols)
-    all_tokens = got[:, :in_rows].reshape(groups * in_rows, width)
+
+    def weight_columns(part):
+        return lax.all_gather(part, "rep", axis=1, tiled=True).reshape(width, ff_cols)
+
+    gate_cols = weight_columns(w_ff[0])
+    up_cols = weight_columns(w_ff[1])
     gains = got[:, in_rows].astype(F32)
     gain_one = gains[:, :shard].reshape(width)
     gain_two = gains[:, shard : 2 * shard].reshape(width)
@@ -650,9 +808,7 @@
     resid = tokens.astype(F32)
     scale_one = rms_scale(resid)
     normed_one = resid * scale_one
-    all_resid = all_tokens.astype(F32)
-    attention_input = (all_resid * rms_scale(all_resid) * gain_one).astype(BF16)
-    raw = dot(attention_input, w_qkv)
+    attention_input, raw = project(got, gain_one, w_qkv, in_rows)
     inverse = ROPE_BASE ** (-jnp.arange(0, HEAD_SIZE, 2, dtype=F32) / HEAD_SIZE)
     angles = jnp.arange(KEY_SPAN, dtype=F32)[:, None] * inverse
     cosine, sine = jnp.cos(angles), jnp.sin(angles)
@@ -677,31 +833,21 @@
     scale_two = rms_scale(hidden_one)
     normed_two = hidden_one * scale_two
     mlp_in = gather((normed_two * gain_two).astype(BF16))
-    gate_pre = dot(mlp_in, w_ff[:, :ff_cols])
-    up_pre = dot(mlp_in, w_ff[:, ff_cols:])
-    sigmoid_gate = jax.nn.sigmoid(gate_pre)
-    activ = (gate_pre * sigmoid_gate * up_pre).astype(BF16)
-
-    grad_activ = dot_bt(all_grads, w_down)
-    grad_gate = (
-        grad_activ * up_pre * sigmoid_gate * (1.0 + gate_pre * (1.0 - sigmoid_gate))
-    ).astype(BF16)
-    grad_up = (grad_activ * (gate_pre * sigmoid_gate)).astype(BF16)
-    grad_ff = jnp.concatenate([grad_gate, grad_up], axis=1)
+    activ, grad_ff = feed_forward(mlp_in, all_grads, gate_cols, up_cols, w_down, in_rows)
+
     down_term = dot_at(activ, all_grads).astype(BF16)
     grad_ff, down_term = lax.optimization_barrier((grad_ff, down_term))
     down_part = replica_scatter(down_term, 0)
     ff_term = dot_at(mlp_in, grad_ff).astype(BF16)
     grad_ff, ff_term = lax.optimization_barrier((grad_ff, ff_term))
     ff_part = replica_scatter(ff_term.reshape(groups, shard, 2 * ff_cols), 1)
-    grad_mlp_in = scatter_sum(dot_bt(grad_ff, w_ff))
+    grad_mlp_in = scatter_sum(input_grad_of(grad_ff, gate_cols, up_cols, in_rows))
     grad_norm_two = norm_back(grad_mlp_in, normed_two, scale_two, gain_two)
     grad_hidden = cotangent.astype(F32) + grad_norm_two
 
     all_hidden = gather(grad_hidden.astype(BF16))
     out_term = dot_at(context, all_hidden).astype(BF16)
     all_hidden, out_term = lax.optimization_barrier((all_hidden, out_term))
-    out_part = replica_scatter(out_term, 0)
     grad_qkv, head_terms = call_attention(
         attention_back_kernel,
         tables,
@@ -728,8 +874,13 @@
 
     small_term = qkv_term
     grad_qkv, small_term, ff_part = lax.optimization_barrier((grad_qkv, small_term, ff_part))
-    small_cols = small_term.shape[1]
-    small_part = replica_scatter(small_term.reshape(groups, shard, small_cols), 1)
+    piece = shard // replicas
+    small_term = small_term.reshape(groups, replicas, piece, qkv_cols)
+    lane = math.gcd(qkv_cols, width)
+    small_term = jnp.swapaxes(small_term, 0, 1).reshape(replicas, -1, lane)
+    small_rows = small_term.shape[1]
+    rest_term = jnp.concatenate([small_term, out_term.reshape(replicas, -1, lane)], axis=1)
+    rest_part = lax.psum_scatter(rest_term, "rep", scatter_dimension=0, tiled=False)
     ff_full = columns_home(ff_part)
     grad_attn_in = scatter_sum(dot_bt(grad_qkv, w_qkv))
     grad_norm_one = norm_back(grad_attn_in, normed_one, scale_one, gain_one)
@@ -737,10 +888,15 @@
     activ, grad_attn_in = lax.optimization_barrier((activ, grad_attn_in))
     last_sum = scatter_sum(dot(activ, w_down))
     output = (hidden_one + last_sum).astype(BF16)
-    small_part, last_sum = lax.optimization_barrier((small_part, last_sum))
-    small_full = columns_home(small_part)
+    rest_part, last_sum = lax.optimization_barrier((rest_part, last_sum))
+    small_home = lax.all_to_all(
+        rest_part[:small_rows].reshape(groups, piece, qkv_cols),
+        "fsdp", split_axis=0, concat_axis=0, tiled=True,
+    ).reshape(small_rows, lane)
     down_full = replica_gather(down_part)
-    out_full = replica_gather(out_part)
+    rest_full = replica_gather(jnp.concatenate([small_home, rest_part[small_rows:]]))
+    small_full = rest_full[:, :small_rows].reshape(replicas, groups, piece, qkv_cols)
+    out_full = rest_full[:, small_rows:]
 
     gate_share, up_share = place_columns(ff_full, (ff_cols, ff_cols), (1, 1))
     query_share, key_share, value_share = place_columns(
@@ -748,7 +904,8 @@
     )
     gain_terms = (
         gain_column(w_qkv, qkv_term, gain_one),
-        gain_column(w_ff, ff_term, gain_two),
+        gain_column(gate_cols, ff_term[:, :ff_cols], gain_two)
+        + gain_column(up_cols, ff_term[:, ff_cols:], gain_two),
         head_terms[0],
         head_terms[1],
     )

time: 858 us -> 812 us (0.946)
  Pallas kernels: 394 us -> 468 us
  matrix products: 139 us -> 75.4 us
  other arithmetic: 65 us -> 32.4 us
  waiting for transfers between devices: 146 us -> 121 us
  blocking collectives: 82.6 us -> 69.2 us
  local copies, waits for them, and re-layouts: 11.1 us -> 24.2 us
    pallas_call x0 -> x4, Pallas kernels: none -> 78.2 us  [the longest x1 25.2 us: feed_forward(): pl.pallas_call(feed_forward_kernel, out_shape=(jax.ShapeDtypeStruct((tota...]
    dot_general x5 -> x2, matrix products: 50.5 us -> 16.4 us  [dot(): return jnp.dot(left, right, preferred_element_type=F32)]
    reduce_scatter x4 -> x2, waiting for transfers between devices: 40.2 us -> 9.28 us  [replica_scatter(): return lax.psum_scatter(term, 'rep', scatter_dimension=axis, tiled=True)]
    dot_general x4 -> x2, matrix products: 44.4 us -> 13.5 us  [dot_bt(): lax.dot_general(left, right, (((1,), (1,)), ((), ())), preferred_element_...]
    pallas_call x1, Pallas kernels: 80.4 us -> 61.6 us  [start(): pl.pallas_call(start_kernel, out_shape=(jax.ShapeDtypeStruct((8, rows, co...]
    convert_element_type x2 -> x0, other arithmetic: 17.7 us -> none  [the longest x1 10.7 us: on_device(): all_resid = all_tokens.astype(F32)]
    all_to_all x2 -> x1, blocking collectives: 39.1 us -> 25.4 us  [columns_home(): part = lax.all_to_all(part, 'fsdp', split_axis=0, concat_axis=0, tiled=True)]
    all_gather x1, waiting for transfers between devices: 9.46 us -> 0.02 us  [on_device(): all_grads = lax.all_gather(cotangent_late, 'fsdp', axis=0, tiled=True)]
  transfers between devices with their start and end apart: 10 -> 10, of which waited for: 3 -> 4; matrix products, arithmetic and copies ran while one was open for 17% -> 10% of each run, Pallas kernels for 36% -> 51%
where the time goes in v4:
time: 812 us; the launch traced here: 808 us
  Pallas kernels  468 us (58%)
  waiting for transfers between devices  121 us (15%)
  matrix products  75.4 us (9%)
  blocking collectives  69.2 us (9%)
  other arithmetic  32.4 us (4%)
  local copies, waits for them, and re-layouts  24.2 us (3%)
  between operations  14.6 us (2%)
    pallas_call x4, Pallas kernels, scatter_rows(): pl.pallas_call(scatter_kernel, out_shape=jax.ShapeDtypeStruct((rows, cols...  164 us
    all_gather x3, waiting for transfers between devices, replica_gather(): return lax.all_gather(part, 'rep', axis=0, tiled=False)  101 us
    pallas_call x2, Pallas kernels, gather_rows(): pl.pallas_call(gather_kernel, out_shape=jax.ShapeDtypeStruct((8, rows, co...  97.1 us
    pallas_call x1, Pallas kernels, start(): pl.pallas_call(start_kernel, out_shape=(jax.ShapeDtypeStruct((8, rows, co...  61.6 us
    pallas_call x2, Pallas kernels, call_attention(): pl.pallas_call(functools.partial(kernel, in_rows, cap), out_shape=outs, i...  55.4 us
    dot_general x4, matrix products, dot_at(): lax.dot_general(left, right, (((0,), (0,)), ((), ())), preferred_element_...  45.6 us
    psum x1, blocking collectives, on_device(): gain_sums = lax.psum(gain_terms, ('rep', 'fsdp'))  43.9 us
    all_to_all x1, blocking collectives, columns_home(): part = lax.all_to_all(part, 'fsdp', split_axis=0, concat_axis=0, tiled=True)  25.4 us
  transfers between devices with their start and end apart: 10, of which 4 were waited for; matrix products, arithmetic and copies ran while one was open for 10% of the time, Pallas kernels for 51%

profile of v4, /device:TPU:0, one launch (start us, length us, event | category | flops | bytes accessed | tf_op | source)
XLA Modules:
  0.0 808.1 jit_solution(16485929104409316923)
XLA Ops:
  8.1 2.3 fusion.9.own
  10.4 22.8 %send_columns.1 = (bf16[8,64,768]{2,1,0:T(8,128)(2,1)}, bf16[8,64,768]{2,1,0:T(8,128)(2,1)}) custom-call(bf16[256,6144]{1,0:T(8,128)(2,1)} %w_gate.1, bf16[256,6144]{1,0:T(8,128)(2,1)} %w_up.1), custom_call_target="tpu_custom_call" | custom-call | bytes 47185920 | tf_op jit(solution)/shard_map/send_columns/pallas_call | solution.py:245
  34.1 61.6 %start.1 = (bf16[8,256,2048]{2,1,0:T(8,128)(2,1)}, bf16[8,256,512]{2,1,0:T(8,128)(2,1)}) custom-call(bf16[256,2048]{1,0:T(8,128)(2,1)} %fusion.9.own, bf16[256,2048]{1,0:T(8,128)(2,1)} %w_query.1, bf16[256,1024]{1,0:T(8,128)(2,1)} %w_key.1, bf16[256,1024]{1,0:T(8,128)(2,1)} %w_value.1), custom_call_target="tpu_custom_call" | custom-call | bytes 157286400 | tf_op jit(solution)/shard_map/start/pallas_call | solution.py:267
  98.8 12.4 %project.1 = (bf16[1920,2048]{1,0:T(8,128)(2,1)}, f32[1920,512]{1,0:T(8,128)}) custom-call(bf16[8,256,2048]{2,1,0:T(8,128)(2,1)} %get-tuple-element.48.got, f32[1,2048]{1,0:T(1,128)} %bitcast.99, bf16[2048,512]{1,0:T(8,128)(2,1)} %bitcast.100), custom_call_target="tpu_custom_call" | custom-call | flops 4026531840 | bytes 16777216 | tf_op jit(solution)/shard_map/project/pallas_call | solution.py:602
  111.2 2.1 copy-done.1
  113.4 22.3 %shard_map.237 = bf16[1920,256]{1,0:T(8,128)(2,1)S(1)} custom-call(s32[8,8]{1,0:T(8,128)S(1)} %get-tuple-element.93.starts, s32[8,8]{1,0:T(8,128)S(1)} %get-tuple-element.92.places, s32[8,8]{1,0:T(8,128)S(1)} %bitcast.67, f32[1920,512]{1,0:T(8,128)S(1)} %copy-done.1, f32[2,128]{1,0:T(2,128)S(1)} %pad_maximum_fusion.5.gains, ...), custom_call_target="tpu_custom_call" | custom-call | flops 679477248 | bytes 4326400 | tf_op jit(solution)/shard_map/pallas_call | solution.py:581
  135.7 5.3 convolution_convert_fusion.2
  141.0 46.7 %scatter_rows.4 = f32[240,2048]{1,0:T(8,128)} custom-call(bf16[8,240,2048]{2,1,0:T(8,128)(2,1)} %bitcast.71), custom_call_target="tpu_custom_call" | custom-call | bytes 98304000 | tf_op jit(solution)/shard_map/scatter_rows/pallas_call | solution.py:365
  187.8 2.0 multiply_reduce_fusion.4
  191.2 58.9 %gather_rows.2 = bf16[8,240,2048]{2,1,0:T(8,128)(2,1)} custom-call(bf16[240,2048]{1,0:T(8,128)(2,1)} %multiply_convert_fusion.own), custom_call_target="tpu_custom_call" | custom-call | bytes 88473600 | tf_op jit(solution)/shard_map/gather_rows/pallas_call | solution.py:122
  250.2 1.9 copy-done.2
  252.1 25.2 %feed_forward.1 = (bf16[1920,768]{1,0:T(8,128)(2,1)S(1)}, bf16[1920,1536]{1,0:T(8,128)(2,1)}) custom-call(bf16[1920,2048]{1,0:T(8,128)(2,1)} %bitcast.78, bf16[1920,2048]{1,0:T(8,128)(2,1)} %all-gather.10.cloned.1.call-done.grads, bf16[2048,768]{1,0:T(8,128)(2,1)S(1)} %bitcast.63, bf16[2048,768]{1,0:T(8,128)(2,1)} %bitcast.83, bf16[768,2048]{1,0:T(8,128)(2,1)} %w_down.1), custom_call_target="tpu_custom_call" | custom-call | flops 18119393280 | bytes 25165824 | tf_op jit(solution)/shard_map/feed_forward/pallas_call | solution.py:647
  277.3 1.6 copy-done.7
  278.8 10.3 %convolution_convert_fusion.4 = bf16[768,2048]{1,0:T(8,128)(2,1)} fusion(bf16[1920,768]{1,0:T(8,128)(2,1)S(1)} %get-tuple-element.63, bf16[1920,2048]{1,0:T(8,128)(2,1)} %all-gather.10.cloned.1.call-done.grads), kind=kOutput, calls=%fused_computation.7 | convolution fusion | flops 6041370624 | bytes 13959168 | tf_op jit(solution)/shard_map/dot_general | solution.py:38
  289.1 19.1 %convolution_convert_fusion.3 = bf16[2048,1536]{1,0:T(8,128)(2,1)} fusion(bf16[1920,2048]{1,0:T(8,128)(2,1)} %bitcast.79, bf16[1920,1536]{1,0:T(8,128)(2,1)} %get-tuple-element.57.grads), kind=kOutput, calls=%fused_computation.3 | convolution fusion | flops 12082741248 | bytes 20054016 | tf_op jit(solution)/shard_map/dot_general | solution.py:38
  308.8 1.9 copy-done.3
  310.7 17.7 %input_grad.1 = bf16[1920,2048]{1,0:T(8,128)(2,1)} custom-call(bf16[1920,1536]{1,0:T(8,128)(2,1)} %get-tuple-element.57.grads, bf16[2048,768]{1,0:T(8,128)(2,1)S(1)} %bitcast.64, bf16[2048,768]{1,0:T(8,128)(2,1)} %bitcast.84), custom_call_target="tpu_custom_call" | custom-call | flops 12079595520 | bytes 20054016 | tf_op jit(solution)/shard_map/input_grad/pallas_call | solution.py:687
  328.4 39.5 %scatter_rows.5 = f32[240,2048]{1,0:T(8,128)} custom-call(bf16[8,240,2048]{2,1,0:T(8,128)(2,1)} %bitcast.76), custom_call_target="tpu_custom_call" | custom-call | bytes 98304000 | tf_op jit(solution)/shard_map/scatter_rows/pallas_call | solution.py:365
  368.0 2.9 fusion.8
  371.5 1.7 fusion.13.own
  373.2 38.2 %gather_rows.3 = bf16[8,240,2048]{2,1,0:T(8,128)(2,1)} custom-call(bf16[240,2048]{1,0:T(8,128)(2,1)} %fusion.13.own), custom_call_target="tpu_custom_call" | custom-call | bytes 88473600 | tf_op jit(solution)/shard_map/gather_rows/pallas_call | solution.py:122
  411.3 6.6 convolution_convert_fusion.6
  417.9 1.7 reshape.129
  419.6 5.5 fusion.17.grads
  425.1 33.1 %shard_map.238 = (bf16[1920,512]{1,0:T(8,128)(2,1)S(1)}, f32[8,128]{1,0:T(8,128)S(1)}) custom-call(s32[8,8]{1,0:T(8,128)S(1)} %get-tuple-element.93.starts, s32[8,8]{1,0:T(8,128)S(1)} %get-tuple-element.92.places, s32[8,8]{1,0:T(8,128)S(1)} %bitcast.68, f32[1920,512]{1,0:T(8,128)} %get-tuple-element.50.raw, f32[1920,256]{1,0:T(8,128)S(1)} %fusion.17.grads, ...), custom_call_target="tpu_custom_call" | custom-call | flops 1698693120 | bytes 6292480 | tf_op jit(solution)/shard_map/pallas_call | solution.py:581
  459.5 9.7 %multiply_reduce_fusion.2 = (f32[2048]{0:T(1024)S(1)}, bf16[2048,512]{1,0:T(8,128)(2,1)}) fusion(bf16[8,256,512]{2,1,0:T(8,128)(2,1)S(1)} %copy-done.19, bf16[1920,2048]{1,0:T(8,128)(2,1)} %get-tuple-element.60, bf16[1920,512]{1,0:T(8,128)(2,1)S(1)} %get-tuple-element.62), kind=kOutput, calls=%fused_computation.6 | convolution fusion | flops 4031772672 | bytes 14032896 | tf_op jit(solution)/shard_map/dot_general | solution.py:38
  469.1 1.8 copy.31
  471.0 1.9 pad_maximum_fusion
  472.9 9.3 %reduce-scatter.8.cloned.1.call-done = bf16[192,2048]{1,0:T(8,128)(2,1)} async-done(((bf16[768,2048]{1,0:T(8,128)(2,1)}), bf16[192,2048]{1,0:T(8,128)(2,1)}) %reduce-scatter.8.cloned.1.call-update) | async-done | bytes 786448 | tf_op jit(solution)/shard_map/reduce_scatter | solution.py:752
  482.3 25.4 %all_to_all.10 = bf16[8,64,1536]{2,1,0:T(8,128)(2,1)} all-to-all(bf16[8,64,1536]{2,1,0:T(8,128)(2,1)} %reduce-scatter.4.cloned.1.call-done), channel_id=1, replica_groups=mesh['rep'=4,'fsdp'=8] {'fsdp'}, dimensions={0} | all-to-all | bytes 3145728 | tf_op jit(solution)/shard_map/all_to_all | solution.py:755
  507.7 8.0 convolution_convert_fusion.1
  515.7 38.0 %scatter_rows.6 = f32[240,2048]{1,0:T(8,128)} custom-call(bf16[8,240,2048]{2,1,0:T(8,128)(2,1)} %bitcast.75), custom_call_target="tpu_custom_call" | custom-call | bytes 98304000 | tf_op jit(solution)/shard_map/scatter_rows/pallas_call | solution.py:365
  553.7 11.1 %convolution_convert_fusion = bf16[1920,2048]{1,0:T(8,128)(2,1)} fusion(bf16[1920,768]{1,0:T(8,128)(2,1)} %copy-done.7, bf16[768,2048]{1,0:T(8,128)(2,1)} %w_down.1), kind=kOutput, calls=%fused_computation | convolution fusion | flops 6043729920 | bytes 13959168 | tf_op jit(solution)/shard_map/dot_general | solution.py:30
  564.7 39.5 %scatter_rows.7 = f32[240,2048]{1,0:T(8,128)} custom-call(bf16[8,240,2048]{2,1,0:T(8,128)(2,1)} %bitcast.77), custom_call_target="tpu_custom_call" | custom-call | bytes 98304000 | tf_op jit(solution)/shard_map/scatter_rows/pallas_call | solution.py:365
  604.3 1.9 slice.48
  606.2 3.5 all-to-all-start
  610.7 8.6 %all-to-all-done = bf16[8,64,512]{2,1,0:T(8,128)(2,1)S(1)} async-done(((bf16[8,64,512]{2,1,0:T(8,128)(2,1)}), bf16[8,64,512]{2,1,0:T(8,128)(2,1)S(1)}, u32[]{:S(2)}, u32[]{:S(2)}) %all-to-all-start) | async-done | bytes 524320 | tf_op jit(solution)/shard_map/all_to_all | solution.py:892
  620.3 6.0 multiply_reduce_fusion.1
  626.3 43.9 %psum.7 = f32[4352]{0:T(1024)S(1)} all-reduce(f32[4352]{0:T(1024)S(1)} %pad_maximum_fusion.3), channel_id=1, replica_groups=mesh['rep'=4,'fsdp'=8] {'rep','fsdp'}, use_global_device_ids=true, to_apply=%region_10.11 | all-reduce | flops 4352 | bytes 34816 | tf_op jit(solution)/shard_map/psum | solution.py:913
  671.5 5.6 convert_element_type.105
  678.9 2.8 fusion.7
  681.7 45.1 %all-gather.18.cloned.1.call-done = bf16[32,64,1536]{2,1,0:T(8,128)(2,1)} async-done(((bf16[8,64,1536]{2,1,0:T(8,128)(2,1)}), bf16[32,64,1536]{2,1,0:T(8,128)(2,1)}) %all-gather.18.cloned.1.call-update) | async-done | bytes 6291472 | tf_op jit(solution)/shard_map/all_gather | solution.py:737
  726.9 7.7 place_columns.3
  734.6 56.1 %all-gather.16.cloned.1.call-done = bf16[3072,512]{1,0:T(8,128)(2,1)} async-done(((bf16[768,512]{1,0:T(8,128)(2,1)}), bf16[3072,512]{1,0:T(8,128)(2,1)}) %all-gather.16.cloned.1.call-update) | async-done | bytes 3145744 | tf_op jit(solution)/shard_map/all_gather | solution.py:737
  790.7 3.0 slice.56
  793.7 1.5 slice_convert_fusion
  795.2 4.1 place_columns.2
  799.4 1.9 reshape.134
  (93 shorter events, 13.9 us)
Async XLA Ops:
  7.2 128.5 %copy-start = (bf16[256,2048]{1,0:T(8,128)(2,1)S(1)}, bf16[256,2048]{1,0:T(8,128)(2,1)}, u32[]{:S(2)}) copy-start(bf16[256,2048]{1,0:T(8,128)(2,1)} %param.25) | copy-start | bytes 3145732
  7.2 242.9 %all-gather.12.cloned.1.call-start = ((), (), s32[]{:S(2)}) async-start(), calls=%async_computation.6 | async-start | bytes 3932160 | tf_op jit(solution)/shard_map/all_gather | solution.py:791
  33.3 216.9 %all-gather.14.cloned.1.call-start = ((), (), s32[]{:S(2)}) async-start(), calls=%async_computation.7 | async-start | bytes 3932160 | tf_op jit(solution)/shard_map/all_gather | solution.py:791
  34.0 61.7 %copy-start.4 = (s32[1,8,8]{2,1,0:T(8,128)S(1)}, s32[1,8,8]{2,1,0:T(8,128)}, u32[]{:S(2)}) copy-start(s32[1,8,8]{2,1,0:T(8,128)} %param.18) | copy-start | bytes 772
  34.0 216.2 %all-gather.10.cloned.1.call-start = ((), (), s32[]{:S(2)}) async-start(), calls=%async_computation.5 | async-start | bytes 8847360 | tf_op jit(solution)/shard_map/all_gather | solution.py:788
  95.7 373.5 %reduce-scatter.4.cloned.1.call-start = ((), (), s32[]{:S(2)}) async-start(), calls=%async_computation.8 | async-start | bytes 7864320 | tf_op jit(solution)/shard_map/reduce_scatter | solution.py:752
  111.2 2.1 copy-start.1
  141.0 46.8 %copy-start.11 = (bf16[240,2048]{1,0:T(8,128)(2,1)S(1)}, bf16[240,2048]{1,0:T(8,128)(2,1)}, u32[]{:S(2)}) copy-start(bf16[240,2048]{1,0:T(8,128)(2,1)} %param.16) | copy-start | bytes 2949124
  187.7 2.1 copy-start.8
  250.2 1.9 copy-start.2
  277.3 1.6 copy-start.7
  308.2 174.0 %reduce-scatter.8.cloned.1.call-start = ((), (), s32[]{:S(2)}) async-start(), calls=%async_computation.10 | async-start | bytes 3932160 | tf_op jit(solution)/shard_map/reduce_scatter | solution.py:752
  308.8 295.5 %reduce-scatter.6.cloned.1.call-start = ((), (), s32[]{:S(2)}) async-start(), calls=%async_computation.9 | async-start | bytes 3932160 | tf_op jit(solution)/shard_map/reduce_scatter | solution.py:883
  308.8 1.9 copy-start.3
  367.9 3.0 copy-start.9
  367.9 3.3 copy-start.13
  368.0 3.5 copy-start.16
  425.1 34.3 %copy-start.19 = (bf16[8,256,512]{2,1,0:T(8,128)(2,1)S(1)}, bf16[8,256,512]{2,1,0:T(8,128)(2,1)}, u32[]{:S(2)}) copy-start(bf16[8,256,512]{2,1,0:T(8,128)(2,1)} %get-tuple-element.49) | copy-start | bytes 6291460
  458.2 1.3 copy-start.5
  472.9 198.6 %all-gather.20.cloned.1.call-start = ((), (), s32[]{:S(2)}) async-start(), calls=%async_computation.13 | async-start | bytes 3932160 | tf_op jit(solution)/shard_map/all_gather | solution.py:737
  482.2 25.5 %copy-start.6 = (bf16[1920,512]{1,0:T(8,128)(2,1)S(1)}, bf16[1920,512]{1,0:T(8,128)(2,1)}, u32[]{:S(2)}) copy-start(bf16[1920,512]{1,0:T(8,128)(2,1)} %copy-done.5) | copy-start | bytes 5898244
  482.2 244.6 %all-gather.18.cloned.1.call-start = ((), (), s32[]{:S(2)}) async-start(), calls=%async_computation.12 | async-start | bytes 7864320 | tf_op jit(solution)/shard_map/all_gather | solution.py:737
  606.2 13.2 %all-to-all-start = ((bf16[8,64,512]{2,1,0:T(8,128)(2,1)}), bf16[8,64,512]{2,1,0:T(8,128)(2,1)S(1)}, u32[]{:S(2)}, u32[]{:S(2)}) async-start(bf16[8,64,512]{2,1,0:T(8,128)(2,1)} %bitcast.19), calls=%async_computation.2 | async-start | bytes 1048576 | tf_op jit(solution)/shard_map/all_to_all | solution.py:892
  609.7 181.0 %all-gather.16.cloned.1.call-start = ((), (), s32[]{:S(2)}) async-start(), calls=%async_computation.11 | async-start | bytes 3932160 | tf_op jit(solution)/shard_map/all_gather | solution.py:737
  671.4 5.7 copy-start.12
  671.5 5.6 copy-start.15
  671.5 6.2 copy-start.14
  671.5 6.2 copy-start.18
  677.1 1.6 copy-start.10
  677.1 1.8 copy-start.17
Sparse Core Ops, SparseCore 0:
  33.4 63.7 all-gather.11
  98.7 62.0 all-gather.13
  162.7 78.8 all-gather.9
  308.3 110.7 reduce-scatter.3
  421.2 60.8 reduce-scatter.7
  484.9 60.3 reduce-scatter.5
  546.8 63.3 all-gather.19
  611.8 115.0 all-gather.17
  729.0 61.6 all-gather.15

commit v5 on v4

--- a/solution.py
+++ b/solution.py
@@ -474,7 +474,7 @@
     column = lax.broadcasted_iota(jnp.int32, scores.shape, 1)
     scores = jnp.where((column <= row) & (column < length), scores, NEG_LARGE)
     exps = jnp.exp(scores - jnp.max(scores, axis=-1, keepdims=True))
-    return exps / jnp.sum(exps, axis=-1, keepdims=True)
+    return exps * (1.0 / jnp.sum(exps, axis=-1, keepdims=True))
 
 
 def attention_kernel(in_rows, cap, starts, places, counts, raw, gains, trig, out, slot, result, packed):
@@ -833,7 +833,7 @@
     scale_two = rms_scale(hidden_one)
     normed_two = hidden_one * scale_two
     mlp_in = gather((normed_two * gain_two).astype(BF16))
-    activ, grad_ff = feed_forward(mlp_in, all_grads, gate_cols, up_cols, w_down, in_rows)
+    activ, grad_ff = feed_forward(mlp_in, all_grads, gate_cols, up_cols, w_down, 2 * in_rows)
 
     down_term = dot_at(activ, all_grads).astype(BF16)
     grad_ff, down_term = lax.optimization_barrier((grad_ff, down_term))
@@ -841,7 +841,7 @@
     ff_term = dot_at(mlp_in, grad_ff).astype(BF16)
     grad_ff, ff_term = lax.optimization_barrier((grad_ff, ff_term))
     ff_part = replica_scatter(ff_term.reshape(groups, shard, 2 * ff_cols), 1)
-    grad_mlp_in = scatter_sum(input_grad_of(grad_ff, gate_cols, up_cols, in_rows))
+    grad_mlp_in = scatter_sum(input_grad_of(grad_ff, gate_cols, up_cols, 2 * in_rows))
     grad_norm_two = norm_back(grad_mlp_in, normed_two, scale_two, gain_two)
     grad_hidden = cotangent.astype(F32) + grad_norm_two
 

time: 812 us -> 817 us (level)
  no operation moved by 1% of the time
where the time goes in v5:
time: 817 us; the launch traced here: 807 us
  Pallas kernels  466 us (57%)
  waiting for transfers between devices  121 us (15%)
  matrix products  75.7 us (9%)
  blocking collectives  69.2 us (8%)
  other arithmetic  32.4 us (4%)
  local copies, waits for them, and re-layouts  24.2 us (3%)
  between operations  14.8 us (2%)
    pallas_call x4, Pallas kernels, scatter_rows(): pl.pallas_call(scatter_kernel, out_shape=jax.ShapeDtypeStruct((rows, cols...  163 us
    all_gather x3, waiting for transfers between devices, replica_gather(): return lax.all_gather(part, 'rep', axis=0, tiled=False)  101 us
    pallas_call x2, Pallas kernels, gather_rows(): pl.pallas_call(gather_kernel, out_shape=jax.ShapeDtypeStruct((8, rows, co...  97.2 us
    pallas_call x1, Pallas kernels, start(): pl.pallas_call(start_kernel, out_shape=(jax.ShapeDtypeStruct((8, rows, co...  61.6 us
    pallas_call x2, Pallas kernels, call_attention(): pl.pallas_call(functools.partial(kernel, in_rows, cap), out_shape=outs, i...  55.4 us
    dot_general x4, matrix products, dot_at(): lax.dot_general(left, right, (((0,), (0,)), ((), ())), preferred_element_...  45.9 us
    psum x1, blocking collectives, on_device(): gain_sums = lax.psum(gain_terms, ('rep', 'fsdp'))  43.9 us
    all_to_all x1, blocking collectives, columns_home(): part = lax.all_to_all(part, 'fsdp', split_axis=0, concat_axis=0, tiled=True)  25.4 us
  transfers between devices with their start and end apart: 10, of which 4 were waited for; matrix products, arithmetic and copies ran while one was open for 10% of the time, Pallas kernels for 51%

profile of v5, /device:TPU:0, one launch (start us, length us, event | category | flops | bytes accessed | tf_op | source)
XLA Modules:
  0.0 807.1 jit_solution(12549548876118240893)
XLA Ops:
  8.1 2.3 fusion.9.own
  10.4 22.8 %send_columns.1 = (bf16[8,64,768]{2,1,0:T(8,128)(2,1)}, bf16[8,64,768]{2,1,0:T(8,128)(2,1)}) custom-call(bf16[256,6144]{1,0:T(8,128)(2,1)} %w_gate.1, bf16[256,6144]{1,0:T(8,128)(2,1)} %w_up.1), custom_call_target="tpu_custom_call" | custom-call | bytes 47185920 | tf_op jit(solution)/shard_map/send_columns/pallas_call | solution.py:245
  34.1 61.6 %start.1 = (bf16[8,256,2048]{2,1,0:T(8,128)(2,1)}, bf16[8,256,512]{2,1,0:T(8,128)(2,1)}) custom-call(bf16[256,2048]{1,0:T(8,128)(2,1)} %fusion.9.own, bf16[256,2048]{1,0:T(8,128)(2,1)} %w_query.1, bf16[256,1024]{1,0:T(8,128)(2,1)} %w_key.1, bf16[256,1024]{1,0:T(8,128)(2,1)} %w_value.1), custom_call_target="tpu_custom_call" | custom-call | bytes 157286400 | tf_op jit(solution)/shard_map/start/pallas_call | solution.py:267
  98.8 11.8 %project.1 = (bf16[1920,2048]{1,0:T(8,128)(2,1)}, f32[1920,512]{1,0:T(8,128)}) custom-call(bf16[8,256,2048]{2,1,0:T(8,128)(2,1)} %get-tuple-element.48.got, f32[1,2048]{1,0:T(1,128)} %bitcast.99, bf16[2048,512]{1,0:T(8,128)(2,1)} %bitcast.100), custom_call_target="tpu_custom_call" | custom-call | flops 4026531840 | bytes 16777216 | tf_op jit(solution)/shard_map/project/pallas_call | solution.py:602
  110.6 2.1 copy-done.1
  112.8 22.3 %shard_map.237 = bf16[1920,256]{1,0:T(8,128)(2,1)S(1)} custom-call(s32[8,8]{1,0:T(8,128)S(1)} %get-tuple-element.93.starts, s32[8,8]{1,0:T(8,128)S(1)} %get-tuple-element.92.places, s32[8,8]{1,0:T(8,128)S(1)} %bitcast.67, f32[1920,512]{1,0:T(8,128)S(1)} %copy-done.1, f32[2,128]{1,0:T(2,128)S(1)} %pad_maximum_fusion.5.gains, ...), custom_call_target="tpu_custom_call" | custom-call | flops 679477248 | bytes 4326400 | tf_op jit(solution)/shard_map/pallas_call | solution.py:581
  135.1 5.3 convolution_convert_fusion.2
  140.4 46.2 %scatter_rows.4 = f32[240,2048]{1,0:T(8,128)} custom-call(bf16[8,240,2048]{2,1,0:T(8,128)(2,1)} %bitcast.71), custom_call_target="tpu_custom_call" | custom-call | bytes 98304000 | tf_op jit(solution)/shard_map/scatter_rows/pallas_call | solution.py:365
  186.6 2.0 multiply_reduce_fusion.4
  190.0 59.0 %gather_rows.2 = bf16[8,240,2048]{2,1,0:T(8,128)(2,1)} custom-call(bf16[240,2048]{1,0:T(8,128)(2,1)} %multiply_convert_fusion.own), custom_call_target="tpu_custom_call" | custom-call | bytes 88473600 | tf_op jit(solution)/shard_map/gather_rows/pallas_call | solution.py:122
  249.1 1.9 copy-done.2
  251.0 24.9 %feed_forward.1 = (bf16[1920,768]{1,0:T(8,128)(2,1)S(1)}, bf16[1920,1536]{1,0:T(8,128)(2,1)}) custom-call(bf16[1920,2048]{1,0:T(8,128)(2,1)} %bitcast.78, bf16[1920,2048]{1,0:T(8,128)(2,1)} %all-gather.10.cloned.1.call-done.grads, bf16[2048,768]{1,0:T(8,128)(2,1)S(1)} %bitcast.63, bf16[2048,768]{1,0:T(8,128)(2,1)} %bitcast.83, bf16[768,2048]{1,0:T(8,128)(2,1)} %w_down.1), custom_call_target="tpu_custom_call" | custom-call | flops 18119393280 | bytes 25165824 | tf_op jit(solution)/shard_map/feed_forward/pallas_call | solution.py:647
  275.9 1.6 copy-done.7
  277.5 10.8 %convolution_convert_fusion.4 = bf16[768,2048]{1,0:T(8,128)(2,1)} fusion(bf16[1920,768]{1,0:T(8,128)(2,1)S(1)} %get-tuple-element.63, bf16[1920,2048]{1,0:T(8,128)(2,1)} %all-gather.10.cloned.1.call-done.grads), kind=kOutput, calls=%fused_computation.7 | convolution fusion | flops 6041370624 | bytes 13959168 | tf_op jit(solution)/shard_map/dot_general | solution.py:38
  288.2 18.9 %convolution_convert_fusion.3 = bf16[2048,1536]{1,0:T(8,128)(2,1)} fusion(bf16[1920,2048]{1,0:T(8,128)(2,1)} %bitcast.79, bf16[1920,1536]{1,0:T(8,128)(2,1)} %get-tuple-element.57.grads), kind=kOutput, calls=%fused_computation.3 | convolution fusion | flops 12082741248 | bytes 20054016 | tf_op jit(solution)/shard_map/dot_general | solution.py:38
  307.8 1.9 copy-done.3
  309.7 16.8 %input_grad.1 = bf16[1920,2048]{1,0:T(8,128)(2,1)} custom-call(bf16[1920,1536]{1,0:T(8,128)(2,1)} %get-tuple-element.57.grads, bf16[2048,768]{1,0:T(8,128)(2,1)S(1)} %bitcast.64, bf16[2048,768]{1,0:T(8,128)(2,1)} %bitcast.84), custom_call_target="tpu_custom_call" | custom-call | flops 12079595520 | bytes 20054016 | tf_op jit(solution)/shard_map/input_grad/pallas_call | solution.py:687
  326.5 39.5 %scatter_rows.5 = f32[240,2048]{1,0:T(8,128)} custom-call(bf16[8,240,2048]{2,1,0:T(8,128)(2,1)} %bitcast.76), custom_call_target="tpu_custom_call" | custom-call | bytes 98304000 | tf_op jit(solution)/shard_map/scatter_rows/pallas_call | solution.py:365
  366.0 2.9 fusion.8
  369.6 1.7 fusion.13.own
  371.3 38.2 %gather_rows.3 = bf16[8,240,2048]{2,1,0:T(8,128)(2,1)} custom-call(bf16[240,2048]{1,0:T(8,128)(2,1)} %fusion.13.own), custom_call_target="tpu_custom_call" | custom-call | bytes 88473600 | tf_op jit(solution)/shard_map/gather_rows/pallas_call | solution.py:122
  409.4 6.6 convolution_convert_fusion.6
  416.0 1.7 reshape.129
  417.7 5.5 fusion.17.grads
  423.2 33.1 %shard_map.238 = (bf16[1920,512]{1,0:T(8,128)(2,1)S(1)}, f32[8,128]{1,0:T(8,128)S(1)}) custom-call(s32[8,8]{1,0:T(8,128)S(1)} %get-tuple-element.93.starts, s32[8,8]{1,0:T(8,128)S(1)} %get-tuple-element.92.places, s32[8,8]{1,0:T(8,128)S(1)} %bitcast.68, f32[1920,512]{1,0:T(8,128)} %get-tuple-element.50.raw, f32[1920,256]{1,0:T(8,128)S(1)} %fusion.17.grads, ...), custom_call_target="tpu_custom_call" | custom-call | flops 1698693120 | bytes 6292480 | tf_op jit(solution)/shard_map/pallas_call | solution.py:581
  457.6 9.6 %multiply_reduce_fusion.2 = (f32[2048]{0:T(1024)S(1)}, bf16[2048,512]{1,0:T(8,128)(2,1)}) fusion(bf16[8,256,512]{2,1,0:T(8,128)(2,1)S(1)} %copy-done.19, bf16[1920,2048]{1,0:T(8,128)(2,1)} %get-tuple-element.60, bf16[1920,512]{1,0:T(8,128)(2,1)S(1)} %get-tuple-element.62), kind=kOutput, calls=%fused_computation.6 | convolution fusion | flops 4031772672 | bytes 14032896 | tf_op jit(solution)/shard_map/dot_general | solution.py:38
  467.2 1.9 copy.31
  469.1 1.9 pad_maximum_fusion
  471.0 10.0 %reduce-scatter.8.cloned.1.call-done = bf16[192,2048]{1,0:T(8,128)(2,1)} async-done(((bf16[768,2048]{1,0:T(8,128)(2,1)}), bf16[192,2048]{1,0:T(8,128)(2,1)}) %reduce-scatter.8.cloned.1.call-update) | async-done | bytes 786448 | tf_op jit(solution)/shard_map/reduce_scatter | solution.py:752
  481.1 25.4 %all_to_all.10 = bf16[8,64,1536]{2,1,0:T(8,128)(2,1)} all-to-all(bf16[8,64,1536]{2,1,0:T(8,128)(2,1)} %reduce-scatter.4.cloned.1.call-done), channel_id=1, replica_groups=mesh['rep'=4,'fsdp'=8] {'fsdp'}, dimensions={0} | all-to-all | bytes 3145728 | tf_op jit(solution)/shard_map/all_to_all | solution.py:755
  506.5 8.0 convolution_convert_fusion.1
  514.5 38.0 %scatter_rows.6 = f32[240,2048]{1,0:T(8,128)} custom-call(bf16[8,240,2048]{2,1,0:T(8,128)(2,1)} %bitcast.75), custom_call_target="tpu_custom_call" | custom-call | bytes 98304000 | tf_op jit(solution)/shard_map/scatter_rows/pallas_call | solution.py:365
  552.5 11.1 %convolution_convert_fusion = bf16[1920,2048]{1,0:T(8,128)(2,1)} fusion(bf16[1920,768]{1,0:T(8,128)(2,1)} %copy-done.7, bf16[768,2048]{1,0:T(8,128)(2,1)} %w_down.1), kind=kOutput, calls=%fused_computation | convolution fusion | flops 6043729920 | bytes 13959168 | tf_op jit(solution)/shard_map/dot_general | solution.py:30
  563.6 39.5 %scatter_rows.7 = f32[240,2048]{1,0:T(8,128)} custom-call(bf16[8,240,2048]{2,1,0:T(8,128)(2,1)} %bitcast.77), custom_call_target="tpu_custom_call" | custom-call | bytes 98304000 | tf_op jit(solution)/shard_map/scatter_rows/pallas_call | solution.py:365
  603.2 1.9 slice.48
  605.0 3.5 all-to-all-start
  609.6 8.6 %all-to-all-done = bf16[8,64,512]{2,1,0:T(8,128)(2,1)S(1)} async-done(((bf16[8,64,512]{2,1,0:T(8,128)(2,1)}), bf16[8,64,512]{2,1,0:T(8,128)(2,1)S(1)}, u32[]{:S(2)}, u32[]{:S(2)}) %all-to-all-start) | async-done | bytes 524320 | tf_op jit(solution)/shard_map/all_to_all | solution.py:892
  619.2 6.0 multiply_reduce_fusion.1
  625.2 43.9 %psum.7 = f32[4352]{0:T(1024)S(1)} all-reduce(f32[4352]{0:T(1024)S(1)} %pad_maximum_fusion.3), channel_id=1, replica_groups=mesh['rep'=4,'fsdp'=8] {'rep','fsdp'}, use_global_device_ids=true, to_apply=%region_10.11 | all-reduce | flops 4352 | bytes 34816 | tf_op jit(solution)/shard_map/psum | solution.py:913
  670.3 5.6 convert_element_type.105
  677.8 2.8 fusion.7
  680.5 45.1 %all-gather.18.cloned.1.call-done = bf16[32,64,1536]{2,1,0:T(8,128)(2,1)} async-done(((bf16[8,64,1536]{2,1,0:T(8,128)(2,1)}), bf16[32,64,1536]{2,1,0:T(8,128)(2,1)}) %all-gather.18.cloned.1.call-update) | async-done | bytes 6291472 | tf_op jit(solution)/shard_map/all_gather | solution.py:737
  725.7 7.7 place_columns.3
  733.4 56.1 %all-gather.16.cloned.1.call-done = bf16[3072,512]{1,0:T(8,128)(2,1)} async-done(((bf16[768,512]{1,0:T(8,128)(2,1)}), bf16[3072,512]{1,0:T(8,128)(2,1)}) %all-gather.16.cloned.1.call-update) | async-done | bytes 3145744 | tf_op jit(solution)/shard_map/all_gather | solution.py:737
  789.5 3.0 slice.56
  792.6 1.5 slice_convert_fusion
  794.1 4.1 place_columns.2
  798.2 1.9 reshape.134
  (93 shorter events, 13.9 us)
Async XLA Ops:
  7.2 127.9 %copy-start = (bf16[256,2048]{1,0:T(8,128)(2,1)S(1)}, bf16[256,2048]{1,0:T(8,128)(2,1)}, u32[]{:S(2)}) copy-start(bf16[256,2048]{1,0:T(8,128)(2,1)} %param.25) | copy-start | bytes 3145732
  7.2 241.9 %all-gather.12.cloned.1.call-start = ((), (), s32[]{:S(2)}) async-start(), calls=%async_computation.6 | async-start | bytes 3932160 | tf_op jit(solution)/shard_map/all_gather | solution.py:791
  33.3 215.8 %all-gather.14.cloned.1.call-start = ((), (), s32[]{:S(2)}) async-start(), calls=%async_computation.7 | async-start | bytes 3932160 | tf_op jit(solution)/shard_map/all_gather | solution.py:791
  34.0 61.7 %copy-start.4 = (s32[1,8,8]{2,1,0:T(8,128)S(1)}, s32[1,8,8]{2,1,0:T(8,128)}, u32[]{:S(2)}) copy-start(s32[1,8,8]{2,1,0:T(8,128)} %param.18) | copy-start | bytes 772
  34.0 215.1 %all-gather.10.cloned.1.call-start = ((), (), s32[]{:S(2)}) async-start(), calls=%async_computation.5 | async-start | bytes 8847360 | tf_op jit(solution)/shard_map/all_gather | solution.py:788
  95.7 371.5 %reduce-scatter.4.cloned.1.call-start = ((), (), s32[]{:S(2)}) async-start(), calls=%async_computation.8 | async-start | bytes 7864320 | tf_op jit(solution)/shard_map/reduce_scatter | solution.py:752
  110.6 2.1 copy-start.1
  140.4 46.2 %copy-start.11 = (bf16[240,2048]{1,0:T(8,128)(2,1)S(1)}, bf16[240,2048]{1,0:T(8,128)(2,1)}, u32[]{:S(2)}) copy-start(bf16[240,2048]{1,0:T(8,128)(2,1)} %param.16) | copy-start | bytes 2949124
  186.5 2.1 copy-start.8
  249.1 1.9 copy-start.2
  275.9 1.6 copy-start.7
  307.2 173.9 %reduce-scatter.8.cloned.1.call-start = ((), (), s32[]{:S(2)}) async-start(), calls=%async_computation.10 | async-start | bytes 3932160 | tf_op jit(solution)/shard_map/reduce_scatter | solution.py:752
  307.8 295.4 %reduce-scatter.6.cloned.1.call-start = ((), (), s32[]{:S(2)}) async-start(), calls=%async_computation.9 | async-start | bytes 3932160 | tf_op jit(solution)/shard_map/reduce_scatter | solution.py:883
  307.8 1.9 copy-start.3
  366.0 3.0 copy-start.9
  366.0 3.3 copy-start.13
  366.0 3.5 copy-start.16
  423.2 34.3 %copy-start.19 = (bf16[8,256,512]{2,1,0:T(8,128)(2,1)S(1)}, bf16[8,256,512]{2,1,0:T(8,128)(2,1)}, u32[]{:S(2)}) copy-start(bf16[8,256,512]{2,1,0:T(8,128)(2,1)} %get-tuple-element.49) | copy-start | bytes 6291460
  456.3 1.3 copy-start.5
  471.0 199.3 %all-gather.20.cloned.1.call-start = ((), (), s32[]{:S(2)}) async-start(), calls=%async_computation.13 | async-start | bytes 3932160 | tf_op jit(solution)/shard_map/all_gather | solution.py:737
  481.1 25.5 %copy-start.6 = (bf16[1920,512]{1,0:T(8,128)(2,1)S(1)}, bf16[1920,512]{1,0:T(8,128)(2,1)}, u32[]{:S(2)}) copy-start(bf16[1920,512]{1,0:T(8,128)(2,1)} %copy-done.5) | copy-start | bytes 5898244
  481.1 244.6 %all-gather.18.cloned.1.call-start = ((), (), s32[]{:S(2)}) async-start(), calls=%async_computation.12 | async-start | bytes 7864320 | tf_op jit(solution)/shard_map/all_gather | solution.py:737
  605.0 13.2 %all-to-all-start = ((bf16[8,64,512]{2,1,0:T(8,128)(2,1)}), bf16[8,64,512]{2,1,0:T(8,128)(2,1)S(1)}, u32[]{:S(2)}, u32[]{:S(2)}) async-start(bf16[8,64,512]{2,1,0:T(8,128)(2,1)} %bitcast.19), calls=%async_computation.2 | async-start | bytes 1048576 | tf_op jit(solution)/shard_map/all_to_all | solution.py:892
  608.5 181.0 %all-gather.16.cloned.1.call-start = ((), (), s32[]{:S(2)}) async-start(), calls=%async_computation.11 | async-start | bytes 3932160 | tf_op jit(solution)/shard_map/all_gather | solution.py:737
  670.3 5.7 copy-start.12
  670.3 5.6 copy-start.15
  670.3 6.2 copy-start.14
  670.3 6.2 copy-start.18
  676.0 1.6 copy-start.10
  676.0 1.8 copy-start.17
Sparse Core Ops, SparseCore 0:
  33.4 63.7 all-gather.11
  98.7 62.0 all-gather.13
  162.7 77.7 all-gather.9
  307.3 110.5 reduce-scatter.3
  420.1 60.9 reduce-scatter.7
  483.8 60.3 reduce-scatter.5
  545.7 63.3 all-gather.19
  610.6 115.0 all-gather.17
  727.8 61.6 all-gather.15
